TPU v7x, 256 devices: a whole 4x4x8 slice. The times are simulated.
256 devices in a mesh: px: 32 (over z, x_lo, core), pz: 8 (over y, x_hi).
Axes of the slice: x: 4 (x_hi: 2, x_lo: 2; x = x_hi * 2 + x_lo), y: 4, z: 8, core: 2. Of those that a mesh axis runs over, the one named last changes fastest.
Arguments:
- base: float32 [3, 256, 256, 128], P(None, 'px', 'pz'), may hold values from -6 to 6
- adjoint: float32 [3, 256, 256, 128], P(None, 'px', 'pz'), may hold values from -6 to 6
- tangent: float32 [1, 3, 256, 256, 128], P(None, None, 'px', 'pz'), may hold values from -6 to 6
- second: float32 [1, 3, 256, 256, 128], P(None, None, 'px', 'pz'), may hold values from -6 to 6
- dealias_mask: int32 [256, 256], P('px', 'pz'), may hold values 0 or 1
- tau_rows: int32 [256, 256, 2], P('px', 'pz'), may hold values from 0 to 63
- tau_inverse: float32 [256, 256, 64, 128], P('px', 'pz'), may hold values from -1 to 2.5, as said below
Outputs:
- base_next: float32 [3, 256, 256, 128], P(None, 'px', 'pz')
- adjoint_next: float32 [3, 256, 256, 128], P(None, 'px', 'pz')
- tangent_next: float32 [1, 3, 256, 256, 128], P(None, None, 'px', 'pz')
- second_next: float32 [1, 3, 256, 256, 128], P(None, None, 'px', 'pz')
Inputs may be any that keep to these rules, and one draw needn't show every extreme that they name: `tau_inverse`: entry [kx, kz, a, p * 64 + b] maps the input at Chebyshev index 2 b + p to the output at index 2 a + p.
All inputs are finite; a program needn't handle non-finite values. No bound on the sum of `dealias_mask` on one device may be relied on, other than what follows from the above.
Results may differ from a plain program's by a relative error of at most 0.00013.
Values sent between devices are 32-bit elements; how exact they have to be, the bound alone decides.
No kernel may reach another device: no remote copies, remote signals or barrier semaphores. Data moves between devices by JAX's collectives and lax.ppermute only.
A program may use at most 128 MiB of HBM per device.

v0:
```python
import math

import jax
import jax.numpy as jnp
from jax import lax
from jax.sharding import PartitionSpec as P

NX = 256
NZ = 256
NY = 128
DIRS = 1
HALF = 64


step_gain = 0.5


def hartley(length):
    indices = jnp.arange(length, dtype=jnp.int32)
    product = indices[:, None] * indices[None, :] % length
    angles = product.astype(jnp.float32) * (2.0 * math.pi / length)
    return (jnp.cos(angles) + jnp.sin(angles)) / math.sqrt(length)


def hartley_slope(length):
    indices = jnp.arange(length, dtype=jnp.int32)
    product = indices[:, None] * indices[None, :] % length
    angles = product.astype(jnp.float32) * (2.0 * math.pi / length)
    signed = jnp.where(indices < length // 2, indices, indices - length).astype(jnp.float32)
    return (
        (jnp.cos(angles) - jnp.sin(angles))
        * (signed * (2.0 * math.pi / length))[None, :]
        / math.sqrt(length)
    )


def chebyshev(length):
    indices = jnp.arange(length, dtype=jnp.int32)
    product = (2 * indices[:, None] + 1) * indices[None, :] % (4 * length)
    angles = product.astype(jnp.float32) * (math.pi / (2 * length))
    column_scale = jnp.where(indices == 0, math.sqrt(1.0 / length), math.sqrt(2.0 / length)).astype(
        jnp.float32
    )
    return jnp.cos(angles) * column_scale[None, :]


def chebyshev_slope(length):
    indices = jnp.arange(length, dtype=jnp.int32)
    product = (2 * indices[:, None] + 1) * indices[None, :] % (4 * length)
    angles = product.astype(jnp.float32) * (math.pi / (2 * length))
    nodes = jnp.sin((2 * indices + 1).astype(jnp.float32) * (math.pi / (2 * length)))
    column_scale = jnp.where(indices == 0, math.sqrt(1.0 / length), math.sqrt(2.0 / length)).astype(
        jnp.float32
    )
    column_scale = column_scale * indices.astype(jnp.float32)
    return jnp.sin(angles) * column_scale[None, :] / (length * nodes[:, None])


def crossed(first, other, axis):
    return jnp.roll(first, -1, axis) * jnp.roll(other, -2, axis) - jnp.roll(
        first, -2, axis
    ) * jnp.roll(other, -1, axis)


def forcings(velocity, vortex):
    grid_shape = velocity.shape[2:]
    base_v, adj_v = (velocity[0], velocity[1])
    tang_v, sec_v = (velocity[2 : 2 + DIRS], velocity[2 + DIRS :])
    base_o, adj_o = (vortex[0], vortex[1])
    tang_o, sec_o = (vortex[2 : 2 + DIRS], vortex[2 + DIRS :])
    force_base = crossed(base_v, base_o, 0)
    force_adjoint = crossed(base_v, adj_o, 0) + crossed(adj_v, base_o, 0)
    force_tangent = crossed(base_v[None], tang_o, 1) + crossed(tang_v, base_o[None], 1)
    force_second = (
        crossed(base_v[None], sec_o, 1)
        + crossed(sec_v, base_o[None], 1)
        + crossed(tang_v, adj_o[None], 1)
        + crossed(adj_v[None], tang_o, 1)
    )
    return jnp.concatenate(
        [
            force_base,
            force_adjoint,
            force_tangent.reshape((3 * DIRS,) + grid_shape),
            force_second.reshape((3 * DIRS,) + grid_shape),
        ],
        0,
    )


def placement_table(parity):
    outputs = jnp.arange(HALF, dtype=jnp.int32)[:, None]
    columns = jnp.arange(NY, dtype=jnp.int32)[None, :]
    return (columns == 2 * outputs + parity).astype(jnp.float32)


def body(base, adjoint, tangent, second, dealias_mask, tau_rows, tau_inverse):
    highest = lax.Precision.HIGHEST
    local_x = base.shape[1]
    local_z = base.shape[2]
    local_shape = (local_x, local_z, NY)
    count = 2 + 2 * DIRS
    hart_x = hartley(NX)
    hart_z = hartley(NZ)
    slope_xt = hartley_slope(NX)
    slope_zt = hartley_slope(NZ)
    cheb_y = chebyshev(NY)
    slope_yt = chebyshev_slope(NY)
    stacked = jnp.concatenate(
        [
            base,
            adjoint,
            tangent.reshape((3 * DIRS,) + local_shape),
            second.reshape((3 * DIRS,) + local_shape),
        ],
        0,
    )
    fields = stacked.shape[0]
    sideways = stacked.reshape((count, 3) + local_shape)[:, 0::2].reshape(
        (2 * count,) + local_shape
    )
    along_y = jnp.einsum("cxzn,jn->cxzj", stacked, cheb_y, precision=highest)
    slope_y = jnp.einsum("cxzn,jn->cxzj", sideways, slope_yt, precision=highest)
    groups_x = lax.axis_size("px")
    groups_z = lax.axis_size("pz")
    block_y = NY // groups_x
    block_x = NX // groups_z
    width = block_y * local_z

    def to_xlines(array):
        lead = array.shape[0]
        array = array.reshape((lead, local_x, local_z, groups_x, block_y))
        return array.transpose(0, 3, 1, 4, 2).reshape((lead, groups_x * local_x, width))

    whole_x, slope_whole = (
        lax.all_to_all(to_xlines(along_y), "px", split_axis=1, concat_axis=1, tiled=True),
        lax.all_to_all(to_xlines(slope_y), "px", split_axis=1, concat_axis=1, tiled=True),
    )
    values = jnp.einsum("ckm,xk->cxm", whole_x, hart_x, precision=highest)
    values = values.reshape((count, 3, NX, width))
    planar = whole_x.reshape((count, 3, NX, width))[:, 1:3].reshape((2 * count, NX, width))
    dx = jnp.einsum("ckm,xk->cxm", planar, slope_xt, precision=highest).reshape(
        (count, 2, NX, width)
    )
    dy = jnp.einsum("ckm,xk->cxm", slope_whole, hart_x, precision=highest).reshape(
        (count, 2, NX, width)
    )
    partial_value = jnp.stack(
        [values[:, 0], values[:, 1], values[:, 2], dy[:, 1], -dx[:, 1], dx[:, 0] - dy[:, 0]], 1
    )
    partial_value = partial_value.reshape((6 * count, NX, width))
    received = lax.all_to_all(partial_value, "pz", split_axis=1, concat_axis=1, tiled=True)
    received = received.reshape((6 * count, groups_z, block_x, block_y, local_z))
    received = received.transpose(0, 2, 3, 1, 4).reshape((count, 6, block_x, block_y, NZ))
    velocity = jnp.einsum("vcxjk,zk->vcxjz", received[:, 0:3], hart_z, precision=highest)
    rotated = jnp.einsum("vcxjk,zk->vcxjz", received[:, 3:6], hart_z, precision=highest)
    slope_v = jnp.einsum("vxjk,zk->vxjz", received[:, 1], slope_zt, precision=highest)
    slope_u = jnp.einsum("vxjk,zk->vxjz", received[:, 0], slope_zt, precision=highest)
    vortex = jnp.stack([rotated[:, 0] - slope_v, rotated[:, 1] + slope_u, rotated[:, 2]], 1)
    returned = jnp.einsum("cxjz,zk->cxjk", forcings(velocity, vortex), hart_z, precision=highest)
    returned = returned.reshape((fields, block_x, block_y, groups_z, local_z))
    returned = returned.transpose(0, 3, 1, 2, 4).reshape((fields, NX, width))
    mixed = lax.all_to_all(returned, "pz", split_axis=1, concat_axis=1, tiled=True)
    spectral_x = jnp.einsum("cxm,xk->ckm", mixed, hart_x, precision=highest)
    whole_y = lax.all_to_all(spectral_x, "px", split_axis=1, concat_axis=1, tiled=True)
    whole_y = whole_y.reshape((fields, groups_x, local_x, block_y, local_z))
    whole_y = whole_y.transpose(0, 2, 4, 1, 3).reshape((fields,) + local_shape)
    forcing_hat = jnp.einsum("cxzj,jn->cxzn", whole_y, cheb_y, precision=highest)
    right_side = (
        stacked + step_gain * forcing_hat * dealias_mask.astype(jnp.float32)[None, :, :, None]
    )
    positions = jnp.arange(HALF, dtype=jnp.int32)[None, None, :]
    even_side = right_side[..., 0::2]
    odd_side = right_side[..., 1::2]
    even_side = jnp.where(
        (positions != tau_rows[:, :, 0:1])[None], even_side, jnp.zeros_like(even_side)
    )
    odd_side = jnp.where(
        (positions != tau_rows[:, :, 1:2])[None], odd_side, jnp.zeros_like(odd_side)
    )
    even_solved = jnp.einsum(
        "xzab,cxzb->cxza", tau_inverse[..., :HALF], even_side, precision=highest
    )
    odd_solved = jnp.einsum("xzab,cxzb->cxza", tau_inverse[..., HALF:], odd_side, precision=highest)
    solved = jnp.einsum(
        "cxza,an->cxzn", even_solved, placement_table(0), precision=highest
    ) + jnp.einsum("cxza,an->cxzn", odd_solved, placement_table(1), precision=highest)
    base_next = solved[0:3]
    adjoint_next = solved[3:6]
    tangent_next = solved[6 : 6 + 3 * DIRS].reshape((DIRS, 3) + local_shape)
    second_next = solved[6 + 3 * DIRS :].reshape((DIRS, 3) + local_shape)
    return (base_next, adjoint_next, tangent_next, second_next)


def solution(mesh):
    in_specs = (
        P(None, "px", "pz", None),
        P(None, "px", "pz", None),
        P(None, None, "px", "pz", None),
        P(None, None, "px", "pz", None),
        P("px", "pz"),
        P("px", "pz", None),
        P("px", "pz", None, None),
    )
    out_specs = (
        P(None, "px", "pz", None),
        P(None, "px", "pz", None),
        P(None, None, "px", "pz", None),
        P(None, None, "px", "pz", None),
    )
    return jax.shard_map(body, mesh=mesh, in_specs=in_specs, out_specs=out_specs, check_vma=False)
```

profile of v0, /device:TPU:1, one launch (start us, length us, event | category | flops | bytes accessed | tf_op | source)
XLA Modules:
  0.0 435.6 jit_solution(2171104519277269522)
XLA Ops:
  0.7 1.5 pad_maximum_fusion.1
  2.2 0.1 slice.354
  2.3 5.7 %convolution_bitcast_fusion = f32[8,32,8,4,32]{1,4,3,2,0:T(8,128)} fusion(f32[8,8,32,128,1]{3,2,4,1,0:T(8,128)S(1)} %bitcast.208, f32[32,4]{0,1:T(4,128)S(1)} %sine_multiply_fusion, f32[128]{0:T(128)S(1)} %convert_multiply_fusion.1, s32[32,4]{0,1:T(4,128)S(1)} %multiply_add_fusion.1), kind=kOutput, calls=%fused_computation.7 | convolution fusion | flops 402915328 | bytes 2098688 | tf_op jit(solution)/shard_map/cxzn,jn->cxzj/dot_general | solution.py:123
  7.9 6.2 %copy.126 = f32[8,32,8,4,32]{4,3,0,2,1:T(4,128)} copy(f32[8,32,8,4,32]{1,4,3,2,0:T(8,128)} %convolution_bitcast_fusion) | data formatting | bytes 2097152 | tf_op jit(solution)/shard_map/reshape | solution.py:133
  14.1 4.5 %reshape.536 = f32[8,256,128]{2,0,1:T(8,128)} reshape(f32[8,32,8,4,32]{4,3,0,2,1:T(4,128)} %copy.126) | data formatting | bytes 2097152 | tf_op jit(solution)/shard_map/reshape | solution.py:133
  18.6 11.2 %all-to-all-start.1 = ((f32[8,256,128]{2,0,1:T(8,128)}), f32[8,256,128]{2,0,1:T(8,128)S(1)}, u32[]{:S(2)}, u32[]{:S(2)}) async-start(f32[8,256,128]{2,0,1:T(8,128)} %reshape.536), calls=%async_computation.1 | async-start | bytes 2097152 | tf_op jit(solution)/shard_map/all_to_all | solution.py:137
  29.8 2.8 fusion.102
  32.6 4.0 copy.76
  36.7 7.3 %copy.124 = f32[12,32,8,4,32]{4,3,0,2,1:T(4,128)} copy(f32[12,32,8,4,32]{4,2,3,1,0:T(8,128)} %bitcast.198) | data formatting | bytes 3145728 | tf_op jit(solution)/shard_map/reshape | solution.py:133
  44.0 6.1 %reshape.535 = f32[12,256,128]{2,0,1:T(8,128)} reshape(f32[12,32,8,4,32]{4,3,0,2,1:T(4,128)} %copy.124) | data formatting | bytes 3145728 | tf_op jit(solution)/shard_map/reshape | solution.py:133
  50.1 7.8 %all-to-all-done.1 = f32[8,256,128]{2,0,1:T(8,128)S(1)} async-done(((f32[8,256,128]{2,0,1:T(8,128)}), f32[8,256,128]{2,0,1:T(8,128)S(1)}, u32[]{:S(2)}, u32[]{:S(2)}) %all-to-all-start.1) | async-done | bytes 1048608 | tf_op jit(solution)/shard_map/all_to_all | solution.py:137
  57.9 1.0 copy-done
  58.9 4.7 %all-to-all-start = ((f32[12,256,128]{2,0,1:T(8,128)}), f32[12,256,128]{2,0,1:T(8,128)S(1)}, u32[]{:S(2)}, u32[]{:S(2)}) async-start(f32[12,256,128]{2,0,1:T(8,128)} %reshape.535), calls=%async_computation | async-start | bytes 4194304 | tf_op jit(solution)/shard_map/all_to_all | solution.py:136
  63.6 3.4 fusion.40
  67.0 46.5 %all-to-all-done = f32[12,256,128]{2,0,1:T(8,128)S(1)} async-done(((f32[12,256,128]{2,0,1:T(8,128)}), f32[12,256,128]{2,0,1:T(8,128)S(1)}, u32[]{:S(2)}, u32[]{:S(2)}) %all-to-all-start) | async-done | bytes 1572896 | tf_op jit(solution)/shard_map/all_to_all | solution.py:136
  113.5 0.5 copy.80
  114.0 2.5 fusion.74
  116.6 0.1 slice.423
  116.6 2.1 fusion.71
  118.8 0.2 fusion.192
  118.9 0.3 pad_maximum_fusion
  119.2 1.8 copy.87
  121.1 43.5 %all_to_all.25 = f32[24,256,128]{2,0,1:T(8,128)S(1)} all-to-all(f32[24,256,128]{2,0,1:T(8,128)S(1)} %copy.87), channel_id=1, replica_groups=mesh['px'=32,'pz'=8] {'pz'}, dimensions={1} | all-to-all | bytes 6291456 | tf_op jit(solution)/shard_map/all_to_all | solution.py:152
  164.6 2.4 copy.88
  167.0 8.4 %reshape.513 = f32[24,8,32,4,32]{2,1,4,3,0:T(8,128)} reshape(f32[24,256,128]{1,2,0:T(8,128)} %copy.88) | data formatting | bytes 6291456 | tf_op jit(solution)/shard_map/reshape | solution.py:153
  175.4 13.0 %copy.89 = f32[24,32,4,8,32]{4,3,1,2,0:T(8,128)} copy(f32[24,32,4,8,32]{1,3,4,2,0:T(8,128)} %bitcast.194) | data formatting | bytes 6291456 | tf_op jit(solution)/shard_map/transpose | solution.py:154
  188.4 8.5 %reshape.514 = f32[4,6,32,4,256]{4,2,3,1,0:T(8,128)S(1)} reshape(f32[24,32,4,8,32]{4,3,1,2,0:T(8,128)} %copy.89) | data formatting | bytes 6291456 | tf_op jit(solution)/shard_map/reshape | solution.py:154
  196.9 2.5 fusion.67
  199.4 1.7 convolution_add_fusion
  201.1 2.5 fusion.69
  203.6 1.7 convolution_subtract_fusion
  205.3 0.1 slice_bitcast_fusion.26
  205.4 0.4 fusion.53
  205.8 0.1 fusion.59
  205.9 0.1 multiply_subtract_fusion
  206.0 0.3 subtract_add_fusion.1
  206.3 0.3 subtract_add_fusion
  206.6 0.7 fusion.45
  207.4 2.7 fusion.18
  210.0 3.7 reshape.515
  213.7 6.8 %copy.99 = f32[12,32,4,8,32]{1,3,4,2,0:T(8,128)} copy(f32[12,32,4,8,32]{4,3,1,2,0:T(8,128)} %reshape.515) | data formatting | bytes 3145728 | tf_op jit(solution)/shard_map/reshape | solution.py:161
  220.5 5.3 %reshape.516 = f32[12,256,128]{1,2,0:T(8,128)} reshape(f32[12,8,32,4,32]{2,1,4,3,0:T(8,128)} %bitcast.199) | data formatting | bytes 3145728 | tf_op jit(solution)/shard_map/reshape | solution.py:162
  225.8 2.1 copy.100
  228.0 28.3 %all_to_all.26 = f32[12,256,128]{2,0,1:T(8,128)S(1)} all-to-all(f32[12,256,128]{2,0,1:T(8,128)S(1)} %copy.100), channel_id=1, replica_groups=mesh['px'=32,'pz'=8] {'pz'}, dimensions={1} | all-to-all | bytes 3145728 | tf_op jit(solution)/shard_map/all_to_all | solution.py:163
  256.3 2.8 fusion.35
  259.1 2.3 copy.102
  261.4 9.8 %all-to-all-start.4 = ((f32[12,256,128]{2,0,1:T(8,128)}), f32[12,256,128]{2,0,1:T(8,128)S(1)}, u32[]{:S(2)}, u32[]{:S(2)}) async-start(f32[12,256,128]{2,0,1:T(8,128)} %copy.102), calls=%async_computation.4 | async-start | bytes 4194304 | tf_op jit(solution)/shard_map/all_to_all | solution.py:165
  271.3 0.7 iota_compare_fusion
  272.0 0.7 iota_compare_fusion.1
  272.7 48.4 %all-to-all-done.4 = f32[12,256,128]{2,0,1:T(8,128)S(1)} async-done(((f32[12,256,128]{2,0,1:T(8,128)}), f32[12,256,128]{2,0,1:T(8,128)S(1)}, u32[]{:S(2)}, u32[]{:S(2)}) %all-to-all-start.4) | async-done | bytes 1572896 | tf_op jit(solution)/shard_map/all_to_all | solution.py:165
  321.1 1.6 copy.103
  322.8 5.8 %reshape.517 = f32[12,32,8,4,32]{4,3,2,1,0:T(4,128)} reshape(f32[12,256,128]{2,1,0:T(8,128)} %copy.103) | data formatting | bytes 3145728 | tf_op jit(solution)/shard_map/reshape | solution.py:166
  328.6 4.0 copy.104
  332.6 10.3 %multiply_add_fusion = f32[12,8,32,128]{3,2,1,0:T(8,128)S(1)} fusion(f32[12,8,32,128]{2,1,3,0:T(8,128)S(1)} %bitcast.197, f32[8,32]{1,0:T(8,128)S(1)} %convert_multiply_fusion, f32[128]{0:T(128)S(1)} %compare_select_fusion.1, s32[128]{0:T(128)S(1)} %multiply_add_fusion.2, f32[3,8,32,128]{3,2,1,0:T(8,128)S(1)} %bitcast.211, ...), kind=kOutput, calls=%fused_computation.27 | convolution fusion | flops 606191616 | bytes 4720640 | tf_op jit(solution)/shard_map/cxzj,jn->cxzn/dot_general | solution.py:168
  342.9 28.9 %slice.416 = f32[12,8,32,64]{3,2,1,0:T(8,128)} slice(f32[12,8,32,128]{3,2,1,0:T(8,128)S(1)} %multiply_add_fusion), slice={[0:12:1], [0:8:1], [0:32:1], [1:128:2]} | slice | bytes 1572864 | tf_op jit(solution)/shard_map/slice | solution.py:174
  371.8 27.6 %slice.413 = f32[12,8,32,64]{3,2,1,0:T(8,128)S(1)} slice(f32[12,8,32,128]{3,2,1,0:T(8,128)S(1)} %multiply_add_fusion), slice={[0:12:1], [0:8:1], [0:32:1], [0:128:2]} | slice | bytes 1572864 | tf_op jit(solution)/shard_map/slice | solution.py:173
  399.4 1.9 broadcast_select_fusion
  401.3 0.0 slice-start.1
  401.3 16.9 %fusion.13 = f32[12,8,32,64]{3,0,2,1:T(8,128)S(1)} fusion(f32[8,32,64,128]{3,2,1,0:T(8,128)} %param.13, f32[12,8,32,64]{3,2,1,0:T(8,128)S(1)} %broadcast_select_fusion), kind=kOutput, calls=%fused_computation.11 | convolution fusion | flops 150994944 | bytes 9961472 | tf_op jit(solution)/shard_map/xzab,cxzb->cxza/dot_general | solution.py:184
  418.2 0.2 broadcast_select_fusion.1
  418.5 13.1 %fusion.8 = f32[12,8,32,64]{3,0,2,1:T(8,128)S(1)} fusion(f32[8,32,64,128]{3,2,1,0:T(8,128)S(1)} %bitcast.196, f32[12,8,32,64]{3,2,1,0:T(8,128)S(1)} %broadcast_select_fusion.1), kind=kOutput, calls=%fused_computation.10 | convolution fusion | flops 150994944 | bytes 9961472 | tf_op jit(solution)/shard_map/xzab,cxzb->cxza/dot_general | solution.py:181
  431.5 1.3 fusion.26
  432.9 1.3 fusion.32
  434.2 1.2 slice_bitcast_fusion.6
  (35 shorter events, 0.2 us)
Async XLA Ops:
  18.6 11.2 %copy-start.1 = (f32[1,3,8,32,128]{4,3,2,1,0:T(8,128)S(1)}, f32[1,3,8,32,128]{4,3,2,1,0:T(8,128)}, u32[]{:S(2)}) copy-start(f32[1,3,8,32,128]{4,3,2,1,0:T(8,128)} %param.10) | copy-start | bytes 1179652
  18.6 11.2 %copy-start.2 = (f32[1,3,8,32,128]{4,3,2,1,0:T(8,128)S(1)}, f32[1,3,8,32,128]{4,3,2,1,0:T(8,128)}, u32[]{:S(2)}) copy-start(f32[1,3,8,32,128]{4,3,2,1,0:T(8,128)} %param.9) | copy-start | bytes 1179652
  18.6 39.3 %all-to-all-start.1 = ((f32[8,256,128]{2,0,1:T(8,128)}), f32[8,256,128]{2,0,1:T(8,128)S(1)}, u32[]{:S(2)}, u32[]{:S(2)}) async-start(f32[8,256,128]{2,0,1:T(8,128)} %reshape.536), calls=%async_computation.1 | async-start | bytes 2097152 | tf_op jit(solution)/shard_map/all_to_all | solution.py:137
  57.9 1.0 copy-start
  58.9 54.6 %all-to-all-start = ((f32[12,256,128]{2,0,1:T(8,128)}), f32[12,256,128]{2,0,1:T(8,128)S(1)}, u32[]{:S(2)}, u32[]{:S(2)}) async-start(f32[12,256,128]{2,0,1:T(8,128)} %reshape.535), calls=%async_computation | async-start | bytes 4194304 | tf_op jit(solution)/shard_map/all_to_all | solution.py:136
  261.4 9.9 %copy-start.9 = (s32[8,32]{1,0:T(8,128)S(1)}, s32[8,32]{1,0:T(8,128)}, u32[]{:S(2)}) copy-start(s32[8,32]{1,0:T(8,128)} %param.11) | copy-start | bytes 3076
  261.4 9.9 %copy-start.8 = (s32[8,32,2]{1,2,0:T(2,128)S(1)}, s32[8,32,2]{1,2,0:T(2,128)}, u32[]{:S(2)}) copy-start(s32[8,32,2]{1,2,0:T(2,128)} %param.12) | copy-start | bytes 6148
  261.4 59.8 %all-to-all-start.4 = ((f32[12,256,128]{2,0,1:T(8,128)}), f32[12,256,128]{2,0,1:T(8,128)S(1)}, u32[]{:S(2)}, u32[]{:S(2)}) async-start(f32[12,256,128]{2,0,1:T(8,128)} %copy.102), calls=%async_computation.4 | async-start | bytes 4194304 | tf_op jit(solution)/shard_map/all_to_all | solution.py:165
  328.6 4.0 copy-start.3
  328.6 4.0 copy-start.4
  328.6 4.0 copy-start.5
  371.8 27.6 %copy-start.7 = (pred[8,32,64]{2,1,0:T(8,128)(4,1)S(1)}, pred[8,32,64]{2,1,0:T(8,128)(4,1)}, u32[]{:S(2)}) copy-start(pred[8,32,64]{2,1,0:T(8,128)(4,1)} %iota_compare_fusion) | copy-start | bytes 49156
  399.4 19.0 %slice-start = ((s8[8388608]{0:T(1024)(128)(4,1)}), s8[4194304]{0:T(1024)(128)(4,1)S(1)}, s32[]{:S(2)}) async-start(s8[8388608]{0:T(1024)(128)(4,1)} %bitcast.195), calls=%async_computation.5 | async-start | bytes 8388608
  401.3 16.9 %copy-start.6 = (pred[8,32,64]{2,1,0:T(8,128)(4,1)S(1)}, pred[8,32,64]{2,1,0:T(8,128)(4,1)}, u32[]{:S(2)}) copy-start(pred[8,32,64]{2,1,0:T(8,128)(4,1)} %iota_compare_fusion.1) | copy-start | bytes 49156
  401.3 17.1 %slice-start.1 = ((s8[8388608]{0:T(1024)(128)(4,1)}), s8[4194304]{0:T(1024)(128)(4,1)S(1)}, s32[]{:S(2)}) async-start(s8[8388608]{0:T(1024)(128)(4,1)} %bitcast.195), calls=%async_computation.6 | async-start | bytes 8388608
where the time goes:
time: 444 us; the launch traced here: 436 us
  local copies, waits for them, and re-layouts  154 us (35%)
  waiting for transfers between devices  103 us (23%)
  matrix products  73.1 us (16%)
  blocking collectives  71.8 us (16%)
  starting transfers between devices  25.7 us (6%)
  other arithmetic  7.4 us (2%)
    all_to_all x1, waiting for transfers between devices, body(): lax.all_to_all(spectral_x, 'px', split_axis=1, concat_axis=1, tiled=True)  48.4 us
    all_to_all x1, waiting for transfers between devices, body(): lax.all_to_all(to_xlines(along_y), 'px', split_axis=1, concat_axis=1, til...  46.5 us
    all_to_all x1, blocking collectives, body(): lax.all_to_all(partial_value, 'pz', split_axis=1, concat_axis=1, tiled=True)  43.5 us
    slice x1, local copies, waits for them, and re-layouts, body(): odd_side = right_side[..., 1::2]  28.9 us
    all_to_all x1, blocking collectives, body(): lax.all_to_all(returned, 'pz', split_axis=1, concat_axis=1, tiled=True)  28.3 us
    slice x1, local copies, waits for them, and re-layouts, body(): even_side = right_side[..., 0::2]  27.6 us
    reshape x4, local copies, waits for them, and re-layouts, to_xlines(): array.transpose(0, 3, 1, 4, 2).reshape((lead, groups_x * local_x, width))  24.1 us
    dot_general x1, matrix products, body(): jnp.einsum('xzab,cxzb->cxza', tau_inverse[..., HALF:], odd_side, precisio...  16.9 us
  transfers between devices with their start and end apart: 3, of which 3 were waited for; matrix products, arithmetic and copies ran while one was open for 6% of the time, Pallas kernels for 0%

commit v1 on v0

v1 whole, which is shorter than its diff:
```python
import math

import jax
import jax.numpy as jnp
import numpy as np
from jax import lax
from jax.experimental import pallas as pl
from jax.experimental.pallas import tpu as pltpu
from jax.sharding import PartitionSpec as P

NX = 256
NZ = 256
NY = 128
HALF = 64
GX = 32
GZ = 8
LX = NX // GX
LZ = NZ // GZ
QY = NY // GX
BX = NX // GZ
F32 = jnp.float32
BF16 = jnp.bfloat16

step_gain = 0.5


def split_table(table):
    table = np.asarray(table, np.float32)
    high = table.astype(jnp.bfloat16)
    low = (table - high.astype(np.float32)).astype(jnp.bfloat16)
    return high, low


def hartley(length):
    index = np.arange(length)
    angle = (index[:, None] * index[None, :] % length) * (2.0 * math.pi / length)
    return (np.cos(angle) + np.sin(angle)) / math.sqrt(length)


def hartley_slope(length):
    index = np.arange(length)
    angle = (index[:, None] * index[None, :] % length) * (2.0 * math.pi / length)
    signed = np.where(index < length // 2, index, index - length)
    return (np.cos(angle) - np.sin(angle)) * (signed * (2.0 * math.pi / length))[None, :] / math.sqrt(length)


def chebyshev(length):
    index = np.arange(length)
    angle = ((2 * index[:, None] + 1) * index[None, :] % (4 * length)) * (math.pi / (2 * length))
    scale = np.where(index == 0, math.sqrt(1.0 / length), math.sqrt(2.0 / length))
    return np.cos(angle) * scale[None, :]


def chebyshev_slope(length):
    index = np.arange(length)
    angle = ((2 * index[:, None] + 1) * index[None, :] % (4 * length)) * (math.pi / (2 * length))
    nodes = np.sin((2 * index + 1) * (math.pi / (2 * length)))
    scale = np.where(index == 0, math.sqrt(1.0 / length), math.sqrt(2.0 / length)) * index
    return np.sin(angle) * scale[None, :] / (length * nodes[:, None])


def node_order():
    return (np.arange(GX)[None, :] * QY + np.arange(QY)[:, None]).reshape(-1)


def parity_order():
    return (2 * np.arange(HALF)[None, :] + np.arange(2)[:, None]).reshape(-1)


def tables():
    nodes = node_order()
    cheb = chebyshev(NY)
    both = np.concatenate([cheb[nodes], chebyshev_slope(NY)[nodes]], 0)
    both_hi, both_lo = split_table(both)
    y_first = np.concatenate([both_hi, both_hi], 1)
    y_second = both_lo
    hx_hi, hx_lo = split_table(hartley(NX))
    dx_hi, dx_lo = split_table(hartley_slope(NX))
    x_value = np.concatenate([hx_hi, hx_hi, hx_lo], 1)
    x_slope = np.concatenate([dx_hi, dx_hi, dx_lo], 1)
    hz_hi, hz_lo = split_table(hartley(NZ).T)
    dz_hi, dz_lo = split_table(hartley_slope(NZ).T)
    z_value = np.concatenate([hz_hi, hz_hi, hz_lo], 0)
    z_slope = np.concatenate([dz_hi, dz_hi, dz_lo], 0)
    order = parity_order()
    back_hi, back_lo = split_table(cheb[nodes][:, order])
    gather = (np.arange(NY)[:, None] == order[None, :]).astype(jnp.bfloat16)
    y_back = np.concatenate([back_hi, back_hi, back_lo, gather, gather], 0)
    place = gather.T
    even, odd = place[:HALF], place[HALF:]
    spread = np.concatenate([even, even, odd, odd] * 2, 0)
    return dict(y_first=y_first, y_second=y_second, x_value=x_value, x_slope=x_slope, z_value=z_value,
                z_slope=z_slope, y_back=y_back, spread=spread)


def dot(left, right):
    return lax.dot_general(left, right, (((1,), (0,)), ((), ())), preferred_element_type=F32)


def dot_nt(left, right):
    return lax.dot_general(left, right, (((1,), (1,)), ((), ())), preferred_element_type=F32)


def halves(array):
    high = array.astype(BF16)
    return high, (array - high.astype(F32)).astype(BF16)


def swap_strips(tiles):
    lane = lax.broadcasted_iota(jnp.int32, tiles[0].shape, 1)
    low = lane < 64
    even = (lane & 32) == 0
    first, second, third, fourth = tiles
    a = jnp.where(low, first, pltpu.roll(third, 64, 1))
    c = jnp.where(low, pltpu.roll(first, 64, 1), third)
    b = jnp.where(low, second, pltpu.roll(fourth, 64, 1))
    d = jnp.where(low, pltpu.roll(second, 64, 1), fourth)
    return [
        jnp.where(even, a, pltpu.roll(b, 32, 1)),
        jnp.where(even, pltpu.roll(a, 96, 1), b),
        jnp.where(even, c, pltpu.roll(d, 32, 1)),
        jnp.where(even, pltpu.roll(c, 96, 1), d),
    ]


def y_forward(velocities, first, second):
    count = len(velocities)
    stride = 5 * count * LX

    def kernel(*refs):
        sources, first_ref, second_ref, out_ref = refs[:count], refs[count], refs[count + 1], refs[count + 2]
        for v in range(count):
            for comp in range(3):
                rows = NY if comp == 1 else 2 * NY
                high, low = halves(sources[v][comp].reshape(LX * LZ, NY))
                result = dot_nt(first_ref[0:rows], jnp.concatenate([high, low], 1)) + dot_nt(second_ref[0:rows], high)
                for part in range(rows // NY):
                    field = 5 * v + (comp if part == 0 else 3 + comp // 2)
                    for quad in range(2):
                        tiles = [
                            result[part * NY + q * GX : part * NY + (q + 1) * GX, quad * 128 : (quad + 1) * 128]
                            for q in range(QY)
                        ]
                        for s, tile in enumerate(swap_strips(tiles)):
                            out_ref[pl.ds(field * LX + quad * 4 + s, GX, stride=stride), :] = tile

    out = pl.pallas_call(
        kernel,
        name="y_forward",
        out_shape=jax.ShapeDtypeStruct((GX * stride, 128), F32),
    )(*velocities, first, second)
    return out.reshape(GX, 5 * count, LX, 128)


def x_forward(received, value, slope):
    count = received.shape[1] // 5

    def kernel(in_ref, value_ref, slope_ref, out_ref):
        def one(v, carry):
            parts = [halves(in_ref[:, 5 * v + i].reshape(NX, 128)) for i in range(5)]
            high = jnp.concatenate([p[0] for p in parts], 1)
            low = jnp.concatenate([p[1] for p in parts], 1)
            stack = jnp.concatenate([high, low, high], 0)
            plain = dot(value_ref[...], stack)
            slopes = dot(slope_ref[...], stack[:, 128:384])
            u, vv, w, dyu, dyw = [plain[:, 128 * i : 128 * (i + 1)] for i in range(5)]
            dxv, dxw = slopes[:, :128], slopes[:, 128:]
            for i, piece in enumerate([u, vv, w, dyw, dxw, dxv - dyu]):
                out_ref[:, 6 * v + i] = piece.reshape(GZ, BX, 128)
            return carry

        lax.fori_loop(0, count, one, 0)

    return pl.pallas_call(
        kernel,
        name="x_forward",
        out_shape=jax.ShapeDtypeStruct((GZ, 6 * count, BX, 128), F32),
    )(received, value, slope)


def z_stage(received, value, slope):
    count = received.shape[1] // 6
    rows = QY * BX

    def kernel(in_ref, value_ref, slope_ref, out_ref, phys, force):
        def forward(v, carry):
            lefts = []
            for i in range(6):
                field = 6 * v + i
                sides = [swap_strips([in_ref[4 * side + h, field] for h in range(4)]) for side in range(2)]
                lines = jnp.concatenate(
                    [jnp.concatenate([sides[0][q], sides[1][q]], 1) for q in range(QY)], 0
                )
                high, low = halves(lines)
                lefts.append(jnp.concatenate([high, low, high], 1))
            values = dot(jnp.concatenate(lefts, 0), value_ref[...])
            slopes = dot(jnp.concatenate(lefts[0:2], 0), slope_ref[...])
            pieces = [values[rows * i : rows * (i + 1)] for i in range(6)]
            pieces[3] = pieces[3] - slopes[rows:]
            pieces[4] = slopes[:rows] - pieces[4]
            for i in range(6):
                phys[6 * v + i] = pieces[i]
            return carry

        lax.fori_loop(0, count, forward, 0)

        def cross_terms(r, carry):
            at = pl.ds(pl.multiple_of(r * 8, 8), 8)
            field = [phys[i, at, :] for i in range(24)]

            def cross(a, b):
                va, ob = field[6 * a : 6 * a + 3], field[6 * b + 3 : 6 * b + 6]
                return [va[(i + 1) % 3] * ob[(i + 2) % 3] - va[(i + 2) % 3] * ob[(i + 1) % 3] for i in range(3)]

            def total(*pairs):
                terms = [cross(a, b) for a, b in pairs]
                return [sum(t[i] for t in terms[1:]) + terms[0][i] if len(terms) > 1 else terms[0][i] for i in range(3)]

            results = (
                total((0, 0)) + total((0, 1), (1, 0)) + total((0, 2), (2, 0)) + total((0, 3), (3, 0), (2, 1), (1, 2))
            )
            for i, piece in enumerate(results):
                force[i, at, :] = piece
            return carry

        lax.fori_loop(0, rows // 8, cross_terms, 0)

        def backward(v, carry):
            lefts = []
            for i in range(3):
                high, low = halves(force[3 * v + i])
                lefts.append(jnp.concatenate([high, low, high], 1))
            result = dot(jnp.concatenate(lefts, 0), value_ref[...])
            for i in range(3):
                for side in range(2):
                    tiles = [
                        result[rows * i + q * BX : rows * i + (q + 1) * BX, 128 * side : 128 * (side + 1)]
                        for q in range(QY)
                    ]
                    for h, tile in enumerate(swap_strips(tiles)):
                        out_ref[4 * side + h, 3 * v + i] = tile
            return carry

        lax.fori_loop(0, count, backward, 0)

    return pl.pallas_call(
        kernel,
        name="z_stage",
        out_shape=jax.ShapeDtypeStruct((GZ, 3 * count, BX, 128), F32),
        scratch_shapes=[pltpu.VMEM((6 * count, rows, NZ), F32), pltpu.VMEM((3 * count, rows, NZ), F32)],
    )(received, value, slope)


def x_backward(received, value):
    fields = received.shape[1]

    def kernel(in_ref, value_ref, out_ref):
        def two(k, carry):
            parts = [halves(in_ref[:, 2 * k + i].reshape(NX, 128)) for i in range(2)]
            high = jnp.concatenate([p[0] for p in parts], 1)
            low = jnp.concatenate([p[1] for p in parts], 1)
            result = dot(value_ref[...], jnp.concatenate([high, low, high], 0))
            for i in range(2):
                out_ref[:, 2 * k + i] = result[:, 128 * i : 128 * (i + 1)].reshape(GX, LX, 128)
            return carry

        lax.fori_loop(0, fields // 2, two, 0)

    return pl.pallas_call(
        kernel,
        name="x_backward",
        out_shape=jax.ShapeDtypeStruct((GX, fields, LX, 128), F32),
    )(received, value)


def y_solve(received, velocities, gain, keep, tau_inverse, y_back, spread):
    fields = received.shape[1]
    lines = LX * LZ
    pad = 16
    stride = fields * LX

    def kernel(in_ref, *refs):
        sources = refs[:4]
        gain_ref, keep_ref, tau_ref, back_ref, spread_ref = refs[4:9]
        outs = refs[9:13]
        right, solved, solved_odd = refs[13:]
        step = pl.program_id(0)

        @pl.when(step == 0)
        def _():
            for f in range(fields):
                quads = []
                for quad in range(2):
                    tiles = swap_strips(
                        [in_ref[pl.ds(f * LX + quad * 4 + s, GX, stride=stride), :] for s in range(4)]
                    )
                    quads.append(jnp.concatenate(tiles, 0).T)
                high, low = halves(jnp.concatenate(quads, 0) * gain_ref[...])
                own_high, own_low = halves(sources[f // 3][f % 3].reshape(lines, NY))
                result = dot(jnp.concatenate([high, low, high, own_high, own_low], 1), back_ref[...])
                right[pl.ds(f, lines, stride=pad), :] = jnp.where(keep_ref[...] > 0.5, result, 0.0)

        lane = lax.broadcasted_iota(jnp.int32, (pad, NY), 1)
        first_half = lane < HALF
        zero = jnp.zeros((4 * pad, NY), BF16)

        def pair(k, carry):
            weights = []
            lefts = []
            for i in range(2):
                mode = 2 * k + i
                high, low = halves(tau_ref[0, mode])
                weights.append(jnp.concatenate([high, low], 0))
                line = right[pl.ds(pl.multiple_of((step * LZ + mode) * pad, pad), pad), :]
                even = halves(jnp.where(first_half, line, 0.0))
                odd = halves(jnp.where(first_half, 0.0, line))
                lefts.append(jnp.concatenate([even[0], odd[0], even[1], odd[1]], 0))
            left = jnp.concatenate(
                [jnp.concatenate([lefts[0], zero], 1), jnp.concatenate([zero, lefts[1]], 1)], 0
            )
            result = dot_nt(left, jnp.concatenate(weights, 1))
            for i in range(2):
                piece = result[4 * pad * i : 4 * pad * (i + 1)]
                piece = piece[: 2 * pad] + piece[2 * pad :]
                at = pl.ds(pl.multiple_of((2 * k + i) * pad, pad), pad)
                solved[at, :] = piece[:pad]
                solved_odd[at, :] = piece[pad:]
            return carry

        lax.fori_loop(0, LZ // 2, pair, 0, unroll=4)

        for f in range(fields):
            high0, low0 = halves(solved[pl.ds(f, LZ, stride=pad), :])
            high1, low1 = halves(solved_odd[pl.ds(f, LZ, stride=pad), :])
            result = dot(jnp.concatenate([high0, high1, low0, low1], 1), spread_ref[...])
            outs[f // 3][f % 3, 0] = result

    whole = lambda *shape: pl.BlockSpec(shape, lambda i: (0,) * len(shape))
    return pl.pallas_call(
        kernel,
        name="y_solve",
        grid=(LX,),
        in_specs=[
            whole(GX * stride, 128),
            *[whole(3, LX, LZ, NY) for _ in range(4)],
            whole(lines, NY),
            whole(lines, NY),
            pl.BlockSpec((1, LZ, HALF, NY), lambda i: (i, 0, 0, 0)),
            whole(5 * NY, NY),
            whole(4 * NY, NY),
        ],
        out_specs=[pl.BlockSpec((3, 1, LZ, NY), lambda i: (0, i, 0, 0)) for _ in range(4)],
        out_shape=[jax.ShapeDtypeStruct((3, LX, LZ, NY), F32) for _ in range(4)],
        scratch_shapes=[pltpu.VMEM((lines * pad, NY), F32), pltpu.VMEM((LZ * pad, NY), F32), pltpu.VMEM((LZ * pad, NY), F32)],
        compiler_params=pltpu.CompilerParams(dimension_semantics=("arbitrary",)),
    )(received.reshape(GX * stride, 128), *velocities, gain, keep, tau_inverse, y_back, spread)


def exchange(array, axis):
    return lax.all_to_all(array, axis, split_axis=0, concat_axis=0, tiled=True)


def body(base, adjoint, tangent, second, dealias_mask, tau_rows, tau_inverse):
    table = tables()
    velocities = [base, adjoint, tangent.reshape(adjoint.shape), second.reshape(adjoint.shape)]
    gain = jnp.broadcast_to((step_gain * dealias_mask.astype(F32)).reshape(LX * LZ, 1), (LX * LZ, NY))
    positions = jnp.arange(HALF, dtype=jnp.int32)
    keep = (positions != tau_rows.reshape(LX * LZ, 2)[:, :, None]).astype(F32).reshape(LX * LZ, NY)

    spectral = y_forward(velocities, table["y_first"], table["y_second"])
    whole_x = exchange(spectral, "px")
    partial = x_forward(whole_x, table["x_value"], table["x_slope"])
    whole_z = exchange(partial, "pz")
    returned = z_stage(whole_z, table["z_value"], table["z_slope"])
    mixed = exchange(returned, "pz")
    spectral_x = x_backward(mixed, table["x_value"])
    whole_y = exchange(spectral_x, "px")
    outs = y_solve(whole_y, velocities, gain, keep, tau_inverse, table["y_back"], table["spread"])
    return (outs[0], outs[1], outs[2].reshape(tangent.shape), outs[3].reshape(second.shape))


def solution(mesh):
    in_specs = (
        P(None, "px", "pz", None),
        P(None, "px", "pz", None),
        P(None, None, "px", "pz", None),
        P(None, None, "px", "pz", None),
        P("px", "pz"),
        P("px", "pz", None),
        P("px", "pz", None, None),
    )
    out_specs = (
        P(None, "px", "pz", None),
        P(None, "px", "pz", None),
        P(None, None, "px", "pz", None),
        P(None, None, "px", "pz", None),
    )
    return jax.shard_map(body, mesh=mesh, in_specs=in_specs, out_specs=out_specs, check_vma=False)
```

time: 444 us -> 236 us (0.53); the launches traced: 436 us -> 235 us
  local copies, waits for them, and re-layouts: 154 us -> 1.57 us
  matrix products: 73.1 us -> 0 us
  blocking collectives: 71.8 us -> 142 us
  waiting for transfers between devices: 103 us -> 38.1 us
  Pallas kernels: 0 us -> 43.5 us
  starting transfers between devices: 25.7 us -> 8.54 us
  other arithmetic: 7.4 us -> 0.67 us
    dot_general x16 -> x0, matrix products: 73.1 us -> none  [the longest x1 16.9 us: body(): jnp.einsum('xzab,cxzb->cxza', tau_inverse[..., HALF:], odd_side, precisio...]
    all_to_all x2 -> x3, blocking collectives: 71.8 us -> 142 us  [exchange(): return lax.all_to_all(array, axis, split_axis=0, concat_axis=0, tiled=True)]
    reshape x13 -> x0, local copies, waits for them, and re-layouts: 67.8 us -> none  [the longest x4 24.1 us: to_xlines(): array.transpose(0, 3, 1, 4, 2).reshape((lead, groups_x * local_x, width))]
    all_to_all x3 -> x1, waiting for transfers between devices: 103 us -> 38.1 us  [exchange(): return lax.all_to_all(array, axis, split_axis=0, concat_axis=0, tiled=True)]
    slice x8 -> x0, local copies, waits for them, and re-layouts: 56.8 us -> none  [the longest x1 28.9 us: body(): odd_side = right_side[..., 1::2]]
    pallas_call x0 -> x5, Pallas kernels: none -> 43.5 us  [the longest x1 17.1 us: y_solve(): pl.pallas_call(kernel, name='y_solve', grid=(LX,), in_specs=[whole(GX * s...]
    transpose x3 -> x0, local copies, waits for them, and re-layouts: 19.2 us -> none  [the longest x1 13 us: body(): received.transpose(0, 2, 3, 1, 4).reshape((count, 6, block_x, block_y, NZ))]
    all_to_all x3 -> x1, starting transfers between devices: 25.7 us -> 8.54 us  [exchange(): return lax.all_to_all(array, axis, split_axis=0, concat_axis=0, tiled=True)]
  transfers between devices with their start and end apart: 3 -> 1, of which waited for: 3 -> 1; matrix products, arithmetic and copies ran while one was open for 6% -> 0% of each run, Pallas kernels for 0% -> 0%
where the time goes in v1:
time: 236 us; the launch traced here: 235 us
  blocking collectives  142 us (60%)
  Pallas kernels  43.5 us (18%)
  waiting for transfers between devices  38.1 us (16%)
  starting transfers between devices  8.54 us (4%)
    all_to_all x3, blocking collectives, exchange(): return lax.all_to_all(array, axis, split_axis=0, concat_axis=0, tiled=True)  142 us
    all_to_all x1, waiting for transfers between devices, exchange(): return lax.all_to_all(array, axis, split_axis=0, concat_axis=0, tiled=True)  38.1 us
    pallas_call x1, Pallas kernels, y_solve(): pl.pallas_call(kernel, name='y_solve', grid=(LX,), in_specs=[whole(GX * s...  17.1 us
    pallas_call x1, Pallas kernels, z_stage(): pl.pallas_call(kernel, name='z_stage', out_shape=jax.ShapeDtypeStruct((GZ...  9.19 us
    all_to_all x1, starting transfers between devices, exchange(): return lax.all_to_all(array, axis, split_axis=0, concat_axis=0, tiled=True)  8.54 us
    pallas_call x1, Pallas kernels, y_forward(): pl.pallas_call(kernel, name='y_forward', out_shape=jax.ShapeDtypeStruct((...  6.98 us
    pallas_call x1, Pallas kernels, x_forward(): pl.pallas_call(kernel, name='x_forward', out_shape=jax.ShapeDtypeStruct((...  5.94 us
  transfers between devices with their start and end apart: 1, of which 1 were waited for; matrix products, arithmetic and copies ran while one was open for 0% of the time, Pallas kernels for 0%

profile of v1, /device:TPU:1, one launch (start us, length us, event | category | flops | bytes accessed | tf_op | source)
XLA Modules:
  0.0 235.3 jit_solution(13278169102169280389)
XLA Ops:
  0.6 7.0 %y_forward.1 = f32[5120,128]{1,0:T(8,128)} custom-call(f32[3,8,32,128]{3,2,1,0:T(8,128)} %refs_0_.3, f32[3,8,32,128]{3,2,1,0:T(8,128)} %refs_1_.3, f32[3,8,32,128]{3,2,1,0:T(8,128)} %bitcast.11, f32[3,8,32,128]{3,2,1,0:T(8,128)} %bitcast.13, bf16[256,256]{1,0:T(8,128)(2,1)} %constant.18.clone.refs_4_, bf16[256,128]{1,0:T(8,128)(2,1)} %constant.19.clone.refs_5_), custom_call_target="tpu_custom_call" | custom-call | tf_op jit(solution)/shard_map/y_forward/pallas_call | solution.py:147
  7.6 72.9 %all_to_all.20.in_ref = f32[32,20,8,128]{3,2,1,0:T(8,128)} all-to-all(f32[32,20,8,128]{3,2,1,0:T(8,128)} %bitcast.9), channel_id=1, replica_groups=mesh['px'=32,'pz'=8] {'px'}, dimensions={0} | all-to-all | bytes 5242880 | tf_op jit(solution)/shard_map/all_to_all | solution.py:360
  80.5 5.9 %x_forward.1 = f32[8,24,32,128]{3,2,1,0:T(8,128)} custom-call(f32[32,20,8,128]{3,2,1,0:T(8,128)} %all_to_all.20.in_ref, bf16[256,768]{1,0:T(8,128)(2,1)} %constant.20.clone.value_ref, bf16[256,768]{1,0:T(8,128)(2,1)} %constant.21.clone.slope_ref), custom_call_target="tpu_custom_call" | custom-call | tf_op jit(solution)/shard_map/x_forward/pallas_call | solution.py:174
  86.4 44.6 %all_to_all.21.in_ref = f32[8,24,32,128]{3,2,1,0:T(8,128)} all-to-all(f32[8,24,32,128]{3,2,1,0:T(8,128)} %x_forward.1), channel_id=1, replica_groups=mesh['px'=32,'pz'=8] {'pz'}, dimensions={0} | all-to-all | bytes 6291456 | tf_op jit(solution)/shard_map/all_to_all | solution.py:360
  131.0 9.2 %z_stage.1 = f32[8,12,32,128]{3,2,1,0:T(8,128)} custom-call(f32[8,24,32,128]{3,2,1,0:T(8,128)} %all_to_all.21.in_ref, bf16[768,256]{1,0:T(8,128)(2,1)} %constant.22.clone.value_ref, bf16[768,256]{1,0:T(8,128)(2,1)} %constant.23.clone.slope_ref), custom_call_target="tpu_custom_call" | custom-call | tf_op jit(solution)/shard_map/z_stage/pallas_call | solution.py:246
  140.2 24.7 %all_to_all.22.in_ref = f32[8,12,32,128]{3,2,1,0:T(8,128)} all-to-all(f32[8,12,32,128]{3,2,1,0:T(8,128)} %z_stage.1), channel_id=1, replica_groups=mesh['px'=32,'pz'=8] {'pz'}, dimensions={0} | all-to-all | bytes 3145728 | tf_op jit(solution)/shard_map/all_to_all | solution.py:360
  165.0 0.0 copy-start.1
  165.0 4.3 %x_backward.1 = f32[32,12,8,128]{3,2,1,0:T(8,128)} custom-call(f32[8,12,32,128]{3,2,1,0:T(8,128)} %all_to_all.22.in_ref, bf16[256,768]{1,0:T(8,128)(2,1)} %constant.20.clone.value_ref), custom_call_target="tpu_custom_call" | custom-call | tf_op jit(solution)/shard_map/x_backward/pallas_call | solution.py:269
  169.2 0.0 copy-start.2
  169.2 8.5 %all-to-all-start.3 = ((f32[32,12,8,128]{3,2,1,0:T(8,128)}), f32[32,12,8,128]{3,2,1,0:T(8,128)S(1)}, u32[]{:S(2)}, u32[]{:S(2)}) async-start(f32[32,12,8,128]{3,2,1,0:T(8,128)} %x_backward.1), calls=%async_computation.3 | async-start | bytes 3145728 | tf_op jit(solution)/shard_map/all_to_all | solution.py:360
  177.8 0.0 copy-done.1
  177.8 0.1 ne.25
  177.9 0.1 copy.20
  178.0 0.1 ne.23
  178.1 0.0 copy-done.2
  178.1 0.1 broadcast_in_dim.8
  178.2 0.7 compare_convert_fusion.refs_5_
  178.8 38.1 %all-to-all-done.3 = f32[32,12,8,128]{3,2,1,0:T(8,128)S(1)} async-done(((f32[32,12,8,128]{3,2,1,0:T(8,128)}), f32[32,12,8,128]{3,2,1,0:T(8,128)S(1)}, u32[]{:S(2)}, u32[]{:S(2)}) %all-to-all-start.3) | async-done | bytes 1572896 | tf_op jit(solution)/shard_map/all_to_all | solution.py:360
  216.9 0.0 copy-start
  217.0 0.9 broadcast_in_dim.9.refs_4_
  217.8 0.3 copy-done
  218.2 17.1 %y_solve.1 = (f32[3,8,32,128]{3,2,1,0:T(8,128)}, f32[3,8,32,128]{3,2,1,0:T(8,128)}, f32[3,8,32,128]{3,2,1,0:T(8,128)}, f32[3,8,32,128]{3,2,1,0:T(8,128)}) custom-call(f32[3072,128]{1,0:T(8,128)} %bitcast.10, f32[3,8,32,128]{3,2,1,0:T(8,128)} %refs_0_.3, f32[3,8,32,128]{3,2,1,0:T(8,128)} %refs_1_.3, f32[3,8,32,128]{3,2,1,0:T(8,128)} %bitcast.12, ...), custom_call_target="tpu_custom_call" | custom-call | tf_op jit(solution)/shard_map/y_solve/pallas_call | solution.py:339
  (4 shorter events, 0.0 us)
Async XLA Ops:
  165.0 12.8 %copy-start.1 = (s32[8,32,2]{1,2,0:T(2,128)S(1)}, s32[8,32,2]{1,2,0:T(2,128)}, u32[]{:S(2)}) copy-start(s32[8,32,2]{1,2,0:T(2,128)} %param.20) | copy-start | bytes 6148
  169.2 8.9 %copy-start.2 = (s32[8,32]{1,0:T(8,128)S(1)}, s32[8,32]{1,0:T(8,128)}, u32[]{:S(2)}) copy-start(s32[8,32]{1,0:T(8,128)} %param.19) | copy-start | bytes 3076
  169.2 47.7 %all-to-all-start.3 = ((f32[32,12,8,128]{3,2,1,0:T(8,128)}), f32[32,12,8,128]{3,2,1,0:T(8,128)S(1)}, u32[]{:S(2)}, u32[]{:S(2)}) async-start(f32[32,12,8,128]{3,2,1,0:T(8,128)} %x_backward.1), calls=%async_computation.3 | async-start | bytes 3145728 | tf_op jit(solution)/shard_map/all_to_all | solution.py:360
  216.9 1.2 copy-start

commit v2 on v1

v2 whole, which is shorter than its diff:
```python
import math

import jax
import jax.numpy as jnp
import numpy as np
from jax import lax
from jax.experimental import pallas as pl
from jax.experimental.pallas import tpu as pltpu
from jax.sharding import PartitionSpec as P

NX = 256
NZ = 256
NY = 128
HALF = 64
GX = 32
GZ = 8
LX = NX // GX
LZ = NZ // GZ
QY = NY // GX
BX = NX // GZ
F32 = jnp.float32
BF16 = jnp.bfloat16

step_gain = 0.5


def split_table(table):
    table = np.asarray(table, np.float32)
    high = table.astype(jnp.bfloat16)
    low = (table - high.astype(np.float32)).astype(jnp.bfloat16)
    return high, low


def hartley(length):
    index = np.arange(length)
    angle = (index[:, None] * index[None, :] % length) * (2.0 * math.pi / length)
    return (np.cos(angle) + np.sin(angle)) / math.sqrt(length)


def hartley_slope(length):
    index = np.arange(length)
    angle = (index[:, None] * index[None, :] % length) * (2.0 * math.pi / length)
    signed = np.where(index < length // 2, index, index - length)
    return (np.cos(angle) - np.sin(angle)) * (signed * (2.0 * math.pi / length))[None, :] / math.sqrt(length)


def chebyshev(length):
    index = np.arange(length)
    angle = ((2 * index[:, None] + 1) * index[None, :] % (4 * length)) * (math.pi / (2 * length))
    scale = np.where(index == 0, math.sqrt(1.0 / length), math.sqrt(2.0 / length))
    return np.cos(angle) * scale[None, :]


def chebyshev_slope(length):
    index = np.arange(length)
    angle = ((2 * index[:, None] + 1) * index[None, :] % (4 * length)) * (math.pi / (2 * length))
    nodes = np.sin((2 * index + 1) * (math.pi / (2 * length)))
    scale = np.where(index == 0, math.sqrt(1.0 / length), math.sqrt(2.0 / length)) * index
    return np.sin(angle) * scale[None, :] / (length * nodes[:, None])


def node_order():
    return (np.arange(GX)[None, :] * QY + np.arange(QY)[:, None]).reshape(-1)


def parity_order():
    return (2 * np.arange(HALF)[None, :] + np.arange(2)[:, None]).reshape(-1)


def beside(table):
    return np.concatenate(split_table(table), 1)


def tables():
    nodes = node_order()
    cheb = chebyshev(NY)
    both = np.concatenate([cheb[nodes], chebyshev_slope(NY)[nodes]], 0)
    order = parity_order()
    gather = (np.arange(NY)[:, None] == order[None, :]).astype(jnp.bfloat16)
    place = gather.T
    even, odd = place[:HALF], place[HALF:]
    return dict(
        y_first=beside(both),
        value=beside(hartley(NX)),
        x_slope=beside(hartley_slope(NX)),
        z_slope=beside(hartley_slope(NZ).T),
        y_back=np.concatenate([*split_table(cheb[nodes][:, order]), gather], 0),
        spread=np.concatenate([even, even, odd, odd], 0),
    )


def three(table):
    half = table.shape[1] // 2
    return jnp.concatenate([table[:, :half], table[:, :half], table[:, half:]], 1)


def near(array):
    return pltpu.with_memory_space_constraint(array, pltpu.VMEM)


def dot(left, right):
    return lax.dot_general(left, right, (((1,), (0,)), ((), ())), preferred_element_type=F32)


def dot_nt(left, right):
    return lax.dot_general(left, right, (((1,), (1,)), ((), ())), preferred_element_type=F32)


def halves(array):
    high = array.astype(BF16)
    return high, (array - high.astype(F32)).astype(BF16)


def swap_strips(tiles):
    lane = lax.broadcasted_iota(jnp.int32, tiles[0].shape, 1)
    low = lane < 64
    even = (lane & 32) == 0
    first, second, third, fourth = tiles
    a = jnp.where(low, first, pltpu.roll(third, 64, 1))
    c = jnp.where(low, pltpu.roll(first, 64, 1), third)
    b = jnp.where(low, second, pltpu.roll(fourth, 64, 1))
    d = jnp.where(low, pltpu.roll(second, 64, 1), fourth)
    return [
        jnp.where(even, a, pltpu.roll(b, 32, 1)),
        jnp.where(even, pltpu.roll(a, 96, 1), b),
        jnp.where(even, c, pltpu.roll(d, 32, 1)),
        jnp.where(even, pltpu.roll(c, 96, 1), d),
    ]


def y_forward(velocities, first):
    count = len(velocities)
    stride = 5 * count * LX

    def kernel(*refs):
        sources, first_ref, out_ref = refs[:count], refs[count], refs[count + 1]
        for v in range(count):
            for comp in range(3):
                rows = NY if comp == 1 else 2 * NY
                high, low = halves(sources[v][comp].reshape(LX * LZ, NY))
                result = dot_nt(three(first_ref[0:rows]), jnp.concatenate([high, low, high], 1))
                for part in range(rows // NY):
                    field = 5 * v + (comp if part == 0 else 3 + comp // 2)
                    for quad in range(2):
                        tiles = [
                            result[part * NY + q * GX : part * NY + (q + 1) * GX, quad * 128 : (quad + 1) * 128]
                            for q in range(QY)
                        ]
                        for s, tile in enumerate(swap_strips(tiles)):
                            out_ref[pl.ds(field * LX + quad * 4 + s, GX, stride=stride), :] = tile

    out = pl.pallas_call(
        kernel,
        name="y_forward",
        out_shape=jax.ShapeDtypeStruct((GX * stride, 128), F32),
    )(*velocities, first)
    return out.reshape(GX, 5 * count, LX, 128)


def fill_blocks(target_ref, first_row, source_ref, first_lane, lanes, position):
    for k in range(GZ):
        start = pl.multiple_of((position ^ k) * BX, BX)
        row = first_row + k * BX
        target_ref[row : row + BX, :] = source_ref[pl.ds(start, BX), first_lane : first_lane + lanes]


def fill_rows(target_ref, source_ref, position):
    for group, lane in enumerate((0, 0, NZ)):
        fill_blocks(target_ref, group * NZ, source_ref, lane, NZ, position)


def x_forward(received, value, slope, position=None):
    count = received.shape[1] // 5
    parts_out = position is not None

    def kernel(*refs):
        if parts_out:
            position_ref, in_ref, value_ref, slope_ref = refs[:4]
            outs = refs[4 : 4 + GZ]
            value_own, slope_own = refs[4 + GZ :]
            fill_blocks(value_own, 0, value_ref, 0, 2 * NX, position_ref[0])
            fill_blocks(slope_own, 0, slope_ref, 0, 2 * NX, position_ref[0])
        else:
            in_ref, value_own, slope_own, out_ref = refs

        @pl.loop(0, count)
        def _(v):
            parts = [halves(in_ref[:, 5 * v + i].reshape(NX, 128)) for i in range(5)]
            high = jnp.concatenate([p[0] for p in parts], 1)
            low = jnp.concatenate([p[1] for p in parts], 1)
            stack = jnp.concatenate([high, low, high], 0)
            plain = dot(three(value_own[...]), stack)
            slopes = dot(three(slope_own[...]), stack[:, 128:384])
            u, vv, w, dyu, dyw = [plain[:, 128 * i : 128 * (i + 1)] for i in range(5)]
            dxv, dxw = slopes[:, :128], slopes[:, 128:]
            for i, piece in enumerate([u, vv, w, dyw, dxw, dxv - dyu]):
                if parts_out:
                    for k in range(GZ):
                        outs[k][6 * v + i] = piece[k * BX : (k + 1) * BX]
                else:
                    out_ref[:, 6 * v + i] = piece.reshape(GZ, BX, 128)

    vmem = pl.BlockSpec(memory_space=pltpu.VMEM)
    if parts_out:
        return pl.pallas_call(
            kernel,
            name="x_forward_parts",
            in_specs=[pl.BlockSpec(memory_space=pltpu.SMEM), vmem, vmem, vmem],
            out_shape=[jax.ShapeDtypeStruct((6 * count, BX, 128), F32)] * GZ,
            scratch_shapes=[pltpu.VMEM((NX, 2 * NX), BF16), pltpu.VMEM((NX, 2 * NX), BF16)],
        )(position, near(received), value, slope)
    return pl.pallas_call(
        kernel,
        name="x_forward",
        in_specs=[vmem, vmem, vmem],
        out_shape=jax.ShapeDtypeStruct((GZ, 6 * count, BX, 128), F32),
    )(near(received), value, slope)


ROWS = QY * BX


def cross(velocity, vortex):
    return [
        velocity[(i + 1) % 3] * vortex[(i + 2) % 3] - velocity[(i + 2) % 3] * vortex[(i + 1) % 3] for i in range(3)
    ]


def added(*terms):
    result = terms[0]
    for term in terms[1:]:
        result = [a + b for a, b in zip(result, term)]
    return result


def z_stage(received, value, slope, position, earlier=None):
    split_in = isinstance(received, (list, tuple))
    inputs = list(received) if split_in else [received]
    count = 2
    keep = earlier is None

    def kernel(*refs):
        position_ref = refs[0]
        in_refs = refs[1 : 1 + len(inputs)]
        at = 1 + len(inputs)
        value_ref, slope_ref = refs[at : at + 2]
        at += 2
        if not keep:
            old = refs[at]
            at += 1
        outs = refs[at : at + GZ]
        at += GZ
        if keep:
            phys = refs[at]
            at += 1
        force, value_own, slope_own, back_own = refs[at : at + 4]
        if not keep:
            phys = refs[at + 4]
        fill_blocks(back_own, 0, value_ref, 0, 2 * NZ, position_ref[0])
        order = position_ref[0] if split_in else 0
        fill_rows(value_own, value_ref, order)
        fill_rows(slope_own, slope_ref, order)
        if split_in:
            source = lambda block, field: in_refs[block][field]
        else:
            source = lambda block, field: in_refs[0][block, field]

        @pl.loop(0, count)
        def _(v):
            lefts = []
            for i in range(6):
                sides = [swap_strips([source(4 * side + h, 6 * v + i) for h in range(4)]) for side in range(2)]
                lines = jnp.concatenate(
                    [jnp.concatenate([sides[0][q], sides[1][q]], 1) for q in range(QY)], 0
                )
                high, low = halves(lines)
                lefts.append(jnp.concatenate([high, low, high], 1))
            values = dot(jnp.concatenate(lefts, 0), value_own[...])
            slopes = dot(jnp.concatenate(lefts[0:2], 0), slope_own[...])
            pieces = [values[ROWS * i : ROWS * (i + 1)] for i in range(6)]
            pieces[3] = pieces[3] - slopes[ROWS:]
            pieces[4] = slopes[:ROWS] - pieces[4]
            for i in range(6):
                phys[6 * v + i] = pieces[i]

        def cross_terms(r, carry):
            rows = pl.ds(pl.multiple_of(r * 8, 8), 8)
            new = [phys[i, rows, :] for i in range(12)]
            if keep:
                base_v, base_o, adj_v, adj_o = new[0:3], new[3:6], new[6:9], new[9:12]
                results = cross(base_v, base_o) + added(cross(base_v, adj_o), cross(adj_v, base_o))
            else:
                past = [old[i, rows, :] for i in range(12)]
                base_v, base_o, adj_v, adj_o = past[0:3], past[3:6], past[6:9], past[9:12]
                tang_v, tang_o, sec_v, sec_o = new[0:3], new[3:6], new[6:9], new[9:12]
                results = added(cross(base_v, tang_o), cross(tang_v, base_o)) + added(
                    cross(base_v, sec_o), cross(sec_v, base_o), cross(tang_v, adj_o), cross(adj_v, tang_o)
                )
            for i, piece in enumerate(results):
                force[i, rows, :] = piece
            return carry

        lax.fori_loop(0, ROWS // 8, cross_terms, 0, unroll=2)

        @pl.loop(0, count)
        def _(v):
            lefts = []
            for i in range(3):
                high, low = halves(force[3 * v + i])
                lefts.append(jnp.concatenate([high, low, high], 1))
            result = dot_nt(jnp.concatenate(lefts, 0), three(back_own[...]))
            for i in range(3):
                for side in range(2):
                    tiles = [
                        result[ROWS * i + q * BX : ROWS * i + (q + 1) * BX, 128 * side : 128 * (side + 1)]
                        for q in range(QY)
                    ]
                    for h, tile in enumerate(swap_strips(tiles)):
                        outs[4 * side + h][3 * v + i] = tile

    vmem = pl.BlockSpec(memory_space=pltpu.VMEM)
    extra = [] if keep else [earlier]
    grid_fields = jax.ShapeDtypeStruct((6 * count, ROWS, NZ), F32)
    scratch = [
        pltpu.VMEM((3 * count, ROWS, NZ), F32),
        pltpu.VMEM((3 * NZ, NZ), BF16),
        pltpu.VMEM((3 * NZ, NZ), BF16),
        pltpu.VMEM((NZ, 2 * NZ), BF16),
    ]
    if not keep:
        scratch.append(pltpu.VMEM((6 * count, ROWS, NZ), F32))
    result = pl.pallas_call(
        kernel,
        name="z_stage_first" if keep else "z_stage_second",
        in_specs=[pl.BlockSpec(memory_space=pltpu.SMEM)] + [vmem] * (len(inputs) + 2 + len(extra)),
        out_shape=[jax.ShapeDtypeStruct((3 * count, BX, 128), F32)] * GZ + ([grid_fields] if keep else []),
        scratch_shapes=scratch,
    )(position, *[near(a) for a in inputs], value, slope, *extra)
    return result[:GZ], (result[GZ] if keep else None)


def x_backward(received, value, position):
    fields = received[0].shape[0]

    def kernel(*refs):
        position_ref = refs[0]
        in_refs = refs[1 : 1 + GZ]
        value_ref, out_ref, lines = refs[1 + GZ :]
        for k in range(GZ):
            start = pl.multiple_of((position_ref[0] ^ k) * BX, BX)
            lines[:, pl.ds(start, BX), :] = in_refs[k][...]
        for pair in range(fields // 2):
            parts = [halves(lines[2 * pair + i]) for i in range(2)]
            high = jnp.concatenate([p[0] for p in parts], 1)
            low = jnp.concatenate([p[1] for p in parts], 1)
            result = dot(three(value_ref[...]), jnp.concatenate([high, low, high], 0))
            for i in range(2):
                out_ref[:, 2 * pair + i] = result[:, 128 * i : 128 * (i + 1)].reshape(GX, LX, 128)

    vmem = pl.BlockSpec(memory_space=pltpu.VMEM)
    return pl.pallas_call(
        kernel,
        name="x_backward",
        in_specs=[pl.BlockSpec(memory_space=pltpu.SMEM)] + [vmem] * (GZ + 1),
        out_shape=jax.ShapeDtypeStruct((GX, fields, LX, 128), F32),
        scratch_shapes=[pltpu.VMEM((fields, NX, 128), F32)],
    )(position, *[near(a) for a in received], value)


PAD = 8


def y_backward(received, velocities, gain, keep, y_back):
    fields = received.shape[1]
    lines = LX * LZ
    stride = fields * LX

    def kernel(in_ref, first, second, gain_ref, keep_ref, back_ref, right):
        sources = [first, second]
        for v in range(2):
            lefts = []
            for comp in range(3):
                f = 3 * v + comp
                quads = []
                for quad in range(2):
                    tiles = swap_strips(
                        [in_ref[pl.ds(f * LX + quad * 4 + s, GX, stride=stride), :] for s in range(4)]
                    )
                    quads.append(jnp.concatenate(tiles, 0).T)
                high, low = halves(jnp.concatenate(quads, 0) * gain_ref[...])
                own_high, own_low = halves(sources[v][comp].reshape(lines, NY))
                lefts.append(jnp.concatenate([high, low, high, own_high, own_low], 1))
            high, low, own = back_ref[0:NY], back_ref[NY : 2 * NY], back_ref[2 * NY : 3 * NY]
            result = dot(jnp.concatenate(lefts, 0), jnp.concatenate([high, high, low, own, own], 0))
            for comp in range(3):
                line = result[lines * comp : lines * (comp + 1)]
                right[pl.ds(3 * v + comp, lines, stride=PAD), :] = jnp.where(keep_ref[...] > 0.5, line, 0.0)

        for f in range(fields, PAD):
            right[pl.ds(f, lines, stride=PAD), :] = jnp.zeros((lines, NY), F32)

    vmem = pl.BlockSpec(memory_space=pltpu.VMEM)
    return pl.pallas_call(
        kernel,
        name="y_backward",
        in_specs=[vmem] * 6,
        out_shape=jax.ShapeDtypeStruct((lines * PAD, NY), F32),
    )(near(received.reshape(GX * stride, 128)), *velocities, near(gain), near(keep), y_back)


def solve(first, second, tau_inverse, spread):
    pad = 2 * PAD

    def kernel(first_ref, second_ref, tau_ref, spread_ref, *refs):
        outs = refs[:4]
        solved, solved_odd = refs[4:]
        lane = lax.broadcasted_iota(jnp.int32, (pad, NY), 1)
        first_half = lane < HALF
        zero = jnp.zeros((4 * pad, NY), BF16)

        def pair(k, carry):
            weights = []
            lefts = []
            for i in range(2):
                mode = 2 * k + i
                high, low = halves(tau_ref[0, mode])
                weights.append(jnp.concatenate([high, low], 0))
                at = pl.ds(pl.multiple_of(mode * PAD, PAD), PAD)
                line = jnp.concatenate([first_ref[at, :], second_ref[at, :]], 0)
                even = halves(jnp.where(first_half, line, 0.0))
                odd = halves(jnp.where(first_half, 0.0, line))
                lefts.append(jnp.concatenate([even[0], odd[0], even[1], odd[1]], 0))
            left = jnp.concatenate(
                [jnp.concatenate([lefts[0], zero], 1), jnp.concatenate([zero, lefts[1]], 1)], 0
            )
            result = dot_nt(left, jnp.concatenate(weights, 1))
            for i in range(2):
                piece = result[4 * pad * i : 4 * pad * (i + 1)]
                piece = piece[: 2 * pad] + piece[2 * pad :]
                at = pl.ds(pl.multiple_of((2 * k + i) * pad, pad), pad)
                solved[at, :] = piece[:pad]
                solved_odd[at, :] = piece[pad:]
            return carry

        lax.fori_loop(0, LZ // 2, pair, 0, unroll=8)

        highs, lows = [], []
        for f in range(12):
            row = f if f < 6 else f + PAD - 6
            high0, low0 = halves(solved[pl.ds(row, LZ, stride=pad), :])
            high1, low1 = halves(solved_odd[pl.ds(row, LZ, stride=pad), :])
            highs.append(jnp.concatenate([high0, high1], 1))
            lows.append(jnp.concatenate([low0, low1], 1))
        result = dot(jnp.concatenate(highs + lows, 0), spread_ref[...])
        for f in range(12):
            outs[f // 3][f % 3, 0] = result[LZ * f : LZ * (f + 1)] + result[LZ * (12 + f) : LZ * (13 + f)]

    return pl.pallas_call(
        kernel,
        name="solve",
        grid=(LX,),
        in_specs=[
            pl.BlockSpec((LZ * PAD, NY), lambda i: (i, 0)),
            pl.BlockSpec((LZ * PAD, NY), lambda i: (i, 0)),
            pl.BlockSpec((1, LZ, HALF, NY), lambda i: (i, 0, 0, 0)),
            pl.BlockSpec((2 * NY, NY), lambda i: (0, 0)),
        ],
        out_specs=[pl.BlockSpec((3, 1, LZ, NY), lambda i: (0, i, 0, 0)) for _ in range(4)],
        out_shape=[jax.ShapeDtypeStruct((3, LX, LZ, NY), F32) for _ in range(4)],
        scratch_shapes=[pltpu.VMEM((LZ * pad, NY), F32), pltpu.VMEM((LZ * pad, NY), F32)],
        compiler_params=pltpu.CompilerParams(dimension_semantics=("arbitrary",)),
    )(first, second, tau_inverse, spread)


def exchange(array, axis):
    return lax.all_to_all(array, axis, split_axis=0, concat_axis=0, tiled=True)


def exchange_parts(parts):
    return [parts[0]] + [lax.ppermute(parts[k], "pz", [(i, i ^ k) for i in range(GZ)]) for k in range(1, GZ)]


def body(base, adjoint, tangent, second, dealias_mask, tau_rows, tau_inverse):
    table = tables()
    one = [base, adjoint]
    two = [tangent.reshape(adjoint.shape), second.reshape(adjoint.shape)]
    position = lax.axis_index("pz").astype(jnp.int32).reshape(1)
    gain = jnp.broadcast_to((step_gain * dealias_mask.astype(F32)).reshape(LX * LZ, 1), (LX * LZ, NY))
    rows = tau_rows.reshape(LX * LZ, 2)[:, :, None]
    keep = (jnp.arange(HALF, dtype=jnp.int32) != rows).astype(F32).reshape(LX * LZ, NY)
    sent_one = y_forward(one, table["y_first"])
    whole_one = exchange(sent_one, "px")
    sent_two = y_forward(two, table["y_first"])
    whole_two = exchange(sent_two, "px")
    parts_one = x_forward(whole_one, table["value"], table["x_slope"], position)
    lines_one = exchange_parts(parts_one)
    partial_two = x_forward(whole_two, table["value"], table["x_slope"])
    lines_two = exchange(partial_two, "pz")
    back_one, grid_one = z_stage(lines_one, table["value"], table["z_slope"], position)
    mixed_one = exchange_parts(back_one)
    modes_one = x_backward(mixed_one, table["value"], position)
    nodes_one = exchange(modes_one, "px")
    back_two, _ = z_stage(
        lines_two, table["value"], table["z_slope"], position, grid_one
    )
    mixed_two = exchange_parts(back_two)
    modes_two = x_backward(mixed_two, table["value"], position)
    nodes_two = exchange(modes_two, "px")
    right_one = y_backward(nodes_one, one, gain, keep, table["y_back"])
    right_two = y_backward(nodes_two, two, gain, keep, table["y_back"])
    outs = solve(right_one, right_two, tau_inverse, table["spread"])
    return (outs[0], outs[1], outs[2].reshape(tangent.shape), outs[3].reshape(second.shape))


def solution(mesh):
    in_specs = (
        P(None, "px", "pz", None),
        P(None, "px", "pz", None),
        P(None, None, "px", "pz", None),
        P(None, None, "px", "pz", None),
        P("px", "pz"),
        P("px", "pz", None),
        P("px", "pz", None, None),
    )
    out_specs = (
        P(None, "px", "pz", None),
        P(None, "px", "pz", None),
        P(None, None, "px", "pz", None),
        P(None, None, "px", "pz", None),
    )
    return jax.shard_map(body, mesh=mesh, in_specs=in_specs, out_specs=out_specs, check_vma=False)
```

time: 236 us -> 249 us (1.055)
  blocking collectives: 142 us -> 0 us
  starting transfers between devices: 8.54 us -> 83.1 us
  waiting for transfers between devices: 38.1 us -> 108 us
  local copies, waits for them, and re-layouts: 1.57 us -> 7.58 us
  Pallas kernels: 43.5 us -> 47.8 us
    all_to_all x3 -> x0, blocking collectives: 142 us -> none  [exchange(): return lax.all_to_all(array, axis, split_axis=0, concat_axis=0, tiled=True)]
    all_to_all x1 -> x5, waiting for transfers between devices: 38.1 us -> 77.9 us  [exchange(): return lax.all_to_all(array, axis, split_axis=0, concat_axis=0, tiled=True)]
    ppermute x0 -> x21, starting transfers between devices: none -> 39.6 us  [exchange_parts(): lax.ppermute(parts[k], 'pz', [(i, i ^ k) for i in range(GZ)])]
    all_to_all x1 -> x5, starting transfers between devices: 8.54 us -> 43.6 us  [exchange(): return lax.all_to_all(array, axis, split_axis=0, concat_axis=0, tiled=True)]
    ppermute x0 -> x21, waiting for transfers between devices: none -> 30.5 us  [exchange_parts(): lax.ppermute(parts[k], 'pz', [(i, i ^ k) for i in range(GZ)])]
    unnamed x7 -> x19, local copies, waits for them, and re-layouts: 0.34 us -> 7.14 us
    pallas_call x4 -> x9, Pallas kernels: 36.5 us -> 41 us  [the longest x2 11.3 us: z_stage(): pl.pallas_call(kernel, name='z_stage_first' if keep else 'z_stage_second'...]
    pallas_call x1 -> x2, Pallas kernels: 6.98 us -> 6.8 us  [y_forward(): pl.pallas_call(kernel, name='y_forward', out_shape=jax.ShapeDtypeStruct((...]
  transfers between devices with their start and end apart: 1 -> 26, of which waited for: 1 -> 11; matrix products, arithmetic and copies ran while one was open for 0% -> 0% of each run, Pallas kernels for 0% -> 12%
where the time goes in v2:
time: 249 us; the launch traced here: 248 us
  waiting for transfers between devices  108 us (43%)
  starting transfers between devices  83.1 us (33%)
  Pallas kernels  47.8 us (19%)
  local copies, waits for them, and re-layouts  7.58 us (3%)
    all_to_all x5, waiting for transfers between devices, exchange(): return lax.all_to_all(array, axis, split_axis=0, concat_axis=0, tiled=True)  77.9 us
    all_to_all x5, starting transfers between devices, exchange(): return lax.all_to_all(array, axis, split_axis=0, concat_axis=0, tiled=True)  43.6 us
    ppermute x21, starting transfers between devices, exchange_parts(): lax.ppermute(parts[k], 'pz', [(i, i ^ k) for i in range(GZ)])  39.6 us
    ppermute x21, waiting for transfers between devices, exchange_parts(): lax.ppermute(parts[k], 'pz', [(i, i ^ k) for i in range(GZ)])  30.5 us
    pallas_call x2, Pallas kernels, z_stage(): pl.pallas_call(kernel, name='z_stage_first' if keep else 'z_stage_second'...  11.3 us
    pallas_call x1, Pallas kernels, solve(): pl.pallas_call(kernel, name='solve', grid=(LX,), in_specs=[pl.BlockSpec((...  11 us
    pallas_call x2, Pallas kernels, y_backward(): pl.pallas_call(kernel, name='y_backward', in_specs=[vmem] * 6, out_shape=...  7.26 us
    unnamed x19, local copies, waits for them, and re-layouts  7.14 us
  transfers between devices with their start and end apart: 26, of which 11 were waited for; matrix products, arithmetic and copies ran while one was open for 0% of the time, Pallas kernels for 12%

profile of v2, /device:TPU:1, one launch (start us, length us, event | category | flops | bytes accessed | tf_op | source)
XLA Modules:
  0.0 247.8 jit_solution(15173873937839162570)
XLA Ops:
  0.6 3.4 %y_forward.3 = f32[2560,128]{1,0:T(8,128)} custom-call(f32[3,8,32,128]{3,2,1,0:T(8,128)} %bitcast.16, f32[3,8,32,128]{3,2,1,0:T(8,128)} %bitcast.18, bf16[256,256]{1,0:T(8,128)(2,1)} %constant.18.clone.refs_2_), custom_call_target="tpu_custom_call" | custom-call | tf_op jit(solution)/shard_map/y_forward/pallas_call | solution.py:152
  4.0 11.0 %all-to-all-start.2 = ((f32[32,10,8,128]{3,2,1,0:T(8,128)}), f32[32,10,8,128]{3,2,1,0:T(8,128)S(1)}, u32[]{:S(2)}, u32[]{:S(2)}) async-start(f32[32,10,8,128]{3,2,1,0:T(8,128)} %bitcast.15), calls=%async_computation.2 | async-start | bytes 2621440 | tf_op jit(solution)/shard_map/all_to_all | solution.py:476
  15.1 3.4 %y_forward.2 = f32[2560,128]{1,0:T(8,128)} custom-call(f32[3,8,32,128]{3,2,1,0:T(8,128)} %first.1, f32[3,8,32,128]{3,2,1,0:T(8,128)} %second.1, bf16[256,256]{1,0:T(8,128)(2,1)} %constant.18.clone.refs_2_), custom_call_target="tpu_custom_call" | custom-call | tf_op jit(solution)/shard_map/y_forward/pallas_call | solution.py:152
  18.5 30.3 %all-to-all-done.2.refs_0_ = f32[32,10,8,128]{3,2,1,0:T(8,128)S(1)} async-done(((f32[32,10,8,128]{3,2,1,0:T(8,128)}), f32[32,10,8,128]{3,2,1,0:T(8,128)S(1)}, u32[]{:S(2)}, u32[]{:S(2)}) %all-to-all-start.2) | async-done | bytes 1310752 | tf_op jit(solution)/shard_map/all_to_all | solution.py:476
  48.8 4.3 %all-to-all-start = ((f32[32,10,8,128]{3,2,1,0:T(8,128)}), f32[32,10,8,128]{3,2,1,0:T(8,128)S(1)}, u32[]{:S(2)}, u32[]{:S(2)}) async-start(f32[32,10,8,128]{3,2,1,0:T(8,128)} %bitcast.14), calls=%async_computation | async-start | bytes 2621440 | tf_op jit(solution)/shard_map/all_to_all | solution.py:476
  53.1 3.4 %x_forward.1 = f32[8,12,32,128]{3,2,1,0:T(8,128)} custom-call(f32[32,10,8,128]{3,2,1,0:T(8,128)S(1)} %all-to-all-done.2.refs_0_, bf16[256,512]{1,0:T(8,128)(2,1)} %constant.19.clone.refs_2_.refs_9_.refs_1_, bf16[256,512]{1,0:T(8,128)(2,1)} %constant.20.clone.refs_3_.refs_2_), custom_call_target="tpu_custom_call" | custom-call | tf_op jit(solution)/shard_map/x_forward/pallas_call | solution.py:212
  56.5 30.3 %all-to-all-done.refs_1_ = f32[32,10,8,128]{3,2,1,0:T(8,128)S(1)} async-done(((f32[32,10,8,128]{3,2,1,0:T(8,128)}), f32[32,10,8,128]{3,2,1,0:T(8,128)S(1)}, u32[]{:S(2)}, u32[]{:S(2)}) %all-to-all-start) | async-done | bytes 1310752 | tf_op jit(solution)/shard_map/all_to_all | solution.py:476
  86.8 1.1 copy-done
  87.9 6.4 %all-to-all-start.3 = ((f32[8,12,32,128]{3,2,1,0:T(8,128)}), f32[8,12,32,128]{3,2,1,0:T(8,128)S(1)}, u32[]{:S(2)}, u32[]{:S(2)}) async-start(f32[8,12,32,128]{3,2,1,0:T(8,128)} %x_forward.1), calls=%async_computation.3 | async-start | bytes 3145728 | tf_op jit(solution)/shard_map/all_to_all | solution.py:476
  94.3 1.3 copy-done.1
  95.6 3.3 %x_forward_parts.1 = (f32[12,32,128]{2,1,0:T(8,128)}, f32[12,32,128]{2,1,0:T(8,128)}, f32[12,32,128]{2,1,0:T(8,128)}, f32[12,32,128]{2,1,0:T(8,128)}, f32[12,32,...) custom-call(s32[1]{0:T(128)} %bitcast.refs_0_, ...), custom_call_target="tpu_custom_call" | custom-call | tf_op jit(solution)/shard_map/x_forward_parts/pallas_call | solution.py:205
  98.9 3.0 %collective-permute-start = (f32[12,32,128]{2,1,0:T(8,128)}, f32[12,32,128]{2,1,0:T(8,128)S(1)}, u32[]{:S(2)}, u32[]{:S(2)}) collective-permute-start(f32[12,32,128]{2,1,0:T(8,128)} %get-tuple-element.34), channel_id=1, source_target_pairs={{0,1},{1,0},{2,3},{3,2},{4,5},{5,4},{6,7},{7,6},{8,9},{9,8},{10,11... | collective-permute-start | bytes 589832 | tf_op jit(solution)/shard_map/ppermute | solution.py:480
  101.9 1.2 collective-permute-start.1
  103.0 0.0 collective-permute-start.2
  103.0 3.0 %collective-permute-start.3 = (f32[12,32,128]{2,1,0:T(8,128)}, f32[12,32,128]{2,1,0:T(8,128)S(1)}, u32[]{:S(2)}, u32[]{:S(2)}) collective-permute-start(f32[12,32,128]{2,1,0:T(8,128)} %get-tuple-element.37), channel_id=1, source_target_pairs={{0,4},{1,5},{2,6},{3,7},{4,0},{5,1},{6,2},{7,3},{8,12},{9,13},{10,... | collective-permute-start | bytes 589832 | tf_op jit(solution)/shard_map/ppermute | solution.py:480
  106.0 2.7 %collective-permute-start.4 = (f32[12,32,128]{2,1,0:T(8,128)}, f32[12,32,128]{2,1,0:T(8,128)S(1)}, u32[]{:S(2)}, u32[]{:S(2)}) collective-permute-start(f32[12,32,128]{2,1,0:T(8,128)} %get-tuple-element.38), channel_id=1, source_target_pairs={{0,5},{1,4},{2,7},{3,6},{4,1},{5,0},{6,3},{7,2},{8,13},{9,12},{10,... | collective-permute-start | bytes 589832 | tf_op jit(solution)/shard_map/ppermute | solution.py:480
  108.7 9.7 %collective-permute-done.refs_2_ = f32[12,32,128]{2,1,0:T(8,128)S(1)} collective-permute-done((f32[12,32,128]{2,1,0:T(8,128)}, f32[12,32,128]{2,1,0:T(8,128)S(1)}, u32[]{:S(2)}, u32[]{:S(2)}) %collective-permute-start) | collective-permute-done | bytes 196640 | tf_op jit(solution)/shard_map/ppermute | solution.py:480
  118.4 2.4 collective-permute-start.5
  120.8 0.8 collective-permute-start.6
  121.7 1.9 collective-permute-done.2.refs_4_
  123.5 7.9 %collective-permute-done.3.refs_5_ = f32[12,32,128]{2,1,0:T(8,128)S(1)} collective-permute-done((f32[12,32,128]{2,1,0:T(8,128)}, f32[12,32,128]{2,1,0:T(8,128)S(1)}, u32[]{:S(2)}, u32[]{:S(2)}) %collective-permute-start.3) | collective-permute-done | bytes 196640 | tf_op jit(solution)/shard_map/ppermute | solution.py:480
  131.4 2.0 collective-permute-done.6.refs_8_
  133.4 0.9 copy-done.4
  134.3 5.6 %z_stage_first.1 = (f32[6,32,128]{2,1,0:T(8,128)}, f32[6,32,128]{2,1,0:T(8,128)}, f32[6,32,128]{2,1,0:T(8,128)}, f32[6,32,128]{2,1,0:T(8,128)}, f32[6,32,128]{2,...) custom-call(s32[1]{0:T(128)} %bitcast.refs_0_, ...), custom_call_target="tpu_custom_call" | custom-call | tf_op jit(solution)/shard_map/z_stage_first/pallas_call | solution.py:332
  139.9 0.6 collective-permute-start.10
  140.5 4.1 %collective-permute-start.11 = (f32[6,32,128]{2,1,0:T(8,128)}, f32[6,32,128]{2,1,0:T(8,128)S(1)}, u32[]{:S(2)}, u32[]{:S(2)}) collective-permute-start(f32[6,32,128]{2,1,0:T(8,128)} %get-tuple-element.46), channel_id=1, source_target_pairs={{0,5},{1,4},{2,7},{3,6},{4,1},{5,0},{6,3},{7,2},{8,13},{9,12},{10,... | collective-permute-start | bytes 294920 | tf_op jit(solution)/shard_map/ppermute | solution.py:480
  144.6 2.6 %collective-permute-start.12 = (f32[6,32,128]{2,1,0:T(8,128)}, f32[6,32,128]{2,1,0:T(8,128)S(1)}, u32[]{:S(2)}, u32[]{:S(2)}) collective-permute-start(f32[6,32,128]{2,1,0:T(8,128)} %get-tuple-element.47), channel_id=1, source_target_pairs={{0,6},{1,7},{2,4},{3,5},{4,2},{5,3},{6,0},{7,1},{8,14},{9,15},{10,... | collective-permute-start | bytes 294920 | tf_op jit(solution)/shard_map/ppermute | solution.py:480
  147.2 0.7 collective-permute-start.13
  147.9 2.0 collective-permute-start.7
  149.9 0.0 collective-permute-done.10.refs_5_
  149.9 0.8 collective-permute-start.8
  150.8 0.0 collective-permute-done.11.refs_6_
  150.8 2.5 %collective-permute-start.9 = (f32[6,32,128]{2,1,0:T(8,128)}, f32[6,32,128]{2,1,0:T(8,128)S(1)}, u32[]{:S(2)}, u32[]{:S(2)}) collective-permute-start(f32[6,32,128]{2,1,0:T(8,128)} %get-tuple-element.44), channel_id=1, source_target_pairs={{0,3},{1,2},{2,1},{3,0},{4,7},{5,6},{6,5},{7,4},{8,11},{9,10},{10,... | collective-permute-start | bytes 294920 | tf_op jit(solution)/shard_map/ppermute | solution.py:480
  153.3 2.1 collective-permute-done.13.refs_8_
  155.4 0.0 collective-permute-done.7.refs_2_
  155.4 0.0 collective-permute-done.8.refs_3_
  155.4 1.8 collective-permute-done.9.refs_4_
  157.2 0.9 copy-done.5
  158.1 2.3 x_backward.2
  160.4 10.9 %all-to-all-start.1 = ((f32[32,6,8,128]{3,2,1,0:T(8,128)}), f32[32,6,8,128]{3,2,1,0:T(8,128)S(1)}, u32[]{:S(2)}, u32[]{:S(2)}) async-start(f32[32,6,8,128]{3,2,1,0:T(8,128)} %x_backward.2), calls=%async_computation.1 | async-start | bytes 1572864 | tf_op jit(solution)/shard_map/all_to_all | solution.py:476
  171.3 5.7 %z_stage_second.1 = (f32[6,32,128]{2,1,0:T(8,128)}, f32[6,32,128]{2,1,0:T(8,128)}, f32[6,32,128]{2,1,0:T(8,128)}, f32[6,32,128]{2,1,0:T(8,128)}, f32[6,32,128]{2...) custom-call(s32[1]{0:T(128)} %bitcast.refs_0_, ...), custom_call_target="tpu_custom_call" | custom-call | tf_op jit(solution)/shard_map/z_stage_second/pallas_call | solution.py:332
  177.0 1.5 collective-permute-start.14
  178.6 2.0 collective-permute-start.15
  180.6 0.8 collective-permute-start.16
  181.4 3.7 %collective-permute-start.17 = (f32[6,32,128]{2,1,0:T(8,128)}, f32[6,32,128]{2,1,0:T(8,128)S(1)}, u32[]{:S(2)}, u32[]{:S(2)}) collective-permute-start(f32[6,32,128]{2,1,0:T(8,128)} %get-tuple-element.54), channel_id=1, source_target_pairs={{0,4},{1,5},{2,6},{3,7},{4,0},{5,1},{6,2},{7,3},{8,12},{9,13},{10,... | collective-permute-start | bytes 294920 | tf_op jit(solution)/shard_map/ppermute | solution.py:480
  185.1 0.9 collective-permute-start.18
  186.0 0.9 collective-permute-start.19
  186.9 3.3 %collective-permute-start.20 = (f32[6,32,128]{2,1,0:T(8,128)}, f32[6,32,128]{2,1,0:T(8,128)S(1)}, u32[]{:S(2)}, u32[]{:S(2)}) collective-permute-start(f32[6,32,128]{2,1,0:T(8,128)} %get-tuple-element.57), channel_id=1, source_target_pairs={{0,7},{1,6},{2,5},{3,4},{4,3},{5,2},{6,1},{7,0},{8,15},{9,14},{10,... | collective-permute-start | bytes 294920 | tf_op jit(solution)/shard_map/ppermute | solution.py:480
  190.2 4.1 %collective-permute-done.18.refs_6_ = f32[6,32,128]{2,1,0:T(8,128)S(1)} collective-permute-done((f32[6,32,128]{2,1,0:T(8,128)}, f32[6,32,128]{2,1,0:T(8,128)S(1)}, u32[]{:S(2)}, u32[]{:S(2)}) %collective-permute-start.18) | collective-permute-done | bytes 98336 | tf_op jit(solution)/shard_map/ppermute | solution.py:480
  194.3 1.1 collective-permute-done.20.refs_8_
  195.4 0.9 copy-done.6
  196.3 2.4 x_backward.3
  198.6 0.9 copy-done.2
  199.5 11.0 %all-to-all-start.4 = ((f32[32,6,8,128]{3,2,1,0:T(8,128)}), f32[32,6,8,128]{3,2,1,0:T(8,128)S(1)}, u32[]{:S(2)}, u32[]{:S(2)}) async-start(f32[32,6,8,128]{3,2,1,0:T(8,128)} %x_backward.3), calls=%async_computation.4 | async-start | bytes 1572864 | tf_op jit(solution)/shard_map/all_to_all | solution.py:476
  210.5 0.1 ne.25
  210.6 0.1 copy.18
  210.7 0.1 ne.23
  210.8 0.1 broadcast_in_dim.8
  210.9 0.1 broadcast_in_dim.9.gain_ref
  211.0 1.1 copy-done.3
  212.2 3.6 %y_backward.2.first_ref = f32[2048,128]{1,0:T(8,128)} custom-call(f32[1536,128]{1,0:T(8,128)S(1)} %bitcast.12, f32[3,8,32,128]{3,2,1,0:T(8,128)} %first.1, f32[3,8,32,128]{3,2,1,0:T(8,128)} %second.1, f32[256,128]{1,0:T(8,128)S(1)} %broadcast_in_dim.9.gain_ref, f32[256,128]{1,0:T(8,128)S(1)} %compare_convert_fusion.keep_ref, ...), custom_call_target="tpu_custom_call" | custom-call | tf_op jit(solution)/shard_map/y_backward/pallas_call | solution.py:403
  215.8 17.3 %all-to-all-done.4 = f32[32,6,8,128]{3,2,1,0:T(8,128)S(1)} async-done(((f32[32,6,8,128]{3,2,1,0:T(8,128)}), f32[32,6,8,128]{3,2,1,0:T(8,128)S(1)}, u32[]{:S(2)}, u32[]{:S(2)}) %all-to-all-start.4) | async-done | bytes 786464 | tf_op jit(solution)/shard_map/all_to_all | solution.py:476
  233.1 3.6 %y_backward.3.second_ref = f32[2048,128]{1,0:T(8,128)} custom-call(f32[1536,128]{1,0:T(8,128)S(1)} %bitcast.13, f32[3,8,32,128]{3,2,1,0:T(8,128)} %bitcast.17, f32[3,8,32,128]{3,2,1,0:T(8,128)} %bitcast.19, f32[256,128]{1,0:T(8,128)S(1)} %broadcast_in_dim.9.gain_ref, f32[256,128]{1,0:T(8,128)S(1)} %compare_convert_fusion.keep_ref, ...), custom_call_target="tpu_custom_call" | custom-call | tf_op jit(solution)/shard_map/y_backward/pallas_call | solution.py:403
  236.7 11.0 %solve.1 = (f32[3,8,32,128]{3,2,1,0:T(8,128)}, f32[3,8,32,128]{3,2,1,0:T(8,128)}, f32[3,8,32,128]{3,2,1,0:T(8,128)}, f32[3,8,32,128]{3,2,1,0:T(8,128)}) custom-call(f32[2048,128]{1,0:T(8,128)} %y_backward.2.first_ref, f32[2048,128]{1,0:T(8,128)} %y_backward.3.second_ref, f32[8,32,64,128]{3,2,1,0:T(8,128)} %tau_ref.1, bf16[256,128]{1,0:T(8,128)(2,1)} %constant.23.clone.spread_ref), custom_call_target="tpu_custom_call" | custom-call | tf_op jit(solution)/shard_map/solve/pallas_call | solution.py:458
  (27 shorter events, 0.1 us)
Async XLA Ops:
  4.0 44.8 %all-to-all-start.2 = ((f32[32,10,8,128]{3,2,1,0:T(8,128)}), f32[32,10,8,128]{3,2,1,0:T(8,128)S(1)}, u32[]{:S(2)}, u32[]{:S(2)}) async-start(f32[32,10,8,128]{3,2,1,0:T(8,128)} %bitcast.15), calls=%async_computation.2 | async-start | bytes 2621440 | tf_op jit(solution)/shard_map/all_to_all | solution.py:476
  48.8 38.0 %all-to-all-start = ((f32[32,10,8,128]{3,2,1,0:T(8,128)}), f32[32,10,8,128]{3,2,1,0:T(8,128)S(1)}, u32[]{:S(2)}, u32[]{:S(2)}) async-start(f32[32,10,8,128]{3,2,1,0:T(8,128)} %bitcast.14), calls=%async_computation | async-start | bytes 2621440 | tf_op jit(solution)/shard_map/all_to_all | solution.py:476
  86.8 1.1 copy-start
  87.9 72.5 %all-to-all-start.3 = ((f32[8,12,32,128]{3,2,1,0:T(8,128)}), f32[8,12,32,128]{3,2,1,0:T(8,128)S(1)}, u32[]{:S(2)}, u32[]{:S(2)}) async-start(f32[8,12,32,128]{3,2,1,0:T(8,128)} %x_forward.1), calls=%async_computation.3 | async-start | bytes 3145728 | tf_op jit(solution)/shard_map/all_to_all | solution.py:476
  94.2 1.3 copy-start.1
  98.9 19.5 %collective-permute-start = (f32[12,32,128]{2,1,0:T(8,128)}, f32[12,32,128]{2,1,0:T(8,128)S(1)}, u32[]{:S(2)}, u32[]{:S(2)}) collective-permute-start(f32[12,32,128]{2,1,0:T(8,128)} %get-tuple-element.34), channel_id=1, source_target_pairs={{0,1},{1,0},{2,3},{3,2},{4,5},{5,4},{6,7},{7,6},{8,9},{9,8},{10,11... | collective-permute-start | bytes 589832 | tf_op jit(solution)/shard_map/ppermute | solution.py:480
  101.9 19.0 %collective-permute-start.1 = (f32[12,32,128]{2,1,0:T(8,128)}, f32[12,32,128]{2,1,0:T(8,128)S(1)}, u32[]{:S(2)}, u32[]{:S(2)}) collective-permute-start(f32[12,32,128]{2,1,0:T(8,128)} %get-tuple-element.35), channel_id=1, source_target_pairs={{0,2},{1,3},{2,0},{3,1},{4,6},{5,7},{6,4},{7,5},{8,10},{9,11},{10,... | collective-permute-start | bytes 589832 | tf_op jit(solution)/shard_map/ppermute | solution.py:480
  103.0 20.5 %collective-permute-start.2 = (f32[12,32,128]{2,1,0:T(8,128)}, f32[12,32,128]{2,1,0:T(8,128)S(1)}, u32[]{:S(2)}, u32[]{:S(2)}) collective-permute-start(f32[12,32,128]{2,1,0:T(8,128)} %get-tuple-element.36), channel_id=1, source_target_pairs={{0,3},{1,2},{2,1},{3,0},{4,7},{5,6},{6,5},{7,4},{8,11},{9,10},{10,... | collective-permute-start | bytes 589832 | tf_op jit(solution)/shard_map/ppermute | solution.py:480
  103.0 28.4 %collective-permute-start.3 = (f32[12,32,128]{2,1,0:T(8,128)}, f32[12,32,128]{2,1,0:T(8,128)S(1)}, u32[]{:S(2)}, u32[]{:S(2)}) collective-permute-start(f32[12,32,128]{2,1,0:T(8,128)} %get-tuple-element.37), channel_id=1, source_target_pairs={{0,4},{1,5},{2,6},{3,7},{4,0},{5,1},{6,2},{7,3},{8,12},{9,13},{10,... | collective-permute-start | bytes 589832 | tf_op jit(solution)/shard_map/ppermute | solution.py:480
  106.0 25.4 %collective-permute-start.4 = (f32[12,32,128]{2,1,0:T(8,128)}, f32[12,32,128]{2,1,0:T(8,128)S(1)}, u32[]{:S(2)}, u32[]{:S(2)}) collective-permute-start(f32[12,32,128]{2,1,0:T(8,128)} %get-tuple-element.38), channel_id=1, source_target_pairs={{0,5},{1,4},{2,7},{3,6},{4,1},{5,0},{6,3},{7,2},{8,13},{9,12},{10,... | collective-permute-start | bytes 589832 | tf_op jit(solution)/shard_map/ppermute | solution.py:480
  118.4 13.0 %collective-permute-start.5 = (f32[12,32,128]{2,1,0:T(8,128)}, f32[12,32,128]{2,1,0:T(8,128)S(1)}, u32[]{:S(2)}, u32[]{:S(2)}) collective-permute-start(f32[12,32,128]{2,1,0:T(8,128)} %get-tuple-element.39), channel_id=1, source_target_pairs={{0,6},{1,7},{2,4},{3,5},{4,2},{5,3},{6,0},{7,1},{8,14},{9,15},{10,... | collective-permute-start | bytes 589832 | tf_op jit(solution)/shard_map/ppermute | solution.py:480
  120.8 12.6 %collective-permute-start.6 = (f32[12,32,128]{2,1,0:T(8,128)}, f32[12,32,128]{2,1,0:T(8,128)S(1)}, u32[]{:S(2)}, u32[]{:S(2)}) collective-permute-start(f32[12,32,128]{2,1,0:T(8,128)} %get-tuple-element.40), channel_id=1, source_target_pairs={{0,7},{1,6},{2,5},{3,4},{4,3},{5,2},{6,1},{7,0},{8,15},{9,14},{10,... | collective-permute-start | bytes 589832 | tf_op jit(solution)/shard_map/ppermute | solution.py:480
  133.4 0.9 copy-start.4
  139.9 10.0 %collective-permute-start.10 = (f32[6,32,128]{2,1,0:T(8,128)}, f32[6,32,128]{2,1,0:T(8,128)S(1)}, u32[]{:S(2)}, u32[]{:S(2)}) collective-permute-start(f32[6,32,128]{2,1,0:T(8,128)} %get-tuple-element.45), channel_id=1, source_target_pairs={{0,4},{1,5},{2,6},{3,7},{4,0},{5,1},{6,2},{7,3},{8,12},{9,13},{10,... | collective-permute-start | bytes 294920 | tf_op jit(solution)/shard_map/ppermute | solution.py:480
  140.5 10.3 %collective-permute-start.11 = (f32[6,32,128]{2,1,0:T(8,128)}, f32[6,32,128]{2,1,0:T(8,128)S(1)}, u32[]{:S(2)}, u32[]{:S(2)}) collective-permute-start(f32[6,32,128]{2,1,0:T(8,128)} %get-tuple-element.46), channel_id=1, source_target_pairs={{0,5},{1,4},{2,7},{3,6},{4,1},{5,0},{6,3},{7,2},{8,13},{9,12},{10,... | collective-permute-start | bytes 294920 | tf_op jit(solution)/shard_map/ppermute | solution.py:480
  144.6 8.7 %collective-permute-start.12 = (f32[6,32,128]{2,1,0:T(8,128)}, f32[6,32,128]{2,1,0:T(8,128)S(1)}, u32[]{:S(2)}, u32[]{:S(2)}) collective-permute-start(f32[6,32,128]{2,1,0:T(8,128)} %get-tuple-element.47), channel_id=1, source_target_pairs={{0,6},{1,7},{2,4},{3,5},{4,2},{5,3},{6,0},{7,1},{8,14},{9,15},{10,... | collective-permute-start | bytes 294920 | tf_op jit(solution)/shard_map/ppermute | solution.py:480
  147.2 8.2 %collective-permute-start.13 = (f32[6,32,128]{2,1,0:T(8,128)}, f32[6,32,128]{2,1,0:T(8,128)S(1)}, u32[]{:S(2)}, u32[]{:S(2)}) collective-permute-start(f32[6,32,128]{2,1,0:T(8,128)} %get-tuple-element.48), channel_id=1, source_target_pairs={{0,7},{1,6},{2,5},{3,4},{4,3},{5,2},{6,1},{7,0},{8,15},{9,14},{10,... | collective-permute-start | bytes 294920 | tf_op jit(solution)/shard_map/ppermute | solution.py:480
  147.9 7.4 %collective-permute-start.7 = (f32[6,32,128]{2,1,0:T(8,128)}, f32[6,32,128]{2,1,0:T(8,128)S(1)}, u32[]{:S(2)}, u32[]{:S(2)}) collective-permute-start(f32[6,32,128]{2,1,0:T(8,128)} %get-tuple-element.42), channel_id=1, source_target_pairs={{0,1},{1,0},{2,3},{3,2},{4,5},{5,4},{6,7},{7,6},{8,9},{9,8},{10,11... | collective-permute-start | bytes 294920 | tf_op jit(solution)/shard_map/ppermute | solution.py:480
  149.9 5.4 %collective-permute-start.8 = (f32[6,32,128]{2,1,0:T(8,128)}, f32[6,32,128]{2,1,0:T(8,128)S(1)}, u32[]{:S(2)}, u32[]{:S(2)}) collective-permute-start(f32[6,32,128]{2,1,0:T(8,128)} %get-tuple-element.43), channel_id=1, source_target_pairs={{0,2},{1,3},{2,0},{3,1},{4,6},{5,7},{6,4},{7,5},{8,10},{9,11},{10,... | collective-permute-start | bytes 294920 | tf_op jit(solution)/shard_map/ppermute | solution.py:480
  150.8 6.4 %collective-permute-start.9 = (f32[6,32,128]{2,1,0:T(8,128)}, f32[6,32,128]{2,1,0:T(8,128)S(1)}, u32[]{:S(2)}, u32[]{:S(2)}) collective-permute-start(f32[6,32,128]{2,1,0:T(8,128)} %get-tuple-element.44), channel_id=1, source_target_pairs={{0,3},{1,2},{2,1},{3,0},{4,7},{5,6},{6,5},{7,4},{8,11},{9,10},{10,... | collective-permute-start | bytes 294920 | tf_op jit(solution)/shard_map/ppermute | solution.py:480
  157.2 0.9 copy-start.5
  160.4 38.2 %all-to-all-start.1 = ((f32[32,6,8,128]{3,2,1,0:T(8,128)}), f32[32,6,8,128]{3,2,1,0:T(8,128)S(1)}, u32[]{:S(2)}, u32[]{:S(2)}) async-start(f32[32,6,8,128]{3,2,1,0:T(8,128)} %x_backward.2), calls=%async_computation.1 | async-start | bytes 1572864 | tf_op jit(solution)/shard_map/all_to_all | solution.py:476
  177.0 8.9 %collective-permute-start.14 = (f32[6,32,128]{2,1,0:T(8,128)}, f32[6,32,128]{2,1,0:T(8,128)S(1)}, u32[]{:S(2)}, u32[]{:S(2)}) collective-permute-start(f32[6,32,128]{2,1,0:T(8,128)} %get-tuple-element.51), channel_id=1, source_target_pairs={{0,1},{1,0},{2,3},{3,2},{4,5},{5,4},{6,7},{7,6},{8,9},{9,8},{10,11... | collective-permute-start | bytes 294920 | tf_op jit(solution)/shard_map/ppermute | solution.py:480
  178.6 8.4 %collective-permute-start.15 = (f32[6,32,128]{2,1,0:T(8,128)}, f32[6,32,128]{2,1,0:T(8,128)S(1)}, u32[]{:S(2)}, u32[]{:S(2)}) collective-permute-start(f32[6,32,128]{2,1,0:T(8,128)} %get-tuple-element.52), channel_id=1, source_target_pairs={{0,2},{1,3},{2,0},{3,1},{4,6},{5,7},{6,4},{7,5},{8,10},{9,11},{10,... | collective-permute-start | bytes 294920 | tf_op jit(solution)/shard_map/ppermute | solution.py:480
  180.6 9.6 %collective-permute-start.16 = (f32[6,32,128]{2,1,0:T(8,128)}, f32[6,32,128]{2,1,0:T(8,128)S(1)}, u32[]{:S(2)}, u32[]{:S(2)}) collective-permute-start(f32[6,32,128]{2,1,0:T(8,128)} %get-tuple-element.53), channel_id=1, source_target_pairs={{0,3},{1,2},{2,1},{3,0},{4,7},{5,6},{6,5},{7,4},{8,11},{9,10},{10,... | collective-permute-start | bytes 294920 | tf_op jit(solution)/shard_map/ppermute | solution.py:480
  181.4 8.8 %collective-permute-start.17 = (f32[6,32,128]{2,1,0:T(8,128)}, f32[6,32,128]{2,1,0:T(8,128)S(1)}, u32[]{:S(2)}, u32[]{:S(2)}) collective-permute-start(f32[6,32,128]{2,1,0:T(8,128)} %get-tuple-element.54), channel_id=1, source_target_pairs={{0,4},{1,5},{2,6},{3,7},{4,0},{5,1},{6,2},{7,3},{8,12},{9,13},{10,... | collective-permute-start | bytes 294920 | tf_op jit(solution)/shard_map/ppermute | solution.py:480
  185.1 9.2 %collective-permute-start.18 = (f32[6,32,128]{2,1,0:T(8,128)}, f32[6,32,128]{2,1,0:T(8,128)S(1)}, u32[]{:S(2)}, u32[]{:S(2)}) collective-permute-start(f32[6,32,128]{2,1,0:T(8,128)} %get-tuple-element.55), channel_id=1, source_target_pairs={{0,5},{1,4},{2,7},{3,6},{4,1},{5,0},{6,3},{7,2},{8,13},{9,12},{10,... | collective-permute-start | bytes 294920 | tf_op jit(solution)/shard_map/ppermute | solution.py:480
  186.0 8.3 %collective-permute-start.19 = (f32[6,32,128]{2,1,0:T(8,128)}, f32[6,32,128]{2,1,0:T(8,128)S(1)}, u32[]{:S(2)}, u32[]{:S(2)}) collective-permute-start(f32[6,32,128]{2,1,0:T(8,128)} %get-tuple-element.56), channel_id=1, source_target_pairs={{0,6},{1,7},{2,4},{3,5},{4,2},{5,3},{6,0},{7,1},{8,14},{9,15},{10,... | collective-permute-start | bytes 294920 | tf_op jit(solution)/shard_map/ppermute | solution.py:480
  186.9 8.4 %collective-permute-start.20 = (f32[6,32,128]{2,1,0:T(8,128)}, f32[6,32,128]{2,1,0:T(8,128)S(1)}, u32[]{:S(2)}, u32[]{:S(2)}) collective-permute-start(f32[6,32,128]{2,1,0:T(8,128)} %get-tuple-element.57), channel_id=1, source_target_pairs={{0,7},{1,6},{2,5},{3,4},{4,3},{5,2},{6,1},{7,0},{8,15},{9,14},{10,... | collective-permute-start | bytes 294920 | tf_op jit(solution)/shard_map/ppermute | solution.py:480
  195.4 0.9 copy-start.6
  196.3 14.3 %copy-start.7 = (s32[8,32,2]{1,2,0:T(2,128)S(1)}, s32[8,32,2]{1,2,0:T(2,128)}, u32[]{:S(2)}) copy-start(s32[8,32,2]{1,2,0:T(2,128)} %param.18) | copy-start | bytes 6148
  196.3 14.6 %copy-start.8 = (s32[8,32]{1,0:T(8,128)S(1)}, s32[8,32]{1,0:T(8,128)}, u32[]{:S(2)}) copy-start(s32[8,32]{1,0:T(8,128)} %param.17) | copy-start | bytes 3076
  198.6 0.9 copy-start.2
  199.5 33.5 %all-to-all-start.4 = ((f32[32,6,8,128]{3,2,1,0:T(8,128)}), f32[32,6,8,128]{3,2,1,0:T(8,128)S(1)}, u32[]{:S(2)}, u32[]{:S(2)}) async-start(f32[32,6,8,128]{3,2,1,0:T(8,128)} %x_backward.3), calls=%async_computation.4 | async-start | bytes 1572864 | tf_op jit(solution)/shard_map/all_to_all | solution.py:476
  211.0 1.1 copy-start.3

commit v3 on v2

--- a/solution.py
+++ b/solution.py
@@ -128,26 +128,38 @@
     ]
 
 
-def y_forward(velocities, first):
+def y_forward(velocities, first, compact):
     count = len(velocities)
     stride = 5 * count * LX
 
     def kernel(*refs):
         sources, first_ref, out_ref = refs[:count], refs[count], refs[count + 1]
+
+        def one(source, rows, fields):
+            high, low = halves(source.reshape(LX * LZ, NY))
+            result = dot_nt(three(first_ref[0:rows]), jnp.concatenate([high, low, high], 1))
+            for part, field in enumerate(fields):
+                for quad in range(2):
+                    tiles = [
+                        result[part * NY + q * GX : part * NY + (q + 1) * GX, quad * 128 : (quad + 1) * 128]
+                        for q in range(QY)
+                    ]
+                    for s, tile in enumerate(swap_strips(tiles)):
+                        out_ref[pl.ds(field * LX + quad * 4 + s, GX, stride=stride), :] = tile
+
         for v in range(count):
-            for comp in range(3):
-                rows = NY if comp == 1 else 2 * NY
-                high, low = halves(sources[v][comp].reshape(LX * LZ, NY))
-                result = dot_nt(three(first_ref[0:rows]), jnp.concatenate([high, low, high], 1))
-                for part in range(rows // NY):
-                    field = 5 * v + (comp if part == 0 else 3 + comp // 2)
-                    for quad in range(2):
-                        tiles = [
-                            result[part * NY + q * GX : part * NY + (q + 1) * GX, quad * 128 : (quad + 1) * 128]
-                            for q in range(QY)
-                        ]
-                        for s, tile in enumerate(swap_strips(tiles)):
-                            out_ref[pl.ds(field * LX + quad * 4 + s, GX, stride=stride), :] = tile
+
+            if compact:
+
+                @pl.loop(0, 2)
+                def _(i):
+                    one(sources[v][2 * i], 2 * NY, (5 * v + 2 * i, 5 * v + 3 + i))
+
+            else:
+                for i in range(2):
+                    one(sources[v][2 * i], 2 * NY, (5 * v + 2 * i, 5 * v + 3 + i))
+
+            one(sources[v][1], NY, (5 * v + 1,))
 
     out = pl.pallas_call(
         kernel,
@@ -368,108 +380,137 @@
 
 
 PAD = 8
-
-
-def y_backward(received, velocities, gain, keep, y_back):
+LINES = LX * LZ
+
+
+def split_inverse(tau_inverse):
+    def kernel(in_ref, out_ref):
+        @pl.loop(0, LZ, unroll=4)
+        def _(m):
+            high, low = halves(in_ref[0, m])
+            out_ref[0, m] = jnp.concatenate([high, low], 0)
+
+    return pl.pallas_call(
+        kernel,
+        name="split_inverse",
+        grid=(LX,),
+        in_specs=[pl.BlockSpec((1, LZ, HALF, NY), lambda i: (i, 0, 0, 0))],
+        out_specs=pl.BlockSpec((1, LZ, 2 * HALF, NY), lambda i: (i, 0, 0, 0)),
+        out_shape=jax.ShapeDtypeStruct((LX, LZ, 2 * HALF, NY), BF16),
+        compiler_params=pltpu.CompilerParams(dimension_semantics=("arbitrary",)),
+    )(tau_inverse).reshape(LINES, 2 * HALF, NY)
+
+
+def finish(received, velocities, gain, keep, inverse, y_back, spread, compact):
     fields = received.shape[1]
-    lines = LX * LZ
     stride = fields * LX
-
-    def kernel(in_ref, first, second, gain_ref, keep_ref, back_ref, right):
+    blocks = 8
+    block = LINES // blocks
+
+    def kernel(in_ref, first, second, gain_ref, keep_ref, inverse_far, back_far, spread_far, *refs):
         sources = [first, second]
-        for v in range(2):
-            lefts = []
-            for comp in range(3):
-                f = 3 * v + comp
-                quads = []
-                for quad in range(2):
-                    tiles = swap_strips(
-                        [in_ref[pl.ds(f * LX + quad * 4 + s, GX, stride=stride), :] for s in range(4)]
-                    )
-                    quads.append(jnp.concatenate(tiles, 0).T)
-                high, low = halves(jnp.concatenate(quads, 0) * gain_ref[...])
-                own_high, own_low = halves(sources[v][comp].reshape(lines, NY))
-                lefts.append(jnp.concatenate([high, low, high, own_high, own_low], 1))
+        outs = refs[:2]
+        right, even_part, odd_part, inverse_ref, back_ref, spread_ref, block_sems, back_sem, spread_sem = refs[2:]
+
+        def block_copy(b):
+            at = pl.ds(pl.multiple_of(b * block, block), block)
+            return pltpu.make_async_copy(inverse_far.at[at], inverse_ref.at[at], block_sems.at[b])
+
+        back_copy = pltpu.make_async_copy(back_far, back_ref, back_sem)
+        spread_copy = pltpu.make_async_copy(spread_far, spread_ref, spread_sem)
+        back_copy.start()
+        for b in range(blocks):
+            block_copy(b).start()
+        spread_copy.start()
+
+        def lines_of(v, comp):
+            f = 3 * v + comp
+            quads = []
+            for quad in range(2):
+                tiles = swap_strips([in_ref[pl.ds(f * LX + quad * 4 + s, GX, stride=stride), :] for s in range(4)])
+                quads.append(jnp.concatenate(tiles, 0).T)
+            high, low = halves(jnp.concatenate(quads, 0) * gain_ref[...])
+            own_high, own_low = halves(sources[v][comp].reshape(LINES, NY))
+            return jnp.concatenate([high, low, high, own_high, own_low], 1)
+
+        def put(v, comps, lefts):
             high, low, own = back_ref[0:NY], back_ref[NY : 2 * NY], back_ref[2 * NY : 3 * NY]
             result = dot(jnp.concatenate(lefts, 0), jnp.concatenate([high, high, low, own, own], 0))
+            for i, comp in enumerate(comps):
+                line = result[LINES * i : LINES * (i + 1)]
+                right[pl.ds(3 * v + comp, LINES, stride=PAD), :] = jnp.where(keep_ref[...] > 0.5, line, 0.0)
+
+        for v in range(2):
+            if compact:
+                if v == 0:
+                    back_copy.wait()
+
+                @pl.loop(0, 3)
+                def _(comp):
+                    put(v, [comp], [lines_of(v, comp)])
+
+            else:
+                lefts = [lines_of(v, comp) for comp in range(3)]
+                if v == 0:
+                    back_copy.wait()
+                put(v, range(3), lefts)
+        for f in range(fields, PAD):
+            right[pl.ds(f, LINES, stride=PAD), :] = jnp.zeros((LINES, NY), F32)
+
+        first_half = lax.broadcasted_iota(jnp.int32, (PAD, NY), 1) < HALF
+        zero = jnp.zeros((4 * PAD, NY), BF16)
+
+        @pl.loop(0, blocks)
+        def _(b):
+            block_copy(b).wait()
+
+            @pl.loop(0, block // 2, unroll=4 if compact else 16)
+            def _(step):
+                k = b * (block // 2) + step
+                lefts = []
+                for i in range(2):
+                    line = right[pl.ds(pl.multiple_of((2 * k + i) * PAD, PAD), PAD), :]
+                    both = jnp.concatenate([jnp.where(first_half, line, 0.0), jnp.where(first_half, 0.0, line)], 0)
+                    lefts.append(jnp.concatenate(halves(both), 0))
+                left = jnp.concatenate(
+                    [jnp.concatenate([lefts[0], zero], 1), jnp.concatenate([zero, lefts[1]], 1)], 0
+                )
+                weights = jnp.concatenate([inverse_ref[2 * k], inverse_ref[2 * k + 1]], 1)
+                result = dot_nt(left, weights)
+                for i in range(2):
+                    piece = result[4 * PAD * i : 4 * PAD * (i + 1)]
+                    piece = piece[: 2 * PAD] + piece[2 * PAD :]
+                    at = pl.ds(pl.multiple_of((2 * k + i) * PAD, PAD), PAD)
+                    even_part[at, :] = piece[:PAD]
+                    odd_part[at, :] = piece[PAD:]
+
+        spread_copy.wait()
+        for v in range(2):
+            highs, lows = [], []
             for comp in range(3):
-                line = result[lines * comp : lines * (comp + 1)]
-                right[pl.ds(3 * v + comp, lines, stride=PAD), :] = jnp.where(keep_ref[...] > 0.5, line, 0.0)
-
-        for f in range(fields, PAD):
-            right[pl.ds(f, lines, stride=PAD), :] = jnp.zeros((lines, NY), F32)
+                at = pl.ds(3 * v + comp, LINES, stride=PAD)
+                high0, low0 = halves(even_part[at, :])
+                high1, low1 = halves(odd_part[at, :])
+                highs.append(jnp.concatenate([high0, high1], 1))
+                lows.append(jnp.concatenate([low0, low1], 1))
+            result = dot(jnp.concatenate(highs + lows, 0), spread_ref[...])
+            for comp in range(3):
+                value = result[LINES * comp : LINES * (comp + 1)] + result[LINES * (3 + comp) : LINES * (4 + comp)]
+                outs[v][comp] = value.reshape(LX, LZ, NY)
 
     vmem = pl.BlockSpec(memory_space=pltpu.VMEM)
+    far = pl.BlockSpec(memory_space=pltpu.HBM)
+    operands = (received.reshape(GX * stride, 128), *velocities, gain, keep)
     return pl.pallas_call(
         kernel,
-        name="y_backward",
-        in_specs=[vmem] * 6,
-        out_shape=jax.ShapeDtypeStruct((lines * PAD, NY), F32),
-    )(near(received.reshape(GX * stride, 128)), *velocities, near(gain), near(keep), y_back)
-
-
-def solve(first, second, tau_inverse, spread):
-    pad = 2 * PAD
-
-    def kernel(first_ref, second_ref, tau_ref, spread_ref, *refs):
-        outs = refs[:4]
-        solved, solved_odd = refs[4:]
-        lane = lax.broadcasted_iota(jnp.int32, (pad, NY), 1)
-        first_half = lane < HALF
-        zero = jnp.zeros((4 * pad, NY), BF16)
-
-        def pair(k, carry):
-            weights = []
-            lefts = []
-            for i in range(2):
-                mode = 2 * k + i
-                high, low = halves(tau_ref[0, mode])
-                weights.append(jnp.concatenate([high, low], 0))
-                at = pl.ds(pl.multiple_of(mode * PAD, PAD), PAD)
-                line = jnp.concatenate([first_ref[at, :], second_ref[at, :]], 0)
-                even = halves(jnp.where(first_half, line, 0.0))
-                odd = halves(jnp.where(first_half, 0.0, line))
-                lefts.append(jnp.concatenate([even[0], odd[0], even[1], odd[1]], 0))
-            left = jnp.concatenate(
-                [jnp.concatenate([lefts[0], zero], 1), jnp.concatenate([zero, lefts[1]], 1)], 0
-            )
-            result = dot_nt(left, jnp.concatenate(weights, 1))
-            for i in range(2):
-                piece = result[4 * pad * i : 4 * pad * (i + 1)]
-                piece = piece[: 2 * pad] + piece[2 * pad :]
-                at = pl.ds(pl.multiple_of((2 * k + i) * pad, pad), pad)
-                solved[at, :] = piece[:pad]
-                solved_odd[at, :] = piece[pad:]
-            return carry
-
-        lax.fori_loop(0, LZ // 2, pair, 0, unroll=8)
-
-        highs, lows = [], []
-        for f in range(12):
-            row = f if f < 6 else f + PAD - 6
-            high0, low0 = halves(solved[pl.ds(row, LZ, stride=pad), :])
-            high1, low1 = halves(solved_odd[pl.ds(row, LZ, stride=pad), :])
-            highs.append(jnp.concatenate([high0, high1], 1))
-            lows.append(jnp.concatenate([low0, low1], 1))
-        result = dot(jnp.concatenate(highs + lows, 0), spread_ref[...])
-        for f in range(12):
-            outs[f // 3][f % 3, 0] = result[LZ * f : LZ * (f + 1)] + result[LZ * (12 + f) : LZ * (13 + f)]
-
-    return pl.pallas_call(
-        kernel,
-        name="solve",
-        grid=(LX,),
-        in_specs=[
-            pl.BlockSpec((LZ * PAD, NY), lambda i: (i, 0)),
-            pl.BlockSpec((LZ * PAD, NY), lambda i: (i, 0)),
-            pl.BlockSpec((1, LZ, HALF, NY), lambda i: (i, 0, 0, 0)),
-            pl.BlockSpec((2 * NY, NY), lambda i: (0, 0)),
-        ],
-        out_specs=[pl.BlockSpec((3, 1, LZ, NY), lambda i: (0, i, 0, 0)) for _ in range(4)],
-        out_shape=[jax.ShapeDtypeStruct((3, LX, LZ, NY), F32) for _ in range(4)],
-        scratch_shapes=[pltpu.VMEM((LZ * pad, NY), F32), pltpu.VMEM((LZ * pad, NY), F32)],
-        compiler_params=pltpu.CompilerParams(dimension_semantics=("arbitrary",)),
-    )(first, second, tau_inverse, spread)
+        name="finish",
+        in_specs=[vmem] * 5 + [far] * 3,
+        out_shape=[jax.ShapeDtypeStruct((3, LX, LZ, NY), F32) for _ in range(2)],
+        scratch_shapes=[pltpu.VMEM((LINES * PAD, NY), F32) for _ in range(3)]
+        + [pltpu.VMEM(a.shape, a.dtype) for a in (inverse, y_back, spread)]
+        + [pltpu.SemaphoreType.DMA((blocks,)), pltpu.SemaphoreType.DMA, pltpu.SemaphoreType.DMA],
+        compiler_params=pltpu.CompilerParams(vmem_limit_bytes=44 * 1024 * 1024),
+    )(*[near(a) for a in operands], *[pltpu.with_memory_space_constraint(a, pltpu.HBM) for a in (inverse, y_back, spread)])
 
 
 def exchange(array, axis):
@@ -488,9 +529,10 @@
     gain = jnp.broadcast_to((step_gain * dealias_mask.astype(F32)).reshape(LX * LZ, 1), (LX * LZ, NY))
     rows = tau_rows.reshape(LX * LZ, 2)[:, :, None]
     keep = (jnp.arange(HALF, dtype=jnp.int32) != rows).astype(F32).reshape(LX * LZ, NY)
-    sent_one = y_forward(one, table["y_first"])
+    sent_one = y_forward(one, table["y_first"], False)
     whole_one = exchange(sent_one, "px")
-    sent_two = y_forward(two, table["y_first"])
+    sent_two = y_forward(two, table["y_first"], True)
+    inverse = split_inverse(tau_inverse)
     whole_two = exchange(sent_two, "px")
     parts_one = x_forward(whole_one, table["value"], table["x_slope"], position)
     lines_one = exchange_parts(parts_one)
@@ -506,9 +548,8 @@
     mixed_two = exchange_parts(back_two)
     modes_two = x_backward(mixed_two, table["value"], position)
     nodes_two = exchange(modes_two, "px")
-    right_one = y_backward(nodes_one, one, gain, keep, table["y_back"])
-    right_two = y_backward(nodes_two, two, gain, keep, table["y_back"])
-    outs = solve(right_one, right_two, tau_inverse, table["spread"])
+    outs = finish(nodes_one, one, gain, keep, inverse, table["y_back"], table["spread"], True)
+    outs += finish(nodes_two, two, gain, keep, inverse, table["y_back"], table["spread"], False)
     return (outs[0], outs[1], outs[2].reshape(tangent.shape), outs[3].reshape(second.shape))
 
 

time: 249 us -> 246 us (0.988)
  Pallas kernels: 47.8 us -> 64 us
  waiting for transfers between devices: 108 us -> 93.3 us
    all_to_all x5, waiting for transfers between devices: 77.9 us -> 60.6 us  [exchange(): return lax.all_to_all(array, axis, split_axis=0, concat_axis=0, tiled=True)]
    pallas_call x3, Pallas kernels: 18.2 us -> 33.1 us  [the longest x2 23.7 us: finish(): pl.pallas_call(kernel, name='finish', in_specs=[vmem] * 5 + [far] * 3, ou...]
    unnamed x19 -> x23, local copies, waits for them, and re-layouts: 7.14 us -> 5.12 us
  transfers between devices with their start and end apart: 26 -> 26, of which waited for: 11 -> 11; matrix products, arithmetic and copies ran while one was open for 0% -> 0% of each run, Pallas kernels for 12% -> 20%
where the time goes in v3:
time: 246 us; the launch traced here: 245 us
  waiting for transfers between devices  93.3 us (38%)
  starting transfers between devices  81.4 us (33%)
  Pallas kernels  64 us (26%)
  local copies, waits for them, and re-layouts  5.55 us (2%)
    all_to_all x5, waiting for transfers between devices, exchange(): return lax.all_to_all(array, axis, split_axis=0, concat_axis=0, tiled=True)  60.6 us
    all_to_all x5, starting transfers between devices, exchange(): return lax.all_to_all(array, axis, split_axis=0, concat_axis=0, tiled=True)  44 us
    ppermute x21, starting transfers between devices, exchange_parts(): lax.ppermute(parts[k], 'pz', [(i, i ^ k) for i in range(GZ)])  37.4 us
    ppermute x21, waiting for transfers between devices, exchange_parts(): lax.ppermute(parts[k], 'pz', [(i, i ^ k) for i in range(GZ)])  32.7 us
    pallas_call x2, Pallas kernels, finish(): pl.pallas_call(kernel, name='finish', in_specs=[vmem] * 5 + [far] * 3, ou...  23.7 us
    pallas_call x2, Pallas kernels, z_stage(): pl.pallas_call(kernel, name='z_stage_first' if keep else 'z_stage_second'...  11.3 us
    pallas_call x1, Pallas kernels, split_inverse(): pl.pallas_call(kernel, name='split_inverse', grid=(LX,), in_specs=[pl.Blo...  9.35 us
    pallas_call x2, Pallas kernels, y_forward(): pl.pallas_call(kernel, name='y_forward', out_shape=jax.ShapeDtypeStruct((...  8.1 us
  transfers between devices with their start and end apart: 26, of which 11 were waited for; matrix products, arithmetic and copies ran while one was open for 0% of the time, Pallas kernels for 20%

profile of v3, /device:TPU:1, one launch (start us, length us, event | category | flops | bytes accessed | tf_op | source)
XLA Modules:
  0.0 245.2 jit_solution(5396791415886259851)
XLA Ops:
  0.6 4.7 %y_forward.3 = f32[2560,128]{1,0:T(8,128)} custom-call(f32[3,8,32,128]{3,2,1,0:T(8,128)} %bitcast.15, f32[3,8,32,128]{3,2,1,0:T(8,128)} %bitcast.17, bf16[256,256]{1,0:T(8,128)(2,1)} %constant.18.clone.refs_2_), custom_call_target="tpu_custom_call" | custom-call | tf_op jit(solution)/shard_map/y_forward/pallas_call | solution.py:164
  5.3 11.0 %all-to-all-start.2 = ((f32[32,10,8,128]{3,2,1,0:T(8,128)}), f32[32,10,8,128]{3,2,1,0:T(8,128)S(1)}, u32[]{:S(2)}, u32[]{:S(2)}) async-start(f32[32,10,8,128]{3,2,1,0:T(8,128)} %bitcast.22), calls=%async_computation.2 | async-start | bytes 2621440 | tf_op jit(solution)/shard_map/all_to_all | solution.py:517
  16.4 3.4 %y_forward.2 = f32[2560,128]{1,0:T(8,128)} custom-call(f32[3,8,32,128]{3,2,1,0:T(8,128)} %first.1, f32[3,8,32,128]{3,2,1,0:T(8,128)} %second.1, bf16[256,256]{1,0:T(8,128)(2,1)} %constant.18.clone.refs_2_), custom_call_target="tpu_custom_call" | custom-call | tf_op jit(solution)/shard_map/y_forward/pallas_call | solution.py:164
  19.8 30.3 %all-to-all-done.2.refs_0_ = f32[32,10,8,128]{3,2,1,0:T(8,128)S(1)} async-done(((f32[32,10,8,128]{3,2,1,0:T(8,128)}), f32[32,10,8,128]{3,2,1,0:T(8,128)S(1)}, u32[]{:S(2)}, u32[]{:S(2)}) %all-to-all-start.2) | async-done | bytes 1310752 | tf_op jit(solution)/shard_map/all_to_all | solution.py:517
  50.1 4.3 %all-to-all-start = ((f32[32,10,8,128]{3,2,1,0:T(8,128)}), f32[32,10,8,128]{3,2,1,0:T(8,128)S(1)}, u32[]{:S(2)}, u32[]{:S(2)}) async-start(f32[32,10,8,128]{3,2,1,0:T(8,128)} %bitcast.21), calls=%async_computation | async-start | bytes 2621440 | tf_op jit(solution)/shard_map/all_to_all | solution.py:517
  54.4 3.4 %x_forward.1 = f32[8,12,32,128]{3,2,1,0:T(8,128)} custom-call(f32[32,10,8,128]{3,2,1,0:T(8,128)S(1)} %all-to-all-done.2.refs_0_, bf16[256,512]{1,0:T(8,128)(2,1)} %constant.19.clone.refs_2_.refs_9_.refs_1_, bf16[256,512]{1,0:T(8,128)(2,1)} %constant.20.clone.refs_3_.refs_2_), custom_call_target="tpu_custom_call" | custom-call | tf_op jit(solution)/shard_map/x_forward/pallas_call | solution.py:224
  57.8 30.3 %all-to-all-done.refs_1_ = f32[32,10,8,128]{3,2,1,0:T(8,128)S(1)} async-done(((f32[32,10,8,128]{3,2,1,0:T(8,128)}), f32[32,10,8,128]{3,2,1,0:T(8,128)S(1)}, u32[]{:S(2)}, u32[]{:S(2)}) %all-to-all-start) | async-done | bytes 1310752 | tf_op jit(solution)/shard_map/all_to_all | solution.py:517
  88.1 1.1 copy-done
  89.1 6.4 %all-to-all-start.3 = ((f32[8,12,32,128]{3,2,1,0:T(8,128)}), f32[8,12,32,128]{3,2,1,0:T(8,128)S(1)}, u32[]{:S(2)}, u32[]{:S(2)}) async-start(f32[8,12,32,128]{3,2,1,0:T(8,128)} %x_forward.1), calls=%async_computation.3 | async-start | bytes 3145728 | tf_op jit(solution)/shard_map/all_to_all | solution.py:517
  95.5 1.3 copy-done.1
  96.8 3.3 %x_forward_parts.1 = (f32[12,32,128]{2,1,0:T(8,128)}, f32[12,32,128]{2,1,0:T(8,128)}, f32[12,32,128]{2,1,0:T(8,128)}, f32[12,32,128]{2,1,0:T(8,128)}, f32[12,32,...) custom-call(s32[1]{0:T(128)} %bitcast.refs_0_, ...), custom_call_target="tpu_custom_call" | custom-call | tf_op jit(solution)/shard_map/x_forward_parts/pallas_call | solution.py:217
  100.1 3.0 %collective-permute-start = (f32[12,32,128]{2,1,0:T(8,128)}, f32[12,32,128]{2,1,0:T(8,128)S(1)}, u32[]{:S(2)}, u32[]{:S(2)}) collective-permute-start(f32[12,32,128]{2,1,0:T(8,128)} %get-tuple-element.34), channel_id=1, source_target_pairs={{0,1},{1,0},{2,3},{3,2},{4,5},{5,4},{6,7},{7,6},{8,9},{9,8},{10,11... | collective-permute-start | bytes 589832 | tf_op jit(solution)/shard_map/ppermute | solution.py:521
  103.1 1.2 collective-permute-start.1
  104.3 3.0 %collective-permute-start.3 = (f32[12,32,128]{2,1,0:T(8,128)}, f32[12,32,128]{2,1,0:T(8,128)S(1)}, u32[]{:S(2)}, u32[]{:S(2)}) collective-permute-start(f32[12,32,128]{2,1,0:T(8,128)} %get-tuple-element.37), channel_id=1, source_target_pairs={{0,4},{1,5},{2,6},{3,7},{4,0},{5,1},{6,2},{7,3},{8,12},{9,13},{10,... | collective-permute-start | bytes 589832 | tf_op jit(solution)/shard_map/ppermute | solution.py:521
  107.3 2.7 %collective-permute-start.4 = (f32[12,32,128]{2,1,0:T(8,128)}, f32[12,32,128]{2,1,0:T(8,128)S(1)}, u32[]{:S(2)}, u32[]{:S(2)}) collective-permute-start(f32[12,32,128]{2,1,0:T(8,128)} %get-tuple-element.38), channel_id=1, source_target_pairs={{0,5},{1,4},{2,7},{3,6},{4,1},{5,0},{6,3},{7,2},{8,13},{9,12},{10,... | collective-permute-start | bytes 589832 | tf_op jit(solution)/shard_map/ppermute | solution.py:521
  110.0 9.7 %collective-permute-done.refs_2_ = f32[12,32,128]{2,1,0:T(8,128)S(1)} collective-permute-done((f32[12,32,128]{2,1,0:T(8,128)}, f32[12,32,128]{2,1,0:T(8,128)S(1)}, u32[]{:S(2)}, u32[]{:S(2)}) %collective-permute-start) | collective-permute-done | bytes 196640 | tf_op jit(solution)/shard_map/ppermute | solution.py:521
  119.7 2.4 collective-permute-start.5
  122.1 0.0 collective-permute-done.1.refs_3_
  122.1 0.8 collective-permute-start.6
  122.9 1.9 collective-permute-done.2.refs_4_
  124.8 7.9 %collective-permute-done.3.refs_5_ = f32[12,32,128]{2,1,0:T(8,128)S(1)} collective-permute-done((f32[12,32,128]{2,1,0:T(8,128)}, f32[12,32,128]{2,1,0:T(8,128)S(1)}, u32[]{:S(2)}, u32[]{:S(2)}) %collective-permute-start.3) | collective-permute-done | bytes 196640 | tf_op jit(solution)/shard_map/ppermute | solution.py:521
  132.7 0.0 collective-permute-done.5.refs_7_
  132.7 2.0 collective-permute-done.6.refs_8_
  134.7 0.9 copy-done.6
  135.6 5.6 %z_stage_first.1 = (f32[6,32,128]{2,1,0:T(8,128)}, f32[6,32,128]{2,1,0:T(8,128)}, f32[6,32,128]{2,1,0:T(8,128)}, f32[6,32,128]{2,1,0:T(8,128)}, f32[6,32,128]{2,...) custom-call(s32[1]{0:T(128)} %bitcast.refs_0_, ...), custom_call_target="tpu_custom_call" | custom-call | tf_op jit(solution)/shard_map/z_stage_first/pallas_call | solution.py:344
  141.2 2.0 collective-permute-start.7
  143.1 2.0 collective-permute-start.8
  145.2 0.1 collective-permute-start.9
  145.3 1.6 collective-permute-start.10
  147.0 3.6 %collective-permute-start.11 = (f32[6,32,128]{2,1,0:T(8,128)}, f32[6,32,128]{2,1,0:T(8,128)S(1)}, u32[]{:S(2)}, u32[]{:S(2)}) collective-permute-start(f32[6,32,128]{2,1,0:T(8,128)} %get-tuple-element.46), channel_id=1, source_target_pairs={{0,5},{1,4},{2,7},{3,6},{4,1},{5,0},{6,3},{7,2},{8,13},{9,12},{10,... | collective-permute-start | bytes 294920 | tf_op jit(solution)/shard_map/ppermute | solution.py:521
  150.6 0.0 collective-permute-done.7.refs_2_
  150.6 2.1 collective-permute-start.12
  152.6 0.7 collective-permute-start.13
  153.4 1.3 collective-permute-done.11.refs_6_
  154.7 1.7 collective-permute-done.12.refs_7_
  156.4 4.1 %collective-permute-done.13.refs_8_ = f32[6,32,128]{2,1,0:T(8,128)S(1)} collective-permute-done((f32[6,32,128]{2,1,0:T(8,128)}, f32[6,32,128]{2,1,0:T(8,128)S(1)}, u32[]{:S(2)}, u32[]{:S(2)}) %collective-permute-start.13) | collective-permute-done | bytes 98336 | tf_op jit(solution)/shard_map/ppermute | solution.py:521
  160.5 0.9 copy-done.7
  161.4 2.4 x_backward.2
  163.7 0.0 all-to-all-done.3.refs_1_
  163.7 11.6 %all-to-all-start.1 = ((f32[32,6,8,128]{3,2,1,0:T(8,128)}), f32[32,6,8,128]{3,2,1,0:T(8,128)S(1)}, u32[]{:S(2)}, u32[]{:S(2)}) async-start(f32[32,6,8,128]{3,2,1,0:T(8,128)} %x_backward.2), calls=%async_computation.1 | async-start | bytes 1572864 | tf_op jit(solution)/shard_map/all_to_all | solution.py:517
  175.3 5.7 %z_stage_second.1 = (f32[6,32,128]{2,1,0:T(8,128)}, f32[6,32,128]{2,1,0:T(8,128)}, f32[6,32,128]{2,1,0:T(8,128)}, f32[6,32,128]{2,1,0:T(8,128)}, f32[6,32,128]{2...) custom-call(s32[1]{0:T(128)} %bitcast.refs_0_, ...), custom_call_target="tpu_custom_call" | custom-call | tf_op jit(solution)/shard_map/z_stage_second/pallas_call | solution.py:344
  181.1 0.1 collective-permute-start.14
  181.2 4.1 %collective-permute-start.16 = (f32[6,32,128]{2,1,0:T(8,128)}, f32[6,32,128]{2,1,0:T(8,128)S(1)}, u32[]{:S(2)}, u32[]{:S(2)}) collective-permute-start(f32[6,32,128]{2,1,0:T(8,128)} %get-tuple-element.55), channel_id=1, source_target_pairs={{0,3},{1,2},{2,1},{3,0},{4,7},{5,6},{6,5},{7,4},{8,11},{9,10},{10,... | collective-permute-start | bytes 294920 | tf_op jit(solution)/shard_map/ppermute | solution.py:521
  185.2 2.8 %collective-permute-start.18 = (f32[6,32,128]{2,1,0:T(8,128)}, f32[6,32,128]{2,1,0:T(8,128)S(1)}, u32[]{:S(2)}, u32[]{:S(2)}) collective-permute-start(f32[6,32,128]{2,1,0:T(8,128)} %get-tuple-element.57), channel_id=1, source_target_pairs={{0,5},{1,4},{2,7},{3,6},{4,1},{5,0},{6,3},{7,2},{8,13},{9,12},{10,... | collective-permute-start | bytes 294920 | tf_op jit(solution)/shard_map/ppermute | solution.py:521
  188.0 0.0 collective-permute-done.14.refs_2_
  188.0 0.6 collective-permute-start.19
  188.7 4.6 %collective-permute-start.20 = (f32[6,32,128]{2,1,0:T(8,128)}, f32[6,32,128]{2,1,0:T(8,128)S(1)}, u32[]{:S(2)}, u32[]{:S(2)}) collective-permute-start(f32[6,32,128]{2,1,0:T(8,128)} %get-tuple-element.59), channel_id=1, source_target_pairs={{0,7},{1,6},{2,5},{3,4},{4,3},{5,2},{6,1},{7,0},{8,15},{9,14},{10,... | collective-permute-start | bytes 294920 | tf_op jit(solution)/shard_map/ppermute | solution.py:521
  193.3 0.7 collective-permute-done.18.refs_6_
  194.0 3.3 %collective-permute-done.19.refs_7_ = f32[6,32,128]{2,1,0:T(8,128)S(1)} collective-permute-done((f32[6,32,128]{2,1,0:T(8,128)}, f32[6,32,128]{2,1,0:T(8,128)S(1)}, u32[]{:S(2)}, u32[]{:S(2)}) %collective-permute-start.19) | collective-permute-done | bytes 98336 | tf_op jit(solution)/shard_map/ppermute | solution.py:521
  197.3 0.9 copy-done.8
  198.2 2.4 x_backward.3
  200.6 10.8 %all-to-all-start.4 = ((f32[32,6,8,128]{3,2,1,0:T(8,128)}), f32[32,6,8,128]{3,2,1,0:T(8,128)S(1)}, u32[]{:S(2)}, u32[]{:S(2)}) async-start(f32[32,6,8,128]{3,2,1,0:T(8,128)} %x_backward.3), calls=%async_computation.4 | async-start | bytes 1572864 | tf_op jit(solution)/shard_map/all_to_all | solution.py:517
  211.4 0.1 ne.23
  211.5 0.1 broadcast_in_dim.8
  211.6 0.1 ne.25
  211.7 0.1 copy.18
  211.8 0.0 copy-start.2
  211.8 0.0 copy-start.3
  211.8 9.4 %split_inverse.1 = bf16[8,32,128,128]{3,2,1,0:T(8,128)(2,1)} custom-call(f32[8,32,64,128]{3,2,1,0:T(8,128)} %in_ref.1), custom_call_target="tpu_custom_call" | custom-call | tf_op jit(solution)/shard_map/split_inverse/pallas_call | solution.py:393
  221.2 0.1 broadcast_in_dim.9.gain_ref
  221.3 0.0 copy-start.4
  221.3 0.0 copy-start.5
  221.3 14.3 %finish.2 = (f32[3,8,32,128]{3,2,1,0:T(8,128)}, f32[3,8,32,128]{3,2,1,0:T(8,128)}) custom-call(f32[1536,128]{1,0:T(8,128)S(1)} %bitcast.13, f32[3,8,32,128]{3,2,1,0:T(8,128)S(1)} %copy-done.2, f32[3,8,32,128]{3,2,1,0:T(8,128)S(1)} %copy-done.3, f32[256,128]{1,0:T(8,128)S(1)} %broadcast_in_dim.9.gain_ref, f32[256,128]{1,0:T(8,128)S(1)} %compare_convert_fusion.keep_ref, ...), custom_call_target="tpu_custom_call" | custom-call | tf_op jit(solution)/shard_map/finish/pallas_call | solution.py:504
  235.7 9.4 %finish.3 = (f32[3,8,32,128]{3,2,1,0:T(8,128)}, f32[3,8,32,128]{3,2,1,0:T(8,128)}) custom-call(f32[1536,128]{1,0:T(8,128)S(1)} %bitcast.14, f32[3,8,32,128]{3,2,1,0:T(8,128)S(1)} %bitcast.16, f32[3,8,32,128]{3,2,1,0:T(8,128)S(1)} %bitcast.18, f32[256,128]{1,0:T(8,128)S(1)} %broadcast_in_dim.9.gain_ref, f32[256,128]{1,0:T(8,128)S(1)} %compare_convert_fusion.keep_ref, ...), custom_call_target="tpu_custom_call" | custom-call | tf_op jit(solution)/shard_map/finish/pallas_call | solution.py:504
  (31 shorter events, 0.1 us)
Async XLA Ops:
  5.3 44.8 %all-to-all-start.2 = ((f32[32,10,8,128]{3,2,1,0:T(8,128)}), f32[32,10,8,128]{3,2,1,0:T(8,128)S(1)}, u32[]{:S(2)}, u32[]{:S(2)}) async-start(f32[32,10,8,128]{3,2,1,0:T(8,128)} %bitcast.22), calls=%async_computation.2 | async-start | bytes 2621440 | tf_op jit(solution)/shard_map/all_to_all | solution.py:517
  50.1 38.0 %all-to-all-start = ((f32[32,10,8,128]{3,2,1,0:T(8,128)}), f32[32,10,8,128]{3,2,1,0:T(8,128)S(1)}, u32[]{:S(2)}, u32[]{:S(2)}) async-start(f32[32,10,8,128]{3,2,1,0:T(8,128)} %bitcast.21), calls=%async_computation | async-start | bytes 2621440 | tf_op jit(solution)/shard_map/all_to_all | solution.py:517
  88.1 1.1 copy-start
  89.1 74.6 %all-to-all-start.3 = ((f32[8,12,32,128]{3,2,1,0:T(8,128)}), f32[8,12,32,128]{3,2,1,0:T(8,128)S(1)}, u32[]{:S(2)}, u32[]{:S(2)}) async-start(f32[8,12,32,128]{3,2,1,0:T(8,128)} %x_forward.1), calls=%async_computation.3 | async-start | bytes 3145728 | tf_op jit(solution)/shard_map/all_to_all | solution.py:517
  95.5 1.3 copy-start.1
  100.1 19.5 %collective-permute-start = (f32[12,32,128]{2,1,0:T(8,128)}, f32[12,32,128]{2,1,0:T(8,128)S(1)}, u32[]{:S(2)}, u32[]{:S(2)}) collective-permute-start(f32[12,32,128]{2,1,0:T(8,128)} %get-tuple-element.34), channel_id=1, source_target_pairs={{0,1},{1,0},{2,3},{3,2},{4,5},{5,4},{6,7},{7,6},{8,9},{9,8},{10,11... | collective-permute-start | bytes 589832 | tf_op jit(solution)/shard_map/ppermute | solution.py:521
  103.1 19.0 %collective-permute-start.1 = (f32[12,32,128]{2,1,0:T(8,128)}, f32[12,32,128]{2,1,0:T(8,128)S(1)}, u32[]{:S(2)}, u32[]{:S(2)}) collective-permute-start(f32[12,32,128]{2,1,0:T(8,128)} %get-tuple-element.35), channel_id=1, source_target_pairs={{0,2},{1,3},{2,0},{3,1},{4,6},{5,7},{6,4},{7,5},{8,10},{9,11},{10,... | collective-permute-start | bytes 589832 | tf_op jit(solution)/shard_map/ppermute | solution.py:521
  104.3 20.5 %collective-permute-start.2 = (f32[12,32,128]{2,1,0:T(8,128)}, f32[12,32,128]{2,1,0:T(8,128)S(1)}, u32[]{:S(2)}, u32[]{:S(2)}) collective-permute-start(f32[12,32,128]{2,1,0:T(8,128)} %get-tuple-element.36), channel_id=1, source_target_pairs={{0,3},{1,2},{2,1},{3,0},{4,7},{5,6},{6,5},{7,4},{8,11},{9,10},{10,... | collective-permute-start | bytes 589832 | tf_op jit(solution)/shard_map/ppermute | solution.py:521
  104.3 28.4 %collective-permute-start.3 = (f32[12,32,128]{2,1,0:T(8,128)}, f32[12,32,128]{2,1,0:T(8,128)S(1)}, u32[]{:S(2)}, u32[]{:S(2)}) collective-permute-start(f32[12,32,128]{2,1,0:T(8,128)} %get-tuple-element.37), channel_id=1, source_target_pairs={{0,4},{1,5},{2,6},{3,7},{4,0},{5,1},{6,2},{7,3},{8,12},{9,13},{10,... | collective-permute-start | bytes 589832 | tf_op jit(solution)/shard_map/ppermute | solution.py:521
  107.3 25.4 %collective-permute-start.4 = (f32[12,32,128]{2,1,0:T(8,128)}, f32[12,32,128]{2,1,0:T(8,128)S(1)}, u32[]{:S(2)}, u32[]{:S(2)}) collective-permute-start(f32[12,32,128]{2,1,0:T(8,128)} %get-tuple-element.38), channel_id=1, source_target_pairs={{0,5},{1,4},{2,7},{3,6},{4,1},{5,0},{6,3},{7,2},{8,13},{9,12},{10,... | collective-permute-start | bytes 589832 | tf_op jit(solution)/shard_map/ppermute | solution.py:521
  119.7 13.0 %collective-permute-start.5 = (f32[12,32,128]{2,1,0:T(8,128)}, f32[12,32,128]{2,1,0:T(8,128)S(1)}, u32[]{:S(2)}, u32[]{:S(2)}) collective-permute-start(f32[12,32,128]{2,1,0:T(8,128)} %get-tuple-element.39), channel_id=1, source_target_pairs={{0,6},{1,7},{2,4},{3,5},{4,2},{5,3},{6,0},{7,1},{8,14},{9,15},{10,... | collective-permute-start | bytes 589832 | tf_op jit(solution)/shard_map/ppermute | solution.py:521
  122.1 12.6 %collective-permute-start.6 = (f32[12,32,128]{2,1,0:T(8,128)}, f32[12,32,128]{2,1,0:T(8,128)S(1)}, u32[]{:S(2)}, u32[]{:S(2)}) collective-permute-start(f32[12,32,128]{2,1,0:T(8,128)} %get-tuple-element.40), channel_id=1, source_target_pairs={{0,7},{1,6},{2,5},{3,4},{4,3},{5,2},{6,1},{7,0},{8,15},{9,14},{10,... | collective-permute-start | bytes 589832 | tf_op jit(solution)/shard_map/ppermute | solution.py:521
  134.6 0.9 copy-start.6
  141.2 9.4 %collective-permute-start.7 = (f32[6,32,128]{2,1,0:T(8,128)}, f32[6,32,128]{2,1,0:T(8,128)S(1)}, u32[]{:S(2)}, u32[]{:S(2)}) collective-permute-start(f32[6,32,128]{2,1,0:T(8,128)} %get-tuple-element.42), channel_id=1, source_target_pairs={{0,1},{1,0},{2,3},{3,2},{4,5},{5,4},{6,7},{7,6},{8,9},{9,8},{10,11... | collective-permute-start | bytes 294920 | tf_op jit(solution)/shard_map/ppermute | solution.py:521
  143.1 9.5 %collective-permute-start.8 = (f32[6,32,128]{2,1,0:T(8,128)}, f32[6,32,128]{2,1,0:T(8,128)S(1)}, u32[]{:S(2)}, u32[]{:S(2)}) collective-permute-start(f32[6,32,128]{2,1,0:T(8,128)} %get-tuple-element.43), channel_id=1, source_target_pairs={{0,2},{1,3},{2,0},{3,1},{4,6},{5,7},{6,4},{7,5},{8,10},{9,11},{10,... | collective-permute-start | bytes 294920 | tf_op jit(solution)/shard_map/ppermute | solution.py:521
  145.2 8.2 %collective-permute-start.9 = (f32[6,32,128]{2,1,0:T(8,128)}, f32[6,32,128]{2,1,0:T(8,128)S(1)}, u32[]{:S(2)}, u32[]{:S(2)}) collective-permute-start(f32[6,32,128]{2,1,0:T(8,128)} %get-tuple-element.44), channel_id=1, source_target_pairs={{0,3},{1,2},{2,1},{3,0},{4,7},{5,6},{6,5},{7,4},{8,11},{9,10},{10,... | collective-permute-start | bytes 294920 | tf_op jit(solution)/shard_map/ppermute | solution.py:521
  145.3 8.1 %collective-permute-start.10 = (f32[6,32,128]{2,1,0:T(8,128)}, f32[6,32,128]{2,1,0:T(8,128)S(1)}, u32[]{:S(2)}, u32[]{:S(2)}) collective-permute-start(f32[6,32,128]{2,1,0:T(8,128)} %get-tuple-element.45), channel_id=1, source_target_pairs={{0,4},{1,5},{2,6},{3,7},{4,0},{5,1},{6,2},{7,3},{8,12},{9,13},{10,... | collective-permute-start | bytes 294920 | tf_op jit(solution)/shard_map/ppermute | solution.py:521
  147.0 7.7 %collective-permute-start.11 = (f32[6,32,128]{2,1,0:T(8,128)}, f32[6,32,128]{2,1,0:T(8,128)S(1)}, u32[]{:S(2)}, u32[]{:S(2)}) collective-permute-start(f32[6,32,128]{2,1,0:T(8,128)} %get-tuple-element.46), channel_id=1, source_target_pairs={{0,5},{1,4},{2,7},{3,6},{4,1},{5,0},{6,3},{7,2},{8,13},{9,12},{10,... | collective-permute-start | bytes 294920 | tf_op jit(solution)/shard_map/ppermute | solution.py:521
  150.6 5.8 %collective-permute-start.12 = (f32[6,32,128]{2,1,0:T(8,128)}, f32[6,32,128]{2,1,0:T(8,128)S(1)}, u32[]{:S(2)}, u32[]{:S(2)}) collective-permute-start(f32[6,32,128]{2,1,0:T(8,128)} %get-tuple-element.47), channel_id=1, source_target_pairs={{0,6},{1,7},{2,4},{3,5},{4,2},{5,3},{6,0},{7,1},{8,14},{9,15},{10,... | collective-permute-start | bytes 294920 | tf_op jit(solution)/shard_map/ppermute | solution.py:521
  152.6 7.9 %collective-permute-start.13 = (f32[6,32,128]{2,1,0:T(8,128)}, f32[6,32,128]{2,1,0:T(8,128)S(1)}, u32[]{:S(2)}, u32[]{:S(2)}) collective-permute-start(f32[6,32,128]{2,1,0:T(8,128)} %get-tuple-element.48), channel_id=1, source_target_pairs={{0,7},{1,6},{2,5},{3,4},{4,3},{5,2},{6,1},{7,0},{8,15},{9,14},{10,... | collective-permute-start | bytes 294920 | tf_op jit(solution)/shard_map/ppermute | solution.py:521
  160.5 0.9 copy-start.7
  163.7 36.9 %all-to-all-start.1 = ((f32[32,6,8,128]{3,2,1,0:T(8,128)}), f32[32,6,8,128]{3,2,1,0:T(8,128)S(1)}, u32[]{:S(2)}, u32[]{:S(2)}) async-start(f32[32,6,8,128]{3,2,1,0:T(8,128)} %x_backward.2), calls=%async_computation.1 | async-start | bytes 1572864 | tf_op jit(solution)/shard_map/all_to_all | solution.py:517
  181.1 7.0 %collective-permute-start.14 = (f32[6,32,128]{2,1,0:T(8,128)}, f32[6,32,128]{2,1,0:T(8,128)S(1)}, u32[]{:S(2)}, u32[]{:S(2)}) collective-permute-start(f32[6,32,128]{2,1,0:T(8,128)} %get-tuple-element.53), channel_id=1, source_target_pairs={{0,1},{1,0},{2,3},{3,2},{4,5},{5,4},{6,7},{7,6},{8,9},{9,8},{10,11... | collective-permute-start | bytes 294920 | tf_op jit(solution)/shard_map/ppermute | solution.py:521
  181.2 7.5 %collective-permute-start.15 = (f32[6,32,128]{2,1,0:T(8,128)}, f32[6,32,128]{2,1,0:T(8,128)S(1)}, u32[]{:S(2)}, u32[]{:S(2)}) collective-permute-start(f32[6,32,128]{2,1,0:T(8,128)} %get-tuple-element.54), channel_id=1, source_target_pairs={{0,2},{1,3},{2,0},{3,1},{4,6},{5,7},{6,4},{7,5},{8,10},{9,11},{10,... | collective-permute-start | bytes 294920 | tf_op jit(solution)/shard_map/ppermute | solution.py:521
  181.2 12.1 %collective-permute-start.16 = (f32[6,32,128]{2,1,0:T(8,128)}, f32[6,32,128]{2,1,0:T(8,128)S(1)}, u32[]{:S(2)}, u32[]{:S(2)}) collective-permute-start(f32[6,32,128]{2,1,0:T(8,128)} %get-tuple-element.55), channel_id=1, source_target_pairs={{0,3},{1,2},{2,1},{3,0},{4,7},{5,6},{6,5},{7,4},{8,11},{9,10},{10,... | collective-permute-start | bytes 294920 | tf_op jit(solution)/shard_map/ppermute | solution.py:521
  185.2 8.1 %collective-permute-start.17 = (f32[6,32,128]{2,1,0:T(8,128)}, f32[6,32,128]{2,1,0:T(8,128)S(1)}, u32[]{:S(2)}, u32[]{:S(2)}) collective-permute-start(f32[6,32,128]{2,1,0:T(8,128)} %get-tuple-element.56), channel_id=1, source_target_pairs={{0,4},{1,5},{2,6},{3,7},{4,0},{5,1},{6,2},{7,3},{8,12},{9,13},{10,... | collective-permute-start | bytes 294920 | tf_op jit(solution)/shard_map/ppermute | solution.py:521
  185.2 8.8 %collective-permute-start.18 = (f32[6,32,128]{2,1,0:T(8,128)}, f32[6,32,128]{2,1,0:T(8,128)S(1)}, u32[]{:S(2)}, u32[]{:S(2)}) collective-permute-start(f32[6,32,128]{2,1,0:T(8,128)} %get-tuple-element.57), channel_id=1, source_target_pairs={{0,5},{1,4},{2,7},{3,6},{4,1},{5,0},{6,3},{7,2},{8,13},{9,12},{10,... | collective-permute-start | bytes 294920 | tf_op jit(solution)/shard_map/ppermute | solution.py:521
  188.0 9.3 %collective-permute-start.19 = (f32[6,32,128]{2,1,0:T(8,128)}, f32[6,32,128]{2,1,0:T(8,128)S(1)}, u32[]{:S(2)}, u32[]{:S(2)}) collective-permute-start(f32[6,32,128]{2,1,0:T(8,128)} %get-tuple-element.58), channel_id=1, source_target_pairs={{0,6},{1,7},{2,4},{3,5},{4,2},{5,3},{6,0},{7,1},{8,14},{9,15},{10,... | collective-permute-start | bytes 294920 | tf_op jit(solution)/shard_map/ppermute | solution.py:521
  188.7 8.6 %collective-permute-start.20 = (f32[6,32,128]{2,1,0:T(8,128)}, f32[6,32,128]{2,1,0:T(8,128)S(1)}, u32[]{:S(2)}, u32[]{:S(2)}) collective-permute-start(f32[6,32,128]{2,1,0:T(8,128)} %get-tuple-element.59), channel_id=1, source_target_pairs={{0,7},{1,6},{2,5},{3,4},{4,3},{5,2},{6,1},{7,0},{8,15},{9,14},{10,... | collective-permute-start | bytes 294920 | tf_op jit(solution)/shard_map/ppermute | solution.py:521
  197.3 0.9 copy-start.8
  198.2 13.3 %copy-start.10 = (s32[8,32]{1,0:T(8,128)S(1)}, s32[8,32]{1,0:T(8,128)}, u32[]{:S(2)}) copy-start(s32[8,32]{1,0:T(8,128)} %param.17) | copy-start | bytes 3076
  198.2 13.4 %copy-start.9 = (s32[8,32,2]{1,2,0:T(2,128)S(1)}, s32[8,32,2]{1,2,0:T(2,128)}, u32[]{:S(2)}) copy-start(s32[8,32,2]{1,2,0:T(2,128)} %param.18) | copy-start | bytes 6148
  200.6 35.0 %all-to-all-start.4 = ((f32[32,6,8,128]{3,2,1,0:T(8,128)}), f32[32,6,8,128]{3,2,1,0:T(8,128)S(1)}, u32[]{:S(2)}, u32[]{:S(2)}) async-start(f32[32,6,8,128]{3,2,1,0:T(8,128)} %x_backward.3), calls=%async_computation.4 | async-start | bytes 1572864 | tf_op jit(solution)/shard_map/all_to_all | solution.py:517
  211.8 9.5 %copy-start.2 = (f32[3,8,32,128]{3,2,1,0:T(8,128)S(1)}, f32[3,8,32,128]{3,2,1,0:T(8,128)}, u32[]{:S(2)}) copy-start(f32[3,8,32,128]{3,2,1,0:T(8,128)} %first.1) | copy-start | bytes 1179652
  211.8 9.5 %copy-start.3 = (f32[3,8,32,128]{3,2,1,0:T(8,128)S(1)}, f32[3,8,32,128]{3,2,1,0:T(8,128)}, u32[]{:S(2)}) copy-start(f32[3,8,32,128]{3,2,1,0:T(8,128)} %second.1) | copy-start | bytes 1179652
  221.3 14.4 %copy-start.4 = (f32[1,3,8,32,128]{4,3,2,1,0:T(8,128)S(1)}, f32[1,3,8,32,128]{4,3,2,1,0:T(8,128)}, u32[]{:S(2)}) copy-start(f32[1,3,8,32,128]{4,3,2,1,0:T(8,128)} %param.15) | copy-start | bytes 1179652
  221.3 14.4 %copy-start.5 = (f32[1,3,8,32,128]{4,3,2,1,0:T(8,128)S(1)}, f32[1,3,8,32,128]{4,3,2,1,0:T(8,128)}, u32[]{:S(2)}) copy-start(f32[1,3,8,32,128]{4,3,2,1,0:T(8,128)} %param.16) | copy-start | bytes 1179652

commit v4 on v3

--- a/solution.py
+++ b/solution.py
@@ -226,7 +226,7 @@
         name="x_forward",
         in_specs=[vmem, vmem, vmem],
         out_shape=jax.ShapeDtypeStruct((GZ, 6 * count, BX, 128), F32),
-    )(near(received), value, slope)
+    )(near(received), near(value), near(slope))
 
 
 ROWS = QY * BX
@@ -347,7 +347,7 @@
         in_specs=[pl.BlockSpec(memory_space=pltpu.SMEM)] + [vmem] * (len(inputs) + 2 + len(extra)),
         out_shape=[jax.ShapeDtypeStruct((3 * count, BX, 128), F32)] * GZ + ([grid_fields] if keep else []),
         scratch_shapes=scratch,
-    )(position, *[near(a) for a in inputs], value, slope, *extra)
+    )(position, *[near(a) for a in (*inputs, value, slope)], *extra)
     return result[:GZ], (result[GZ] if keep else None)
 
 
@@ -376,7 +376,7 @@
         in_specs=[pl.BlockSpec(memory_space=pltpu.SMEM)] + [vmem] * (GZ + 1),
         out_shape=jax.ShapeDtypeStruct((GX, fields, LX, 128), F32),
         scratch_shapes=[pltpu.VMEM((fields, NX, 128), F32)],
-    )(position, *[near(a) for a in received], value)
+    )(position, *[near(a) for a in received], near(value))
 
 
 PAD = 8

time: 246 us -> 244 us (level)
  starting transfers between devices: 81.4 us -> 85.5 us
  Pallas kernels: 64 us -> 60.7 us
    ppermute x21, waiting for transfers between devices: 32.7 us -> 30 us  [exchange_parts(): lax.ppermute(parts[k], 'pz', [(i, i ^ k) for i in range(GZ)])]
    unnamed x23 -> x31, local copies, waits for them, and re-layouts: 5.12 us -> 3.83 us
  transfers between devices with their start and end apart: 26 -> 26, of which waited for: 11 -> 10; matrix products, arithmetic and copies ran while one was open for 0% -> 0% of each run, Pallas kernels for 20% -> 19%
where the time goes in v4:
time: 244 us; the launch traced here: 243 us
  waiting for transfers between devices  91.4 us (37%)
  starting transfers between devices  85.5 us (35%)
  Pallas kernels  60.7 us (25%)
  local copies, waits for them, and re-layouts  4.26 us (2%)
    all_to_all x5, waiting for transfers between devices, exchange(): return lax.all_to_all(array, axis, split_axis=0, concat_axis=0, tiled=True)  61.5 us
    all_to_all x5, starting transfers between devices, exchange(): return lax.all_to_all(array, axis, split_axis=0, concat_axis=0, tiled=True)  46.3 us
    ppermute x21, starting transfers between devices, exchange_parts(): lax.ppermute(parts[k], 'pz', [(i, i ^ k) for i in range(GZ)])  39.2 us
    ppermute x21, waiting for transfers between devices, exchange_parts(): lax.ppermute(parts[k], 'pz', [(i, i ^ k) for i in range(GZ)])  30 us
    pallas_call x2, Pallas kernels, finish(): pl.pallas_call(kernel, name='finish', in_specs=[vmem] * 5 + [far] * 3, ou...  23.7 us
    pallas_call x2, Pallas kernels, z_stage(): pl.pallas_call(kernel, name='z_stage_first' if keep else 'z_stage_second'...  10.6 us
    pallas_call x1, Pallas kernels, split_inverse(): pl.pallas_call(kernel, name='split_inverse', grid=(LX,), in_specs=[pl.Blo...  9.35 us
    pallas_call x2, Pallas kernels, y_forward(): pl.pallas_call(kernel, name='y_forward', out_shape=jax.ShapeDtypeStruct((...  8.07 us
  transfers between devices with their start and end apart: 26, of which 10 were waited for; matrix products, arithmetic and copies ran while one was open for 0% of the time, Pallas kernels for 19%

profile of v4, /device:TPU:1, one launch (start us, length us, event | category | flops | bytes accessed | tf_op | source)
XLA Modules:
  0.0 243.0 jit_solution(8897893062380184149)
XLA Ops:
  0.6 4.6 %y_forward.3 = f32[2560,128]{1,0:T(8,128)} custom-call(f32[3,8,32,128]{3,2,1,0:T(8,128)} %bitcast.15, f32[3,8,32,128]{3,2,1,0:T(8,128)} %bitcast.17, bf16[256,256]{1,0:T(8,128)(2,1)} %constant.18.clone.refs_2_), custom_call_target="tpu_custom_call" | custom-call | tf_op jit(solution)/shard_map/y_forward/pallas_call | solution.py:164
  5.3 11.0 %all-to-all-start.2 = ((f32[32,10,8,128]{3,2,1,0:T(8,128)}), f32[32,10,8,128]{3,2,1,0:T(8,128)S(1)}, u32[]{:S(2)}, u32[]{:S(2)}) async-start(f32[32,10,8,128]{3,2,1,0:T(8,128)} %bitcast.22), calls=%async_computation.2 | async-start | bytes 2621440 | tf_op jit(solution)/shard_map/all_to_all | solution.py:517
  16.3 3.5 %y_forward.2 = f32[2560,128]{1,0:T(8,128)} custom-call(f32[3,8,32,128]{3,2,1,0:T(8,128)} %first.1, f32[3,8,32,128]{3,2,1,0:T(8,128)} %second.1, bf16[256,256]{1,0:T(8,128)(2,1)} %constant.18.clone.refs_2_), custom_call_target="tpu_custom_call" | custom-call | tf_op jit(solution)/shard_map/y_forward/pallas_call | solution.py:164
  19.8 30.2 %all-to-all-done.2.refs_0_ = f32[32,10,8,128]{3,2,1,0:T(8,128)S(1)} async-done(((f32[32,10,8,128]{3,2,1,0:T(8,128)}), f32[32,10,8,128]{3,2,1,0:T(8,128)S(1)}, u32[]{:S(2)}, u32[]{:S(2)}) %all-to-all-start.2) | async-done | bytes 1310752 | tf_op jit(solution)/shard_map/all_to_all | solution.py:517
  50.0 1.1 copy-done.2
  51.1 5.0 %all-to-all-start = ((f32[32,10,8,128]{3,2,1,0:T(8,128)}), f32[32,10,8,128]{3,2,1,0:T(8,128)}, u32[]{:S(2)}, u32[]{:S(2)}) async-start(f32[32,10,8,128]{3,2,1,0:T(8,128)} %bitcast.21), calls=%async_computation | async-start | bytes 2621440 | tf_op jit(solution)/shard_map/all_to_all | solution.py:517
  56.1 2.3 x_forward.1
  58.4 31.2 %all-to-all-done.refs_1_ = f32[32,10,8,128]{3,2,1,0:T(8,128)} async-done(((f32[32,10,8,128]{3,2,1,0:T(8,128)}), f32[32,10,8,128]{3,2,1,0:T(8,128)}, u32[]{:S(2)}, u32[]{:S(2)}) %all-to-all-start) | async-done | bytes 1310752 | tf_op jit(solution)/shard_map/all_to_all | solution.py:517
  89.6 6.4 %all-to-all-start.3 = ((f32[8,12,32,128]{3,2,1,0:T(8,128)}), f32[8,12,32,128]{3,2,1,0:T(8,128)}, u32[]{:S(2)}, u32[]{:S(2)}) async-start(f32[8,12,32,128]{3,2,1,0:T(8,128)} %x_forward.1), calls=%async_computation.3 | async-start | bytes 3145728 | tf_op jit(solution)/shard_map/all_to_all | solution.py:517
  96.0 0.0 copy-start.8
  96.0 3.8 %x_forward_parts.1 = (f32[12,32,128]{2,1,0:T(8,128)}, f32[12,32,128]{2,1,0:T(8,128)}, f32[12,32,128]{2,1,0:T(8,128)}, f32[12,32,128]{2,1,0:T(8,128)}, f32[12,32,...) custom-call(s32[1]{0:T(128)} %bitcast.refs_0_, ...), custom_call_target="tpu_custom_call" | custom-call | tf_op jit(solution)/shard_map/x_forward_parts/pallas_call | solution.py:217
  99.8 2.9 %collective-permute-start = (f32[12,32,128]{2,1,0:T(8,128)}, f32[12,32,128]{2,1,0:T(8,128)S(1)}, u32[]{:S(2)}, u32[]{:S(2)}) collective-permute-start(f32[12,32,128]{2,1,0:T(8,128)} %get-tuple-element.34), channel_id=1, source_target_pairs={{0,1},{1,0},{2,3},{3,2},{4,5},{5,4},{6,7},{7,6},{8,9},{9,8},{10,11... | collective-permute-start | bytes 589832 | tf_op jit(solution)/shard_map/ppermute | solution.py:521
  102.7 1.2 collective-permute-start.1
  103.9 0.0 collective-permute-start.2
  103.9 2.9 %collective-permute-start.3 = (f32[12,32,128]{2,1,0:T(8,128)}, f32[12,32,128]{2,1,0:T(8,128)S(1)}, u32[]{:S(2)}, u32[]{:S(2)}) collective-permute-start(f32[12,32,128]{2,1,0:T(8,128)} %get-tuple-element.37), channel_id=1, source_target_pairs={{0,4},{1,5},{2,6},{3,7},{4,0},{5,1},{6,2},{7,3},{8,12},{9,13},{10,... | collective-permute-start | bytes 589832 | tf_op jit(solution)/shard_map/ppermute | solution.py:521
  106.9 2.7 %collective-permute-start.4 = (f32[12,32,128]{2,1,0:T(8,128)}, f32[12,32,128]{2,1,0:T(8,128)S(1)}, u32[]{:S(2)}, u32[]{:S(2)}) collective-permute-start(f32[12,32,128]{2,1,0:T(8,128)} %get-tuple-element.38), channel_id=1, source_target_pairs={{0,5},{1,4},{2,7},{3,6},{4,1},{5,0},{6,3},{7,2},{8,13},{9,12},{10,... | collective-permute-start | bytes 589832 | tf_op jit(solution)/shard_map/ppermute | solution.py:521
  109.5 9.6 %collective-permute-done.refs_2_ = f32[12,32,128]{2,1,0:T(8,128)S(1)} collective-permute-done((f32[12,32,128]{2,1,0:T(8,128)}, f32[12,32,128]{2,1,0:T(8,128)S(1)}, u32[]{:S(2)}, u32[]{:S(2)}) %collective-permute-start) | collective-permute-done | bytes 196640 | tf_op jit(solution)/shard_map/ppermute | solution.py:521
  119.2 2.4 collective-permute-start.5
  121.6 0.0 collective-permute-done.1.refs_3_
  121.6 2.6 %collective-permute-start.6 = (f32[12,32,128]{2,1,0:T(8,128)}, f32[12,32,128]{2,1,0:T(8,128)S(1)}, u32[]{:S(2)}, u32[]{:S(2)}) collective-permute-start(f32[12,32,128]{2,1,0:T(8,128)} %get-tuple-element.40), channel_id=1, source_target_pairs={{0,7},{1,6},{2,5},{3,4},{4,3},{5,2},{6,1},{7,0},{8,15},{9,14},{10,... | collective-permute-start | bytes 589832 | tf_op jit(solution)/shard_map/ppermute | solution.py:521
  124.2 0.9 collective-permute-done.3.refs_5_
  125.1 4.5 %collective-permute-done.4.refs_6_ = f32[12,32,128]{2,1,0:T(8,128)S(1)} collective-permute-done((f32[12,32,128]{2,1,0:T(8,128)}, f32[12,32,128]{2,1,0:T(8,128)S(1)}, u32[]{:S(2)}, u32[]{:S(2)}) %collective-permute-start.4) | collective-permute-done | bytes 196640 | tf_op jit(solution)/shard_map/ppermute | solution.py:521
  129.6 4.8 %collective-permute-done.6.refs_8_ = f32[12,32,128]{2,1,0:T(8,128)S(1)} collective-permute-done((f32[12,32,128]{2,1,0:T(8,128)}, f32[12,32,128]{2,1,0:T(8,128)S(1)}, u32[]{:S(2)}, u32[]{:S(2)}) %collective-permute-start.6) | collective-permute-done | bytes 196640 | tf_op jit(solution)/shard_map/ppermute | solution.py:521
  134.4 0.9 copy-done.10
  135.3 4.5 %z_stage_first.1 = (f32[6,32,128]{2,1,0:T(8,128)}, f32[6,32,128]{2,1,0:T(8,128)}, f32[6,32,128]{2,1,0:T(8,128)}, f32[6,32,128]{2,1,0:T(8,128)}, f32[6,32,128]{2,...) custom-call(s32[1]{0:T(128)} %bitcast.refs_0_, ...), custom_call_target="tpu_custom_call" | custom-call | tf_op jit(solution)/shard_map/z_stage_first/pallas_call | solution.py:344
  139.9 1.0 collective-permute-start.7
  140.9 2.9 %collective-permute-start.8 = (f32[6,32,128]{2,1,0:T(8,128)}, f32[6,32,128]{2,1,0:T(8,128)S(1)}, u32[]{:S(2)}, u32[]{:S(2)}) collective-permute-start(f32[6,32,128]{2,1,0:T(8,128)} %get-tuple-element.43), channel_id=1, source_target_pairs={{0,2},{1,3},{2,0},{3,1},{4,6},{5,7},{6,4},{7,5},{8,10},{9,11},{10,... | collective-permute-start | bytes 294920 | tf_op jit(solution)/shard_map/ppermute | solution.py:521
  143.8 0.2 collective-permute-start.9
  144.0 1.8 collective-permute-start.10
  145.9 3.3 %collective-permute-start.11 = (f32[6,32,128]{2,1,0:T(8,128)}, f32[6,32,128]{2,1,0:T(8,128)S(1)}, u32[]{:S(2)}, u32[]{:S(2)}) collective-permute-start(f32[6,32,128]{2,1,0:T(8,128)} %get-tuple-element.46), channel_id=1, source_target_pairs={{0,5},{1,4},{2,7},{3,6},{4,1},{5,0},{6,3},{7,2},{8,13},{9,12},{10,... | collective-permute-start | bytes 294920 | tf_op jit(solution)/shard_map/ppermute | solution.py:521
  149.2 2.3 collective-permute-start.12
  151.5 0.0 collective-permute-done.8.refs_3_
  151.5 0.6 collective-permute-start.13
  152.1 1.4 collective-permute-done.11.refs_6_
  153.5 1.3 collective-permute-done.12.refs_7_
  154.8 4.0 %collective-permute-done.13.refs_8_ = f32[6,32,128]{2,1,0:T(8,128)S(1)} collective-permute-done((f32[6,32,128]{2,1,0:T(8,128)}, f32[6,32,128]{2,1,0:T(8,128)S(1)}, u32[]{:S(2)}, u32[]{:S(2)}) %collective-permute-start.13) | collective-permute-done | bytes 98336 | tf_op jit(solution)/shard_map/ppermute | solution.py:521
  158.8 0.9 copy-done.11
  159.7 1.5 x_backward.2
  161.2 0.0 all-to-all-done.3.refs_1_
  161.2 12.7 %all-to-all-start.1 = ((f32[32,6,8,128]{3,2,1,0:T(8,128)}), f32[32,6,8,128]{3,2,1,0:T(8,128)S(1)}, u32[]{:S(2)}, u32[]{:S(2)}) async-start(f32[32,6,8,128]{3,2,1,0:T(8,128)} %x_backward.2), calls=%async_computation.1 | async-start | bytes 1572864 | tf_op jit(solution)/shard_map/all_to_all | solution.py:517
  173.9 6.0 %z_stage_second.1 = (f32[6,32,128]{2,1,0:T(8,128)}, f32[6,32,128]{2,1,0:T(8,128)}, f32[6,32,128]{2,1,0:T(8,128)}, f32[6,32,128]{2,1,0:T(8,128)}, f32[6,32,128]{2...) custom-call(s32[1]{0:T(128)} %bitcast.refs_0_, ...), custom_call_target="tpu_custom_call" | custom-call | tf_op jit(solution)/shard_map/z_stage_second/pallas_call | solution.py:344
  179.9 0.2 collective-permute-start.14
  180.1 3.9 %collective-permute-start.16 = (f32[6,32,128]{2,1,0:T(8,128)}, f32[6,32,128]{2,1,0:T(8,128)S(1)}, u32[]{:S(2)}, u32[]{:S(2)}) collective-permute-start(f32[6,32,128]{2,1,0:T(8,128)} %get-tuple-element.55), channel_id=1, source_target_pairs={{0,3},{1,2},{2,1},{3,0},{4,7},{5,6},{6,5},{7,4},{8,11},{9,10},{10,... | collective-permute-start | bytes 294920 | tf_op jit(solution)/shard_map/ppermute | solution.py:521
  184.1 0.0 collective-permute-start.17
  184.1 2.9 %collective-permute-start.18 = (f32[6,32,128]{2,1,0:T(8,128)}, f32[6,32,128]{2,1,0:T(8,128)S(1)}, u32[]{:S(2)}, u32[]{:S(2)}) collective-permute-start(f32[6,32,128]{2,1,0:T(8,128)} %get-tuple-element.57), channel_id=1, source_target_pairs={{0,5},{1,4},{2,7},{3,6},{4,1},{5,0},{6,3},{7,2},{8,13},{9,12},{10,... | collective-permute-start | bytes 294920 | tf_op jit(solution)/shard_map/ppermute | solution.py:521
  187.0 0.0 collective-permute-done.14.refs_2_
  187.0 0.6 collective-permute-start.19
  187.5 4.6 %collective-permute-start.20 = (f32[6,32,128]{2,1,0:T(8,128)}, f32[6,32,128]{2,1,0:T(8,128)S(1)}, u32[]{:S(2)}, u32[]{:S(2)}) collective-permute-start(f32[6,32,128]{2,1,0:T(8,128)} %get-tuple-element.59), channel_id=1, source_target_pairs={{0,7},{1,6},{2,5},{3,4},{4,3},{5,2},{6,1},{7,0},{8,15},{9,14},{10,... | collective-permute-start | bytes 294920 | tf_op jit(solution)/shard_map/ppermute | solution.py:521
  192.2 3.4 %collective-permute-done.19.refs_7_ = f32[6,32,128]{2,1,0:T(8,128)S(1)} collective-permute-done((f32[6,32,128]{2,1,0:T(8,128)}, f32[6,32,128]{2,1,0:T(8,128)S(1)}, u32[]{:S(2)}, u32[]{:S(2)}) %collective-permute-start.19) | collective-permute-done | bytes 98336 | tf_op jit(solution)/shard_map/ppermute | solution.py:521
  195.6 0.9 copy-done.12
  196.5 1.4 x_backward.3
  197.9 11.2 %all-to-all-start.4 = ((f32[32,6,8,128]{3,2,1,0:T(8,128)}), f32[32,6,8,128]{3,2,1,0:T(8,128)S(1)}, u32[]{:S(2)}, u32[]{:S(2)}) async-start(f32[32,6,8,128]{3,2,1,0:T(8,128)} %x_backward.3), calls=%async_computation.4 | async-start | bytes 1572864 | tf_op jit(solution)/shard_map/all_to_all | solution.py:517
  209.1 0.1 ne.23
  209.2 0.1 broadcast_in_dim.8
  209.3 0.1 ne.25
  209.4 0.1 copy.18
  209.5 0.0 copy-start.4
  209.5 0.0 copy-start.5
  209.5 9.3 %split_inverse.1 = bf16[8,32,128,128]{3,2,1,0:T(8,128)(2,1)} custom-call(f32[8,32,64,128]{3,2,1,0:T(8,128)} %in_ref.1), custom_call_target="tpu_custom_call" | custom-call | tf_op jit(solution)/shard_map/split_inverse/pallas_call | solution.py:393
  218.9 0.1 broadcast_in_dim.9.gain_ref
  219.0 0.0 copy-start.6
  219.0 0.0 copy-start.7
  219.0 14.3 %finish.2 = (f32[3,8,32,128]{3,2,1,0:T(8,128)}, f32[3,8,32,128]{3,2,1,0:T(8,128)}) custom-call(f32[1536,128]{1,0:T(8,128)S(1)} %bitcast.13, f32[3,8,32,128]{3,2,1,0:T(8,128)S(1)} %copy-done.4, f32[3,8,32,128]{3,2,1,0:T(8,128)S(1)} %copy-done.5, f32[256,128]{1,0:T(8,128)S(1)} %broadcast_in_dim.9.gain_ref, f32[256,128]{1,0:T(8,128)S(1)} %compare_convert_fusion.keep_ref, ...), custom_call_target="tpu_custom_call" | custom-call | tf_op jit(solution)/shard_map/finish/pallas_call | solution.py:504
  233.4 9.4 %finish.3 = (f32[3,8,32,128]{3,2,1,0:T(8,128)}, f32[3,8,32,128]{3,2,1,0:T(8,128)}) custom-call(f32[1536,128]{1,0:T(8,128)S(1)} %bitcast.14, f32[3,8,32,128]{3,2,1,0:T(8,128)S(1)} %bitcast.16, f32[3,8,32,128]{3,2,1,0:T(8,128)S(1)} %bitcast.18, f32[256,128]{1,0:T(8,128)S(1)} %broadcast_in_dim.9.gain_ref, f32[256,128]{1,0:T(8,128)S(1)} %compare_convert_fusion.keep_ref, ...), custom_call_target="tpu_custom_call" | custom-call | tf_op jit(solution)/shard_map/finish/pallas_call | solution.py:504
  (39 shorter events, 0.1 us)
Async XLA Ops:
  5.3 44.8 %all-to-all-start.2 = ((f32[32,10,8,128]{3,2,1,0:T(8,128)}), f32[32,10,8,128]{3,2,1,0:T(8,128)S(1)}, u32[]{:S(2)}, u32[]{:S(2)}) async-start(f32[32,10,8,128]{3,2,1,0:T(8,128)} %bitcast.22), calls=%async_computation.2 | async-start | bytes 2621440 | tf_op jit(solution)/shard_map/all_to_all | solution.py:517
  19.8 36.3 %copy-start = (bf16[256,512]{1,0:T(8,128)(2,1)S(1)}, bf16[256,512]{1,0:T(8,128)(2,1)}, u32[]{:S(2)}) copy-start(bf16[256,512]{1,0:T(8,128)(2,1)} %constant.19.clone.refs_2_.refs_9_.refs_1_) | copy-start | bytes 786436
  19.8 36.3 %copy-start.9 = (bf16[256,512]{1,0:T(8,128)(2,1)S(1)}, bf16[256,512]{1,0:T(8,128)(2,1)}, u32[]{:S(2)}) copy-start(bf16[256,512]{1,0:T(8,128)(2,1)} %constant.20.clone.refs_3_.refs_2_) | copy-start | bytes 786436
  50.0 1.1 copy-start.2
  51.1 5.0 %copy-start.3 = (f32[32,10,8,128]{3,2,1,0:T(8,128)S(1)}, f32[32,10,8,128]{3,2,1,0:T(8,128)}, u32[]{:S(2)}) copy-start(f32[32,10,8,128]{3,2,1,0:T(8,128)} %copy-done.2) | copy-start | bytes 3932164
  51.1 38.5 %all-to-all-start = ((f32[32,10,8,128]{3,2,1,0:T(8,128)}), f32[32,10,8,128]{3,2,1,0:T(8,128)}, u32[]{:S(2)}, u32[]{:S(2)}) async-start(f32[32,10,8,128]{3,2,1,0:T(8,128)} %bitcast.21), calls=%async_computation | async-start | bytes 2621440 | tf_op jit(solution)/shard_map/all_to_all | solution.py:517
  89.6 71.6 %all-to-all-start.3 = ((f32[8,12,32,128]{3,2,1,0:T(8,128)}), f32[8,12,32,128]{3,2,1,0:T(8,128)}, u32[]{:S(2)}, u32[]{:S(2)}) async-start(f32[8,12,32,128]{3,2,1,0:T(8,128)} %x_forward.1), calls=%async_computation.3 | async-start | bytes 3145728 | tf_op jit(solution)/shard_map/all_to_all | solution.py:517
  96.0 38.4 %copy-start.1 = (bf16[256,512]{1,0:T(8,128)(2,1)S(1)}, bf16[256,512]{1,0:T(8,128)(2,1)}, u32[]{:S(2)}) copy-start(bf16[256,512]{1,0:T(8,128)(2,1)} %constant.19.clone.refs_2_.refs_9_.refs_1_) | copy-start | bytes 786436
  96.0 38.4 %copy-start.8 = (bf16[256,512]{1,0:T(8,128)(2,1)S(1)}, bf16[256,512]{1,0:T(8,128)(2,1)}, u32[]{:S(2)}) copy-start(bf16[256,512]{1,0:T(8,128)(2,1)} %constant.21.clone.refs_10_.refs_3_) | copy-start | bytes 786436
  99.8 19.4 %collective-permute-start = (f32[12,32,128]{2,1,0:T(8,128)}, f32[12,32,128]{2,1,0:T(8,128)S(1)}, u32[]{:S(2)}, u32[]{:S(2)}) collective-permute-start(f32[12,32,128]{2,1,0:T(8,128)} %get-tuple-element.34), channel_id=1, source_target_pairs={{0,1},{1,0},{2,3},{3,2},{4,5},{5,4},{6,7},{7,6},{8,9},{9,8},{10,11... | collective-permute-start | bytes 589832 | tf_op jit(solution)/shard_map/ppermute | solution.py:521
  102.7 18.9 %collective-permute-start.1 = (f32[12,32,128]{2,1,0:T(8,128)}, f32[12,32,128]{2,1,0:T(8,128)S(1)}, u32[]{:S(2)}, u32[]{:S(2)}) collective-permute-start(f32[12,32,128]{2,1,0:T(8,128)} %get-tuple-element.35), channel_id=1, source_target_pairs={{0,2},{1,3},{2,0},{3,1},{4,6},{5,7},{6,4},{7,5},{8,10},{9,11},{10,... | collective-permute-start | bytes 589832 | tf_op jit(solution)/shard_map/ppermute | solution.py:521
  103.9 20.3 %collective-permute-start.2 = (f32[12,32,128]{2,1,0:T(8,128)}, f32[12,32,128]{2,1,0:T(8,128)S(1)}, u32[]{:S(2)}, u32[]{:S(2)}) collective-permute-start(f32[12,32,128]{2,1,0:T(8,128)} %get-tuple-element.36), channel_id=1, source_target_pairs={{0,3},{1,2},{2,1},{3,0},{4,7},{5,6},{6,5},{7,4},{8,11},{9,10},{10,... | collective-permute-start | bytes 589832 | tf_op jit(solution)/shard_map/ppermute | solution.py:521
  103.9 21.2 %collective-permute-start.3 = (f32[12,32,128]{2,1,0:T(8,128)}, f32[12,32,128]{2,1,0:T(8,128)S(1)}, u32[]{:S(2)}, u32[]{:S(2)}) collective-permute-start(f32[12,32,128]{2,1,0:T(8,128)} %get-tuple-element.37), channel_id=1, source_target_pairs={{0,4},{1,5},{2,6},{3,7},{4,0},{5,1},{6,2},{7,3},{8,12},{9,13},{10,... | collective-permute-start | bytes 589832 | tf_op jit(solution)/shard_map/ppermute | solution.py:521
  106.9 22.7 %collective-permute-start.4 = (f32[12,32,128]{2,1,0:T(8,128)}, f32[12,32,128]{2,1,0:T(8,128)S(1)}, u32[]{:S(2)}, u32[]{:S(2)}) collective-permute-start(f32[12,32,128]{2,1,0:T(8,128)} %get-tuple-element.38), channel_id=1, source_target_pairs={{0,5},{1,4},{2,7},{3,6},{4,1},{5,0},{6,3},{7,2},{8,13},{9,12},{10,... | collective-permute-start | bytes 589832 | tf_op jit(solution)/shard_map/ppermute | solution.py:521
  119.2 10.4 %collective-permute-start.5 = (f32[12,32,128]{2,1,0:T(8,128)}, f32[12,32,128]{2,1,0:T(8,128)S(1)}, u32[]{:S(2)}, u32[]{:S(2)}) collective-permute-start(f32[12,32,128]{2,1,0:T(8,128)} %get-tuple-element.39), channel_id=1, source_target_pairs={{0,6},{1,7},{2,4},{3,5},{4,2},{5,3},{6,0},{7,1},{8,14},{9,15},{10,... | collective-permute-start | bytes 589832 | tf_op jit(solution)/shard_map/ppermute | solution.py:521
  121.6 12.8 %collective-permute-start.6 = (f32[12,32,128]{2,1,0:T(8,128)}, f32[12,32,128]{2,1,0:T(8,128)S(1)}, u32[]{:S(2)}, u32[]{:S(2)}) collective-permute-start(f32[12,32,128]{2,1,0:T(8,128)} %get-tuple-element.40), channel_id=1, source_target_pairs={{0,7},{1,6},{2,5},{3,4},{4,3},{5,2},{6,1},{7,0},{8,15},{9,14},{10,... | collective-permute-start | bytes 589832 | tf_op jit(solution)/shard_map/ppermute | solution.py:521
  134.4 0.9 copy-start.10
  139.9 9.3 %collective-permute-start.7 = (f32[6,32,128]{2,1,0:T(8,128)}, f32[6,32,128]{2,1,0:T(8,128)S(1)}, u32[]{:S(2)}, u32[]{:S(2)}) collective-permute-start(f32[6,32,128]{2,1,0:T(8,128)} %get-tuple-element.42), channel_id=1, source_target_pairs={{0,1},{1,0},{2,3},{3,2},{4,5},{5,4},{6,7},{7,6},{8,9},{9,8},{10,11... | collective-permute-start | bytes 294920 | tf_op jit(solution)/shard_map/ppermute | solution.py:521
  140.9 10.6 %collective-permute-start.8 = (f32[6,32,128]{2,1,0:T(8,128)}, f32[6,32,128]{2,1,0:T(8,128)S(1)}, u32[]{:S(2)}, u32[]{:S(2)}) collective-permute-start(f32[6,32,128]{2,1,0:T(8,128)} %get-tuple-element.43), channel_id=1, source_target_pairs={{0,2},{1,3},{2,0},{3,1},{4,6},{5,7},{6,4},{7,5},{8,10},{9,11},{10,... | collective-permute-start | bytes 294920 | tf_op jit(solution)/shard_map/ppermute | solution.py:521
  143.8 8.3 %collective-permute-start.9 = (f32[6,32,128]{2,1,0:T(8,128)}, f32[6,32,128]{2,1,0:T(8,128)S(1)}, u32[]{:S(2)}, u32[]{:S(2)}) collective-permute-start(f32[6,32,128]{2,1,0:T(8,128)} %get-tuple-element.44), channel_id=1, source_target_pairs={{0,3},{1,2},{2,1},{3,0},{4,7},{5,6},{6,5},{7,4},{8,11},{9,10},{10,... | collective-permute-start | bytes 294920 | tf_op jit(solution)/shard_map/ppermute | solution.py:521
  144.0 8.1 %collective-permute-start.10 = (f32[6,32,128]{2,1,0:T(8,128)}, f32[6,32,128]{2,1,0:T(8,128)S(1)}, u32[]{:S(2)}, u32[]{:S(2)}) collective-permute-start(f32[6,32,128]{2,1,0:T(8,128)} %get-tuple-element.45), channel_id=1, source_target_pairs={{0,4},{1,5},{2,6},{3,7},{4,0},{5,1},{6,2},{7,3},{8,12},{9,13},{10,... | collective-permute-start | bytes 294920 | tf_op jit(solution)/shard_map/ppermute | solution.py:521
  145.9 7.6 %collective-permute-start.11 = (f32[6,32,128]{2,1,0:T(8,128)}, f32[6,32,128]{2,1,0:T(8,128)S(1)}, u32[]{:S(2)}, u32[]{:S(2)}) collective-permute-start(f32[6,32,128]{2,1,0:T(8,128)} %get-tuple-element.46), channel_id=1, source_target_pairs={{0,5},{1,4},{2,7},{3,6},{4,1},{5,0},{6,3},{7,2},{8,13},{9,12},{10,... | collective-permute-start | bytes 294920 | tf_op jit(solution)/shard_map/ppermute | solution.py:521
  149.2 5.6 %collective-permute-start.12 = (f32[6,32,128]{2,1,0:T(8,128)}, f32[6,32,128]{2,1,0:T(8,128)S(1)}, u32[]{:S(2)}, u32[]{:S(2)}) collective-permute-start(f32[6,32,128]{2,1,0:T(8,128)} %get-tuple-element.47), channel_id=1, source_target_pairs={{0,6},{1,7},{2,4},{3,5},{4,2},{5,3},{6,0},{7,1},{8,14},{9,15},{10,... | collective-permute-start | bytes 294920 | tf_op jit(solution)/shard_map/ppermute | solution.py:521
  151.5 7.3 %collective-permute-start.13 = (f32[6,32,128]{2,1,0:T(8,128)}, f32[6,32,128]{2,1,0:T(8,128)S(1)}, u32[]{:S(2)}, u32[]{:S(2)}) collective-permute-start(f32[6,32,128]{2,1,0:T(8,128)} %get-tuple-element.48), channel_id=1, source_target_pairs={{0,7},{1,6},{2,5},{3,4},{4,3},{5,2},{6,1},{7,0},{8,15},{9,14},{10,... | collective-permute-start | bytes 294920 | tf_op jit(solution)/shard_map/ppermute | solution.py:521
  158.8 0.9 copy-start.11
  161.2 36.7 %all-to-all-start.1 = ((f32[32,6,8,128]{3,2,1,0:T(8,128)}), f32[32,6,8,128]{3,2,1,0:T(8,128)S(1)}, u32[]{:S(2)}, u32[]{:S(2)}) async-start(f32[32,6,8,128]{3,2,1,0:T(8,128)} %x_backward.2), calls=%async_computation.1 | async-start | bytes 1572864 | tf_op jit(solution)/shard_map/all_to_all | solution.py:517
  179.9 7.0 %collective-permute-start.14 = (f32[6,32,128]{2,1,0:T(8,128)}, f32[6,32,128]{2,1,0:T(8,128)S(1)}, u32[]{:S(2)}, u32[]{:S(2)}) collective-permute-start(f32[6,32,128]{2,1,0:T(8,128)} %get-tuple-element.53), channel_id=1, source_target_pairs={{0,1},{1,0},{2,3},{3,2},{4,5},{5,4},{6,7},{7,6},{8,9},{9,8},{10,11... | collective-permute-start | bytes 294920 | tf_op jit(solution)/shard_map/ppermute | solution.py:521
  180.1 7.4 %collective-permute-start.15 = (f32[6,32,128]{2,1,0:T(8,128)}, f32[6,32,128]{2,1,0:T(8,128)S(1)}, u32[]{:S(2)}, u32[]{:S(2)}) collective-permute-start(f32[6,32,128]{2,1,0:T(8,128)} %get-tuple-element.54), channel_id=1, source_target_pairs={{0,2},{1,3},{2,0},{3,1},{4,6},{5,7},{6,4},{7,5},{8,10},{9,11},{10,... | collective-permute-start | bytes 294920 | tf_op jit(solution)/shard_map/ppermute | solution.py:521
  180.1 12.0 %collective-permute-start.16 = (f32[6,32,128]{2,1,0:T(8,128)}, f32[6,32,128]{2,1,0:T(8,128)S(1)}, u32[]{:S(2)}, u32[]{:S(2)}) collective-permute-start(f32[6,32,128]{2,1,0:T(8,128)} %get-tuple-element.55), channel_id=1, source_target_pairs={{0,3},{1,2},{2,1},{3,0},{4,7},{5,6},{6,5},{7,4},{8,11},{9,10},{10,... | collective-permute-start | bytes 294920 | tf_op jit(solution)/shard_map/ppermute | solution.py:521
  184.1 8.1 %collective-permute-start.17 = (f32[6,32,128]{2,1,0:T(8,128)}, f32[6,32,128]{2,1,0:T(8,128)S(1)}, u32[]{:S(2)}, u32[]{:S(2)}) collective-permute-start(f32[6,32,128]{2,1,0:T(8,128)} %get-tuple-element.56), channel_id=1, source_target_pairs={{0,4},{1,5},{2,6},{3,7},{4,0},{5,1},{6,2},{7,3},{8,12},{9,13},{10,... | collective-permute-start | bytes 294920 | tf_op jit(solution)/shard_map/ppermute | solution.py:521
  184.1 8.1 %collective-permute-start.18 = (f32[6,32,128]{2,1,0:T(8,128)}, f32[6,32,128]{2,1,0:T(8,128)S(1)}, u32[]{:S(2)}, u32[]{:S(2)}) collective-permute-start(f32[6,32,128]{2,1,0:T(8,128)} %get-tuple-element.57), channel_id=1, source_target_pairs={{0,5},{1,4},{2,7},{3,6},{4,1},{5,0},{6,3},{7,2},{8,13},{9,12},{10,... | collective-permute-start | bytes 294920 | tf_op jit(solution)/shard_map/ppermute | solution.py:521
  187.0 8.6 %collective-permute-start.19 = (f32[6,32,128]{2,1,0:T(8,128)}, f32[6,32,128]{2,1,0:T(8,128)S(1)}, u32[]{:S(2)}, u32[]{:S(2)}) collective-permute-start(f32[6,32,128]{2,1,0:T(8,128)} %get-tuple-element.58), channel_id=1, source_target_pairs={{0,6},{1,7},{2,4},{3,5},{4,2},{5,3},{6,0},{7,1},{8,14},{9,15},{10,... | collective-permute-start | bytes 294920 | tf_op jit(solution)/shard_map/ppermute | solution.py:521
  187.5 8.0 %collective-permute-start.20 = (f32[6,32,128]{2,1,0:T(8,128)}, f32[6,32,128]{2,1,0:T(8,128)S(1)}, u32[]{:S(2)}, u32[]{:S(2)}) collective-permute-start(f32[6,32,128]{2,1,0:T(8,128)} %get-tuple-element.59), channel_id=1, source_target_pairs={{0,7},{1,6},{2,5},{3,4},{4,3},{5,2},{6,1},{7,0},{8,15},{9,14},{10,... | collective-permute-start | bytes 294920 | tf_op jit(solution)/shard_map/ppermute | solution.py:521
  195.6 0.9 copy-start.12
  196.5 12.8 %copy-start.14 = (s32[8,32]{1,0:T(8,128)S(1)}, s32[8,32]{1,0:T(8,128)}, u32[]{:S(2)}) copy-start(s32[8,32]{1,0:T(8,128)} %param.17) | copy-start | bytes 3076
  196.5 12.8 %copy-start.13 = (s32[8,32,2]{1,2,0:T(2,128)S(1)}, s32[8,32,2]{1,2,0:T(2,128)}, u32[]{:S(2)}) copy-start(s32[8,32,2]{1,2,0:T(2,128)} %param.18) | copy-start | bytes 6148
  197.9 35.5 %all-to-all-start.4 = ((f32[32,6,8,128]{3,2,1,0:T(8,128)}), f32[32,6,8,128]{3,2,1,0:T(8,128)S(1)}, u32[]{:S(2)}, u32[]{:S(2)}) async-start(f32[32,6,8,128]{3,2,1,0:T(8,128)} %x_backward.3), calls=%async_computation.4 | async-start | bytes 1572864 | tf_op jit(solution)/shard_map/all_to_all | solution.py:517
  209.5 9.5 %copy-start.4 = (f32[3,8,32,128]{3,2,1,0:T(8,128)S(1)}, f32[3,8,32,128]{3,2,1,0:T(8,128)}, u32[]{:S(2)}) copy-start(f32[3,8,32,128]{3,2,1,0:T(8,128)} %first.1) | copy-start | bytes 1179652
  209.5 9.5 %copy-start.5 = (f32[3,8,32,128]{3,2,1,0:T(8,128)S(1)}, f32[3,8,32,128]{3,2,1,0:T(8,128)}, u32[]{:S(2)}) copy-start(f32[3,8,32,128]{3,2,1,0:T(8,128)} %second.1) | copy-start | bytes 1179652
  219.0 14.4 %copy-start.6 = (f32[1,3,8,32,128]{4,3,2,1,0:T(8,128)S(1)}, f32[1,3,8,32,128]{4,3,2,1,0:T(8,128)}, u32[]{:S(2)}) copy-start(f32[1,3,8,32,128]{4,3,2,1,0:T(8,128)} %param.15) | copy-start | bytes 1179652
  219.0 14.4 %copy-start.7 = (f32[1,3,8,32,128]{4,3,2,1,0:T(8,128)S(1)}, f32[1,3,8,32,128]{4,3,2,1,0:T(8,128)}, u32[]{:S(2)}) copy-start(f32[1,3,8,32,128]{4,3,2,1,0:T(8,128)} %param.16) | copy-start | bytes 1179652
